TPU v7x, 8 devices: a whole 2x2x1 slice. The times are simulated.
8 devices in a mesh: data: 2 (over z, y), expert: 4 (over x, core).
Axes of the slice: x: 2, y: 2, z: 1, core: 2. Of those that a mesh axis runs over, the one named last changes fastest.
Arguments:
- x_in: bfloat16 [1024, 1024], P(('data', 'expert')), parts along dimension 0
- expert_idx: int32 [1024, 8], P(('data', 'expert')), parts along dimension 0
- gate_weight: float32 [1024, 8], P(('data', 'expert')), parts along dimension 0
- grad_y: bfloat16 [1024, 1024], P(('data', 'expert')), parts along dimension 0
- w_in: bfloat16 [128, 1024, 384], P('expert')
- w_out: bfloat16 [128, 384, 1024], P('expert')
Outputs:
- output 1: bfloat16 [1024, 1024], P(('data', 'expert')), parts along dimension 0
- output 2: bfloat16 [1024, 1024], P(('data', 'expert')), parts along dimension 0
- output 3: float32 [1024, 8], P(('data', 'expert')), parts along dimension 0
- output 4: bfloat16 [256, 1024, 384], P(('data', 'expert')), parts along dimension 0
- output 5: bfloat16 [256, 384, 1024], P(('data', 'expert')), parts along dimension 0
There are 2 independent parts. A program takes and returns all parts, laid end to end along the dimension named above; an argument that names none is the same for every part.
All inputs are finite; a program needn't handle non-finite values.
Results may differ from a plain program's by a relative error of at most 0.0102157.
Values are sent between devices in bfloat16 or wider.
A program may use at most 1 GiB of HBM per device.

v0:
```python
import jax
import jax.numpy as jnp
from jax import lax
from jax.sharding import PartitionSpec as P

CAP_NUM = 5
CAP_DEN = 4
PAIR_FACTOR = 2


def local_ranks(flat_idx, num_experts):
    one_hot = (flat_idx[:, None] == jnp.arange(num_experts, dtype=jnp.int32)[None, :]).astype(jnp.int32)
    running = jnp.cumsum(one_hot, axis=0)
    return jnp.sum((running - one_hot) * one_hot, axis=1), running[-1]


def exchange_maps(flat_idx, local_rank, counts_all, my_index, local_experts, capacity, pair_cap):
    groups, num_experts = counts_all.shape
    n_pairs = flat_idx.shape[0]
    through = jnp.cumsum(counts_all, axis=0)
    before = through - counts_all
    kept_all = jnp.clip(capacity - before, 0, counts_all)
    before_mine = lax.dynamic_index_in_dim(before, my_index, 0, keepdims=False)
    kept_grid = lax.dynamic_index_in_dim(kept_all, my_index, 0, keepdims=False).reshape(groups, local_experts)
    send_start = (jnp.cumsum(kept_grid, axis=1) - kept_grid).reshape(num_experts)
    pair_slot = before_mine[flat_idx] + local_rank
    target = jnp.where(pair_slot < capacity, (flat_idx // local_experts) * pair_cap + send_start[flat_idx] + local_rank, groups * pair_cap)
    send_src = jnp.full((groups * pair_cap,), n_pairs, jnp.int32).at[target].set(jnp.arange(n_pairs, dtype=jnp.int32), mode='drop')
    first_expert = my_index * local_experts
    through_own = lax.dynamic_slice_in_dim(through, first_expert, local_experts, axis=1)
    before_own = lax.dynamic_slice_in_dim(before, first_expert, local_experts, axis=1)
    kept_own = lax.dynamic_slice_in_dim(kept_all, first_expert, local_experts, axis=1)
    start_own = jnp.cumsum(kept_own, axis=1) - kept_own
    slot_ids = jnp.arange(capacity, dtype=jnp.int32)
    source_dev = jnp.sum((through_own.T[:, None, :] <= slot_ids[None, :, None]).astype(jnp.int32), axis=2)
    filled = slot_ids[None, :] < jnp.minimum(through_own[-1], capacity)[:, None]
    source_dev = jnp.minimum(source_dev, groups - 1)
    start_at = jnp.take_along_axis(start_own.T, source_dev, axis=1)
    before_at = jnp.take_along_axis(before_own.T, source_dev, axis=1)
    recv_pos = jnp.where(filled, source_dev * pair_cap + start_at + slot_ids[None, :] - before_at, groups * pair_cap).reshape(local_experts * capacity)
    back_src = jnp.full((groups * pair_cap,), local_experts * capacity, jnp.int32).at[recv_pos].set(jnp.arange(local_experts * capacity, dtype=jnp.int32), mode='drop')
    return target, send_src, recv_pos, back_src


def exchange(rows):
    return lax.all_to_all(rows, 'expert', 0, 0, tiled=True)


def gather_rows(table, positions):
    return jnp.take(table, positions, axis=0, mode='fill', fill_value=0)


def solution(mesh):
    groups = mesh.shape['expert']
    tok_spec = P(('data', 'expert'), None)
    weight_spec = P('expert', None, None)
    grad_spec = P(('data', 'expert'), None, None)

    def device_pass(x_in, expert_idx, gate_weight, grad_y, w_in, w_out):
        n_tokens, top_k = expert_idx.shape
        local_experts, d_model = w_in.shape[0], w_in.shape[1]
        num_experts = local_experts * groups
        n_pairs = n_tokens * top_k
        capacity = (CAP_NUM * n_pairs * groups) // (CAP_DEN * num_experts)
        pair_cap = PAIR_FACTOR * n_pairs // groups
        my_index = lax.axis_index('expert')
        flat_idx = expert_idx.reshape(n_pairs)
        local_rank, counts = local_ranks(flat_idx, num_experts)
        counts_all = lax.all_gather(counts, 'expert')
        target, send_src, recv_pos, back_src = exchange_maps(flat_idx, local_rank, counts_all, my_index, local_experts, capacity, pair_cap)
        exp_rows = gather_rows(exchange(gather_rows(x_in, send_src // top_k)), recv_pos).reshape(local_experts, capacity, d_model)
        pre_act = jnp.einsum('lcd,ldf->lcf', exp_rows, w_in, preferred_element_type=jnp.float32)
        act_full, gelu_pull = jax.vjp(jax.nn.gelu, pre_act)
        act_bf = act_full.astype(jnp.bfloat16)
        out_rows = jnp.einsum('lcf,lfd->lcd', act_bf, w_out, preferred_element_type=jnp.float32).astype(jnp.bfloat16)
        back_out = gather_rows(out_rows.reshape(local_experts * capacity, d_model), back_src)
        out_pair = gather_rows(exchange(back_out), target).reshape(n_tokens, top_k, d_model)
        y_out = (x_in.astype(jnp.float32) + jnp.sum(gate_weight[:, :, None] * out_pair, axis=1)).astype(jnp.bfloat16)
        grad_gate = jnp.einsum('tkd,td->tk', out_pair, grad_y, preferred_element_type=jnp.float32)
        scaled_grad = (gate_weight[:, :, None] * grad_y[:, None, :]).astype(jnp.bfloat16).reshape(n_pairs, d_model)
        grad_rows = gather_rows(exchange(gather_rows(scaled_grad, send_src)), recv_pos).reshape(local_experts, capacity, d_model)
        grad_act = jnp.einsum('lcd,lfd->lcf', grad_rows, w_out, preferred_element_type=jnp.float32).astype(jnp.bfloat16)
        grad_pre = gelu_pull(grad_act.astype(jnp.float32))[0].astype(jnp.bfloat16)
        grad_w_out = jnp.einsum('lcf,lcd->lfd', act_bf, grad_rows, preferred_element_type=jnp.float32).astype(jnp.bfloat16)
        grad_w_in = jnp.einsum('lcd,lcf->ldf', exp_rows, grad_pre, preferred_element_type=jnp.float32).astype(jnp.bfloat16)
        grad_in_rows = jnp.einsum('lcf,ldf->lcd', grad_pre, w_in, preferred_element_type=jnp.float32).astype(jnp.bfloat16)
        back_grad = gather_rows(grad_in_rows.reshape(local_experts * capacity, d_model), back_src)
        grad_pair = gather_rows(exchange(back_grad), target).reshape(n_tokens, top_k, d_model)
        grad_x = (grad_y.astype(jnp.float32) + jnp.sum(grad_pair, axis=1, dtype=jnp.float32)).astype(jnp.bfloat16)
        return y_out, grad_x, grad_gate, grad_w_in, grad_w_out

    return jax.shard_map(device_pass, mesh=mesh,
                         in_specs=(tok_spec, tok_spec, tok_spec, tok_spec, weight_spec, weight_spec),
                         out_specs=(tok_spec, tok_spec, tok_spec, grad_spec, grad_spec), check_vma=False)
```

profile of v0, /device:TPU:0, one launch (start us, length us, event | category | flops | bytes accessed | tf_op | source)
XLA Modules:
  0.0 369.0 jit_solution(16016309680223830600)
XLA Ops:
  2.3 9.8 %all-gather = s32[4,1,128]{2,1,0:T(1,128)S(1)} all-gather(s32[1,1,128]{2,1,0:T(1,128)S(1)} %slice_bitcast_fusion.1), channel_id=1, replica_groups=mesh['data'=2,'expert'=4] {'expert'}, dimensions={0}, use_global_device_ids=true | all-gather | bytes 2560 | tf_op jit(solution)/shard_map/all_gather | solution.py:69
  12.5 6.6 %gather_fusion.1 = s32[1024]{0:T(1024)S(1)} fusion(s32[128]{0:T(128)S(1)} %bitcast_subtract_fusion, s32[1024]{0:T(1024)S(1)} %broadcast_clamp_fusion.2), kind=kCustom, calls=%fused_computation.9 | custom fusion | bytes 12288 | tf_op jit(solution)/shard_map/gather | solution.py:27
  19.1 6.6 %gather_fusion = s32[1024]{0:T(1024)S(1)} fusion(s32[128]{0:T(128)S(1)} %fusion.34, s32[1024]{0:T(1024)S(1)} %broadcast_clamp_fusion.2), kind=kCustom, calls=%fused_computation.8 | custom fusion | bytes 12288 | tf_op jit(solution)/shard_map/gather | solution.py:26
  26.1 4.3 %scatter_custom_fusion = s32[2048]{0:T(1024)S(1)} fusion(s32[1024]{0:T(1024)S(1)} %bitcast.87, s32[1024]{0:T(1024)S(1)} %iota.21, s32[]{:T(128)} %constant.85.clone.1), kind=kCustom, calls=%fused_computation.109 | custom fusion | bytes 8196 | tf_op jit(solution)/shard_map/scatter | solution.py:28
  31.1 9.6 %gather_fusion.3 = bf16[2048,1024]{1,0:T(8,128)(2,1)} fusion(bf16[1024,1024]{1,0:T(8,128)(2,1)S(1)} %fusion, s32[2048]{0:T(1024)S(1)} %get-tuple-element.17), kind=kCustom, calls=%fused_computation.11 | custom fusion | bytes 8396800 | tf_op jit(solution)/shard_map/jit(_take)/gather | solution.py:50
  40.7 3.8 %broadcast_select_fusion.2 = bf16[4,512,1024]{2,1,0:T(8,128)(2,1)} fusion(bf16[4,512,1024]{2,1,0:T(8,128)(2,1)} %bitcast.74, pred[4,512]{1,0:T(4,128)(4,1)S(1)} %broadcast_in_dim.94), kind=kLoop, calls=%fused_computation.22 | loop fusion | flops 2097152 | bytes 8390656 | tf_op jit(solution)/shard_map/jit(_take)/select_n | solution.py:50
  44.5 5.0 %all-to-all-start.2 = ((bf16[4,512,1024]{2,1,0:T(8,128)(2,1)}), bf16[4,512,1024]{2,1,0:T(8,128)(2,1)}, u32[]{:S(2)}, u32[]{:S(2)}) async-start(bf16[4,512,1024]{2,1,0:T(8,128)(2,1)} %broadcast_select_fusion.2), calls=%async_computation.2 | async-start | bytes 8388608 | tf_op jit(solution)/shard_map/all_to_all | solution.py:46
  49.5 9.6 %gather_fusion.2 = bf16[2048,1024]{1,0:T(8,128)(2,1)} fusion(bf16[128,1024]{1,0:T(8,128)(2,1)S(1)} %copy-done, s32[2048]{0:T(1024)S(1)} %get-tuple-element.18), kind=kCustom, calls=%fused_computation.10 | custom fusion | bytes 8396800 | tf_op jit(solution)/shard_map/jit(_take)/gather | solution.py:50
  63.0 34.4 %all-to-all-done.2 = bf16[4,512,1024]{2,1,0:T(8,128)(2,1)} async-done(((bf16[4,512,1024]{2,1,0:T(8,128)(2,1)}), bf16[4,512,1024]{2,1,0:T(8,128)(2,1)}, u32[]{:S(2)}, u32[]{:S(2)}) %all-to-all-start.2) | async-done | bytes 4194336 | tf_op jit(solution)/shard_map/all_to_all | solution.py:46
  97.4 4.9 %all-to-all-start = ((bf16[4,512,1024]{2,1,0:T(8,128)(2,1)}), bf16[4,512,1024]{2,1,0:T(8,128)(2,1)}, u32[]{:S(2)}, u32[]{:S(2)}) async-start(bf16[4,512,1024]{2,1,0:T(8,128)(2,1)} %broadcast_select_fusion.3), calls=%async_computation | async-start | bytes 8388608 | tf_op jit(solution)/shard_map/all_to_all | solution.py:46
  102.8 10.4 %gather_fusion.5 = s32[1280]{0:T(1024)S(1)} fusion(s32[32,4]{0,1:T(4,128)S(1)} %get-tuple-element.23, s32[1280]{0:T(1024)S(1)} %reshape.430), kind=kCustom, calls=%fused_computation.4.clone | custom fusion | bytes 20480 | tf_op jit(solution)/shard_map/jit(take_along_axis)/gather | solution.py:39
  113.3 10.4 %gather_fusion.4 = s32[1280]{0:T(1024)S(1)} fusion(s32[32,4]{0,1:T(4,128)S(1)} %subtract_bitcast_fusion, s32[1280]{0:T(1024)S(1)} %reshape.430), kind=kCustom, calls=%fused_computation.clone | custom fusion | bytes 20480 | tf_op jit(solution)/shard_map/jit(take_along_axis)/gather | solution.py:38
  124.3 5.2 %scatter_custom_fusion.1 = s32[2048]{0:T(1024)S(1)} fusion(s32[1280]{0:T(1024)S(1)} %fusion.23, s32[1280]{0:T(1024)S(1)} %iota.22, s32[]{:T(128)} %constant.150.clone.1), kind=kCustom, calls=%fused_computation.107 | custom fusion | bytes 8196 | tf_op jit(solution)/shard_map/scatter | solution.py:41
  129.6 8.9 %gather_fusion.9 = bf16[1280,1024]{1,0:T(8,128)(2,1)S(1)} fusion(bf16[2048,1024]{1,0:T(8,128)(2,1)} %bitcast.28, s32[2048]{0:T(1024)S(1)} %pad_clamp_fusion), kind=kCustom, calls=%fused_computation.5.clone | custom fusion | bytes 5248000 | tf_op jit(solution)/shard_map/jit(_take)/gather | solution.py:50
  138.5 11.6 %all-to-all-done = bf16[4,512,1024]{2,1,0:T(8,128)(2,1)} async-done(((bf16[4,512,1024]{2,1,0:T(8,128)(2,1)}), bf16[4,512,1024]{2,1,0:T(8,128)(2,1)}, u32[]{:S(2)}, u32[]{:S(2)}) %all-to-all-start) | async-done | bytes 4194336 | tf_op jit(solution)/shard_map/all_to_all | solution.py:46
  150.2 9.4 %gather_fusion.6 = bf16[1280,1024]{1,0:T(8,128)(2,1)} fusion(bf16[2048,1024]{1,0:T(8,128)(2,1)} %bitcast.20, s32[2048]{0:T(1024)S(1)} %pad_clamp_fusion), kind=kCustom, calls=%fused_computation.1.clone | custom fusion | bytes 5248000 | tf_op jit(solution)/shard_map/jit(_take)/gather | solution.py:50
  164.3 10.1 %fusion.37 = f32[32,40,384]{2,1,0:T(8,128)S(1)} fusion(bf16[32,40,1024]{2,1,0:T(8,128)(2,1)S(1)} %bitcast.72, bf16[32,1024,384]{2,1,0:T(8,128)(2,1)} %param.18), kind=kOutput, calls=%fused_computation.128 | convolution fusion | flops 1006632960 | bytes 29753344 | tf_op jit(solution)/shard_map/lcd,ldf->lcf/dot_general | solution.py:72
  174.4 14.9 %convolution_convert_fusion.3 = bf16[32,40,1024]{2,1,0:T(8,128)(2,1)} fusion(bf16[32,384,1024]{2,1,0:T(8,128)(2,1)} %param.19, f32[32,40,384]{2,1,0:T(8,128)S(1)} %fusion.37), kind=kOutput, calls=%fused_computation.34 | convolution fusion | flops 1012367360 | bytes 29753344 | tf_op jit(solution)/shard_map/lcf,lfd->lcd/dot_general | solution.py:75
  189.4 13.6 %fusion.5 = bf16[32,40,384]{2,1,0:T(8,128)(2,1)} fusion(f32[32,40,384]{2,1,0:T(8,128)S(1)} %fusion.37, bf16[32,40,1024]{2,1,0:T(8,128)(2,1)} %bitcast.70, bf16[32,384,1024]{2,1,0:T(8,128)(2,1)} %param.19), kind=kOutput, calls=%fused_computation.37 | convolution fusion | flops 1017446400 | bytes 30736384 | tf_op jit(solution)/shard_map/lcd,lfd->lcf/dot_general | solution.py:82
  202.9 14.9 %convolution_convert_fusion.2 = bf16[32,40,1024]{2,1,0:T(8,128)(2,1)S(1)} fusion(bf16[32,40,384]{2,1,0:T(8,128)(2,1)} %fusion.5, bf16[32,1024,384]{2,1,0:T(8,128)(2,1)} %param.18), kind=kOutput, calls=%fused_computation.33 | convolution fusion | flops 1007943680 | bytes 28770304 | tf_op jit(solution)/shard_map/lcf,ldf->lcd/dot_general | solution.py:86
  217.9 9.6 %gather_fusion.10 = bf16[2048,1024]{1,0:T(8,128)(2,1)} fusion(bf16[1280,1024]{1,0:T(8,128)(2,1)S(1)} %bitcast.68, s32[2048]{0:T(1024)S(1)} %fusion.22), kind=kCustom, calls=%fused_computation.6.clone | custom fusion | bytes 8396800 | tf_op jit(solution)/shard_map/jit(_take)/gather | solution.py:50
  227.5 13.0 %gather_fusion.7 = bf16[2048,1024]{1,0:T(8,128)(2,1)} fusion(bf16[1280,1024]{1,0:T(8,128)(2,1)} %bitcast.69, s32[2048]{0:T(1024)S(1)} %fusion.22), kind=kCustom, calls=%fused_computation.2.clone | custom fusion | bytes 8396800 | tf_op jit(solution)/shard_map/jit(_take)/gather | solution.py:50
  240.5 5.9 %broadcast_select_fusion.1 = (bf16[2048,1024]{1,0:T(8,128)(2,1)}, bf16[2048,1024]{1,0:T(8,128)(2,1)}) fusion(bf16[2048,1024]{1,0:T(8,128)(2,1)} %gather_fusion.7, pred[2048]{0:T(1024)(128)(4,1)S(1)} %compare_and_fusion, bf16[2048,1024]{1,0:T(8,128)(2,1)} %gather_fusion.10), kind=kLoop, calls=%fused_computation.21 | loop fusion | flops 4194304 | bytes 16779264 | tf_op jit(solution)/shard_map/jit(_take)/select_n | solution.py:50
  246.4 4.9 %all-to-all-start.3 = ((bf16[4,512,1024]{2,1,0:T(8,128)(2,1)}), bf16[4,512,1024]{2,1,0:T(8,128)(2,1)}, u32[]{:S(2)}, u32[]{:S(2)}) async-start(bf16[4,512,1024]{2,1,0:T(8,128)(2,1)} %bitcast.77), calls=%async_computation.3 | async-start | bytes 8388608 | tf_op jit(solution)/shard_map/all_to_all | solution.py:46
  251.4 47.8 %all-to-all-done.3 = bf16[4,512,1024]{2,1,0:T(8,128)(2,1)} async-done(((bf16[4,512,1024]{2,1,0:T(8,128)(2,1)}), bf16[4,512,1024]{2,1,0:T(8,128)(2,1)}, u32[]{:S(2)}, u32[]{:S(2)}) %all-to-all-start.3) | async-done | bytes 4194336 | tf_op jit(solution)/shard_map/all_to_all | solution.py:46
  299.2 5.0 %all-to-all-start.1 = ((bf16[4,512,1024]{2,1,0:T(8,128)(2,1)}), bf16[4,512,1024]{2,1,0:T(8,128)(2,1)}, u32[]{:S(2)}, u32[]{:S(2)}) async-start(bf16[4,512,1024]{2,1,0:T(8,128)(2,1)} %bitcast.76), calls=%async_computation.1 | async-start | bytes 8388608 | tf_op jit(solution)/shard_map/all_to_all | solution.py:46
  304.2 13.9 %convolution_convert_fusion.1 = bf16[32,1024,384]{2,1,0:T(8,128)(2,1)} fusion(bf16[32,40,1024]{2,1,0:T(8,128)(2,1)} %bitcast.73, bf16[32,40,384]{2,1,0:T(8,128)(2,1)S(1)} %copy-done.4), kind=kOutput, calls=%fused_computation.15 | convolution fusion | flops 1019215872 | bytes 28770304 | tf_op jit(solution)/shard_map/lcd,lcf->ldf/dot_general | solution.py:85
  318.1 13.3 %convolution_convert_fusion = bf16[32,384,1024]{2,1,0:T(8,128)(2,1)} fusion(bf16[32,40,1024]{2,1,0:T(8,128)(2,1)} %bitcast.71, f32[32,40,384]{2,1,0:T(8,128)S(1)} %copy-done.2), kind=kOutput, calls=%fused_computation.14 | convolution fusion | flops 1023639552 | bytes 29753344 | tf_op jit(solution)/shard_map/lcf,lcd->lfd/dot_general | solution.py:84
  331.5 7.7 %gather_fusion.11 = bf16[1024,1024]{1,0:T(8,128)(2,1)S(1)} fusion(bf16[2048,1024]{1,0:T(8,128)(2,1)} %bitcast.32, s32[1024]{0:T(1024)S(1)} %broadcast_clamp_fusion.1), kind=kCustom, calls=%fused_computation.7.clone | custom fusion | bytes 4198400 | tf_op jit(solution)/shard_map/jit(_take)/gather | solution.py:50
  339.2 12.9 %all-to-all-done.1 = bf16[4,512,1024]{2,1,0:T(8,128)(2,1)} async-done(((bf16[4,512,1024]{2,1,0:T(8,128)(2,1)}), bf16[4,512,1024]{2,1,0:T(8,128)(2,1)}, u32[]{:S(2)}, u32[]{:S(2)}) %all-to-all-start.1) | async-done | bytes 4194336 | tf_op jit(solution)/shard_map/all_to_all | solution.py:46
  352.1 8.8 %gather_fusion.8 = bf16[1024,1024]{1,0:T(8,128)(2,1)} fusion(bf16[2048,1024]{1,0:T(8,128)(2,1)} %bitcast.24, s32[1024]{0:T(1024)S(1)} %broadcast_clamp_fusion.1), kind=kCustom, calls=%fused_computation.3.clone | custom fusion | bytes 4198400 | tf_op jit(solution)/shard_map/jit(_take)/gather | solution.py:50
  360.9 4.3 %convert_reduce_fusion = (f32[128,1024]{1,0:T(8,128)S(1)}, f32[128,1024]{1,0:T(8,128)S(1)}) fusion(bf16[1024,1024]{1,0:T(8,128)(2,1)S(1)} %gather_fusion.11, pred[1024]{0:T(1024)(128)(4,1)S(1)} %get-tuple-element.11, bf16[1024,1024]{1,0:T(8,128)(2,1)} %gather_fusion.8, f32[128,8]{1,0:T(8,128)S(1)} %copy-done.10), kind=kLoop, calls=%fused_computation.16 | loop fusion | flops 7077888 | bytes 5248000 | tf_op jit(solution)/shard_map/reduce_sum | solution.py:89
  (86 shorter events, 16.5 us)
Async XLA Ops:
  19.1 11.4 %copy-start.11 = (f32[128,8]{0,1:T(8,128)S(1)}, f32[128,8]{0,1:T(8,128)}, u32[]{:S(2)}) copy-start(f32[128,8]{0,1:T(8,128)} %param.16) | copy-start | bytes 12292
  19.1 11.6 %copy-start.6 = (bf16[128,1024]{1,0:T(8,128)(2,1)S(1)}, bf16[128,1024]{1,0:T(8,128)(2,1)}, u32[]{:S(2)}) copy-start(bf16[128,1024]{1,0:T(8,128)(2,1)} %param.17) | copy-start | bytes 786436
  30.6 10.1 %copy-start.9 = (f32[128,8]{1,0:T(8,128)}, f32[128,8]{1,0:T(8,128)S(1)}, u32[]{:S(2)}) copy-start(f32[128,8]{1,0:T(8,128)S(1)} %copy.31) | copy-start | bytes 12292
  44.5 5.0 %copy-start = (bf16[128,1024]{1,0:T(8,128)(2,1)S(1)}, bf16[128,1024]{1,0:T(8,128)(2,1)}, u32[]{:S(2)}) copy-start(bf16[128,1024]{1,0:T(8,128)(2,1)} %param.14) | copy-start | bytes 786436
  44.5 52.9 %all-to-all-start.2 = ((bf16[4,512,1024]{2,1,0:T(8,128)(2,1)}), bf16[4,512,1024]{2,1,0:T(8,128)(2,1)}, u32[]{:S(2)}, u32[]{:S(2)}) async-start(bf16[4,512,1024]{2,1,0:T(8,128)(2,1)} %broadcast_select_fusion.2), calls=%async_computation.2 | async-start | bytes 8388608 | tf_op jit(solution)/shard_map/all_to_all | solution.py:46
  97.4 52.8 %all-to-all-start = ((bf16[4,512,1024]{2,1,0:T(8,128)(2,1)}), bf16[4,512,1024]{2,1,0:T(8,128)(2,1)}, u32[]{:S(2)}, u32[]{:S(2)}) async-start(bf16[4,512,1024]{2,1,0:T(8,128)(2,1)} %broadcast_select_fusion.3), calls=%async_computation | async-start | bytes 8388608 | tf_op jit(solution)/shard_map/all_to_all | solution.py:46
  162.8 1.5 copy-start.3
  174.4 14.9 %copy-start.1 = (f32[32,40,384]{2,1,0:T(8,128)}, f32[32,40,384]{2,1,0:T(8,128)S(1)}, u32[]{:S(2)}) copy-start(f32[32,40,384]{2,1,0:T(8,128)S(1)} %fusion.37) | copy-start | bytes 5898244
  246.4 52.8 %all-to-all-start.3 = ((bf16[4,512,1024]{2,1,0:T(8,128)(2,1)}), bf16[4,512,1024]{2,1,0:T(8,128)(2,1)}, u32[]{:S(2)}, u32[]{:S(2)}) async-start(bf16[4,512,1024]{2,1,0:T(8,128)(2,1)} %bitcast.77), calls=%async_computation.3 | async-start | bytes 8388608 | tf_op jit(solution)/shard_map/all_to_all | solution.py:46
  299.2 5.0 %copy-start.4 = (bf16[32,40,384]{2,1,0:T(8,128)(2,1)S(1)}, bf16[32,40,384]{2,1,0:T(8,128)(2,1)}, u32[]{:S(2)}) copy-start(bf16[32,40,384]{2,1,0:T(8,128)(2,1)} %fusion.5) | copy-start | bytes 2949124
  299.2 52.9 %all-to-all-start.1 = ((bf16[4,512,1024]{2,1,0:T(8,128)(2,1)}), bf16[4,512,1024]{2,1,0:T(8,128)(2,1)}, u32[]{:S(2)}, u32[]{:S(2)}) async-start(bf16[4,512,1024]{2,1,0:T(8,128)(2,1)} %bitcast.76), calls=%async_computation.1 | async-start | bytes 8388608 | tf_op jit(solution)/shard_map/all_to_all | solution.py:46
  304.2 13.9 %copy-start.2 = (f32[32,40,384]{2,1,0:T(8,128)S(1)}, f32[32,40,384]{2,1,0:T(8,128)}, u32[]{:S(2)}) copy-start(f32[32,40,384]{2,1,0:T(8,128)} %copy-done.1) | copy-start | bytes 5898244
  352.1 8.8 %copy-start.10 = (f32[128,8]{1,0:T(8,128)S(1)}, f32[128,8]{1,0:T(8,128)}, u32[]{:S(2)}) copy-start(f32[128,8]{1,0:T(8,128)} %copy-done.9) | copy-start | bytes 12292
  360.9 4.3 %copy-start.5 = (bf16[1024,1024]{1,0:T(8,128)(2,1)S(1)}, bf16[1024,1024]{1,0:T(8,128)(2,1)}, u32[]{:S(2)}) copy-start(bf16[1024,1024]{1,0:T(8,128)(2,1)} %gather_fusion.8) | copy-start | bytes 6291460
  360.9 4.3 %copy-start.7 = (bf16[128,1024]{1,0:T(8,128)(2,1)S(1)}, bf16[128,1024]{1,0:T(8,128)(2,1)}, u32[]{:S(2)}) copy-start(bf16[128,1024]{1,0:T(8,128)(2,1)} %param.17) | copy-start | bytes 786436
  365.2 2.3 copy-start.8
where the time goes:
time: 370 us; the launch traced here: 369 us
  local copies, waits for them, and re-layouts  125 us (34%)
  waiting for transfers between devices  107 us (29%)
  matrix products  82.3 us (22%)
  other arithmetic  24.4 us (7%)
  starting transfers between devices  19.8 us (5%)
  blocking collectives  9.81 us (3%)
    all_to_all x4, waiting for transfers between devices, exchange(): return lax.all_to_all(rows, 'expert', 0, 0, tiled=True)  107 us
    gather x8, local copies, waits for them, and re-layouts, gather_rows(): return jnp.take(table, positions, axis=0, mode='fill', fill_value=0)  76.7 us
    all_to_all x4, starting transfers between devices, exchange(): return lax.all_to_all(rows, 'expert', 0, 0, tiled=True)  19.8 us
    select_n x5, other arithmetic, gather_rows(): return jnp.take(table, positions, axis=0, mode='fill', fill_value=0)  16.8 us
    dot_general x1, matrix products, device_pass(): jnp.einsum('lcf,lfd->lcd', act_bf, w_out, preferred_element_type=jnp.floa...  14.9 us
    dot_general x1, matrix products, device_pass(): jnp.einsum('lcf,ldf->lcd', grad_pre, w_in, preferred_element_type=jnp.flo...  14.9 us
    dot_general x1, matrix products, device_pass(): jnp.einsum('lcd,lcf->ldf', exp_rows, grad_pre, preferred_element_type=jnp...  13.9 us
    dot_general x1, matrix products, device_pass(): jnp.einsum('lcd,lfd->lcf', grad_rows, w_out, preferred_element_type=jnp.f...  13.6 us
  transfers between devices with their start and end apart: 4, of which 4 were waited for; matrix products, arithmetic and copies ran while one was open for 23% of the time, Pallas kernels for 0%

commit v1 on v0

v1 whole, which is shorter than its diff:
```python
import functools

import jax
import jax.numpy as jnp
from jax import lax
from jax.experimental import pallas as pl
from jax.experimental.pallas import tpu as pltpu
from jax.sharding import PartitionSpec as P

MESH = pl.DeviceIdType.MESH
CAP = 40
SLOTS = 48
PAIR = 2
C0 = 0.7978845608028654
C1 = 0.044715


def dot(a, b, dims=((1,), (0,))):
    return lax.dot_general(a, b, (dims, ((), ())), preferred_element_type=jnp.float32)


def gather_kernel(x_ref, dy_ref, idx_ref, gate_ref, xa, dya, ida, ga, small_s, small_r, sib_s, sib_r,
                  cross_s, cross_r, fwd_s, fwd_r):
    me = lax.axis_index("expert")
    sib, cross = me + 1 - 2 * lax.rem(me, 2), lax.rem(me + 2, 4)
    diag = lax.rem(sib + 2, 4)
    barrier = pltpu.get_barrier_semaphore()
    for peer in (sib, cross, diag):
        pl.semaphore_signal(barrier, inc=1, device_id={"expert": peer}, device_id_type=MESH)
    pl.semaphore_wait(barrier, 3)

    def send(src, dst, s, r, peer):
        copy = pltpu.make_async_remote_copy(src_ref=src, dst_ref=dst, send_sem=s, recv_sem=r,
                                            device_id={"expert": peer}, device_id_type=MESH)
        copy.start()
        return copy

    copies = []
    for k, peer in enumerate((cross, diag, sib)):
        copies.append(send(idx_ref, ida.at[me], small_s.at[2 * k], small_r.at[2 * k], peer))
        copies.append(send(gate_ref, ga.at[me], small_s.at[2 * k + 1], small_r.at[2 * k + 1], peer))
    over = []
    for a, (src, dst) in enumerate(((x_ref, xa), (dy_ref, dya))):
        for c in range(2):
            rows = pl.ds(64 * c, 64)
            over.append((dst, rows, send(src.at[rows], dst.at[me, rows], cross_s.at[2 * a + c], cross_r.at[2 * a + c], cross)))
        copies.append(send(src, dst.at[me], sib_s.at[a], sib_r.at[a], sib))
    xa[me] = x_ref[...]
    dya[me] = dy_ref[...]
    ida[me] = idx_ref[...]
    ga[me] = gate_ref[...]
    for n, (dst, rows, copy) in enumerate(over):
        copy.wait_recv()
        copies.append(send(dst.at[cross, rows], dst.at[cross, rows], fwd_s.at[n], fwd_r.at[n], sib))
    for _, _, copy in over:
        copy.wait_send()
    for copy in copies:
        copy.wait()


def gather_group(x, dy, idx_t, gate_t):
    rows, width = x.shape
    vmem = pl.BlockSpec(memory_space=pltpu.VMEM)
    dma = pltpu.SemaphoreType.DMA
    return pl.pallas_call(
        gather_kernel,
        out_shape=[jax.ShapeDtypeStruct((4, rows, width), jnp.bfloat16)] * 2
        + [jax.ShapeDtypeStruct((4, 8, rows), jnp.int32), jax.ShapeDtypeStruct((4, 8, rows), jnp.float32)],
        in_specs=[vmem] * 4,
        out_specs=[vmem] * 4,
        scratch_shapes=[dma((6,)), dma((6,)), dma((2,)), dma((2,)), dma((4,)), dma((4,)), dma((4,)), dma((4,))],
        compiler_params=pltpu.CompilerParams(collective_id=0, has_side_effects=True),
    )(x, dy, idx_t, gate_t)


def route(idx, gate, first, rj, r0s, r1s, pm, pt, gs):
    eid = lax.broadcasted_iota(jnp.int32, (32, 128), 0) + first
    earlier = (lax.broadcasted_iota(jnp.int32, (128, 128), 0) < lax.broadcasted_iota(jnp.int32, (128, 128), 1)).astype(jnp.bfloat16)
    offset = jnp.zeros((32, 1), jnp.float32)
    for d in range(4):
        ids = idx[d]
        hits = [(ids[j:j + 1, :] == eid).astype(jnp.float32) for j in range(8)]
        count = sum(hits[1:], hits[0])
        rank = dot(count.astype(jnp.bfloat16), earlier) + offset
        r0s[d] = rank
        for j in range(8):
            rj[j, d] = jnp.where((hits[j] > 0.0) & (rank < CAP), rank, -1.0)
            rank = rank + hits[j]
        r1s[d] = jnp.minimum(rank, CAP)
        offset = offset + jnp.sum(count, axis=1, keepdims=True)

    rows = lax.broadcasted_iota(jnp.int32, (SLOTS, 128), 0).astype(jnp.float32)

    def one(e, _):
        at = pl.ds(pl.multiple_of(e * SLOTS, SLOTS), SLOTS)
        total = jnp.zeros((SLOTS, 128), jnp.float32)
        for d in range(4):
            lanes = slice(128 * d, 128 * (d + 1))
            inside = (rows >= r0s[d, pl.ds(e, 1), :]) & (rows < r1s[d, pl.ds(e, 1), :])
            pm[at, lanes] = jnp.where(inside, 1.0, 0.0).astype(jnp.bfloat16)
            for j in range(8):
                total = jnp.where(rows == rj[j, d, pl.ds(e, 1), :], total + gate[d, j:j + 1, :], total)
        gs[at, :] = jnp.sum(total, axis=1, keepdims=True)
        return 0

    lax.fori_loop(0, 32, one, 0)

    def turn(c, _):
        at = pl.ds(pl.multiple_of(c * 128, 128), 128)
        pt[:, at] = pm[at, :].astype(jnp.float32).T.astype(jnp.bfloat16)
        return 0

    lax.fori_loop(0, 32 * SLOTS // 128, turn, 0)


def expert_kernel(idx, gate, xa, dya, w_in, w_out, yp, dxp, dgp, b_out, h_out, g_out, da_out,
                  rj, r0s, r1s, pm, pt, gs, gx, sp, o_s, slope, dg_tab):
    step = pl.program_id(0)
    half = pl.num_programs(0) // 2
    slots = 32 * SLOTS

    @pl.when(step == 0)
    def _():
        route(idx, gate, lax.axis_index("expert") * 32, rj, r0s, r1s, pm, pt, gs)

        def pick(c, _):
            at = pl.ds(pl.multiple_of(c * 256, 256), 256)
            gx[at, :] = dot(pm[at, :], xa[...]).astype(jnp.bfloat16)
            return 0

        lax.fori_loop(0, slots // 256, pick, 0)

    @pl.when(step < half)
    def _():
        for p in range(PAIR):
            at = pl.ds(pl.multiple_of((step * PAIR + p) * SLOTS, SLOTS), SLOTS)
            here = pl.ds(p * SLOTS, SLOTS)
            rows = gx[at, :]
            b_out[here, :] = rows
            a = dot(rows, w_in[p])
            th = jnp.tanh(C0 * (a + C1 * (a * a * a)))
            cdf = 0.5 * (1.0 + th)
            slope[at, :] = cdf + 0.5 * a * (1.0 - th * th) * (C0 * (1.0 + 3.0 * C1 * (a * a)))
            h = (a * cdf).astype(jnp.bfloat16)
            h_out[here, :] = h
            o = dot(h, w_out[p]).astype(jnp.bfloat16)
            o_s[at, :] = o
            s = o.astype(jnp.float32) * gs[at, :]
            s1 = s.astype(jnp.bfloat16)
            s = s - s1.astype(jnp.float32)
            s2 = s.astype(jnp.bfloat16)
            s = s - s2.astype(jnp.float32)
            sp[0, at, :] = s1
            sp[1, at, :] = s2
            sp[2, at, :] = s.astype(jnp.bfloat16)

    @pl.when(step == half)
    def _():
        def combine(n, _):
            lanes = pl.ds(pl.multiple_of(n * 256, 256), 256)
            out = dot(pt[...], sp[0, :, lanes]) + dot(pt[...], sp[1, :, lanes]) + dot(pt[...], sp[2, :, lanes])
            for d in range(4):
                yp[d, :, lanes] = out[128 * d:128 * (d + 1)]
            return 0

        lax.fori_loop(0, 4, combine, 0)

        def pick(c, _):
            at = pl.ds(pl.multiple_of(c * 256, 256), 256)
            gx[at, :] = dot(pm[at, :], dya[...]).astype(jnp.bfloat16)
            return 0

        lax.fori_loop(0, slots // 256, pick, 0)

    @pl.when(step >= half)
    def _():
        for p in range(PAIR):
            e = (2 * half - 1 - step) * PAIR + p
            at = pl.ds(pl.multiple_of(e * SLOTS, SLOTS), SLOTS)
            here = pl.ds(p * SLOTS, SLOTS)
            rows = gx[at, :].astype(jnp.float32)
            g = (rows * gs[at, :]).astype(jnp.bfloat16)
            g_out[here, :] = g
            prod = rows * o_s[at, :].astype(jnp.float32)
            part = sum((prod[:, 128 * c:128 * (c + 1)] for c in range(1, 8)), prod[:, :128])
            dg_tab[pl.ds(e, 1), :SLOTS] = jnp.sum(part.T, axis=0, keepdims=True)
            dh = dot(w_out[p], g, ((1,), (1,))).T
            da = (dh.astype(jnp.bfloat16).astype(jnp.float32) * slope[at, :]).astype(jnp.bfloat16)
            da_out[here, :] = da
            sp[0, at, :] = dot(w_in[p], da, ((1,), (1,))).T.astype(jnp.bfloat16)

    @pl.when(step == 2 * half - 1)
    def _():
        def combine(n, _):
            lanes = pl.ds(pl.multiple_of(n * 256, 256), 256)
            out = dot(pt[...], sp[0, :, lanes])
            for d in range(4):
                dxp[d, :, lanes] = out[128 * d:128 * (d + 1)]
            return 0

        lax.fori_loop(0, 4, combine, 0)
        for d in range(4):
            for j in range(8):
                at = rj[j, d].astype(jnp.int32)
                got = jnp.take_along_axis(dg_tab[...], jnp.maximum(at, 0), axis=1)
                dgp[d, j:j + 1, :] = jnp.sum(jnp.where(at >= 0, got, 0.0), axis=0, keepdims=True)


def experts(idx, gate, xa, dya, w_in, w_out):
    n_e, d_model, d_ff = w_in.shape
    half = n_e // PAIR
    slots = n_e * SLOTS
    both = 2 * half - 1

    def whole(a):
        return pl.BlockSpec(a.shape, lambda i: (0,) * a.ndim)

    def weights(i):
        return (jnp.where(i < half, i, both - i), 0, 0)

    def first(i):
        return (jnp.minimum(i, half - 1), 0)

    def second(i):
        return (jnp.minimum(both - i, half - 1), 0)

    bf, f32 = jnp.bfloat16, jnp.float32
    outs = [jax.ShapeDtypeStruct((4, 128, d_model), f32), jax.ShapeDtypeStruct((4, 128, d_model), f32),
            jax.ShapeDtypeStruct((4, 8, 128), f32),
            jax.ShapeDtypeStruct((slots, d_model), bf), jax.ShapeDtypeStruct((slots, d_ff), bf),
            jax.ShapeDtypeStruct((slots, d_model), bf), jax.ShapeDtypeStruct((slots, d_ff), bf)]
    return pl.pallas_call(
        expert_kernel,
        grid=(2 * half,),
        out_shape=outs,
        in_specs=[whole(idx), whole(gate), whole(xa), whole(dya),
                  pl.BlockSpec((PAIR, d_model, d_ff), weights), pl.BlockSpec((PAIR, d_ff, d_model), weights)],
        out_specs=[whole(outs[0]), whole(outs[1]), whole(outs[2]),
                   pl.BlockSpec((PAIR * SLOTS, d_model), first), pl.BlockSpec((PAIR * SLOTS, d_ff), first),
                   pl.BlockSpec((PAIR * SLOTS, d_model), second), pl.BlockSpec((PAIR * SLOTS, d_ff), second)],
        scratch_shapes=[pltpu.VMEM((8, 4, n_e, 128), f32), pltpu.VMEM((4, n_e, 128), f32), pltpu.VMEM((4, n_e, 128), f32),
                        pltpu.VMEM((slots, 512), bf), pltpu.VMEM((512, slots), bf), pltpu.VMEM((slots, 1), f32),
                        pltpu.VMEM((slots, d_model), bf), pltpu.VMEM((3, slots, d_model), bf),
                        pltpu.VMEM((slots, d_model), bf), pltpu.VMEM((slots, d_ff), f32), pltpu.VMEM((n_e, 128), f32)],
        compiler_params=pltpu.CompilerParams(vmem_limit_bytes=62 * 1024 * 1024),
        cost_estimate=pl.CostEstimate(flops=8 * slots * d_model * d_ff, bytes_accessed=4 * n_e * d_model * d_ff, transcendentals=0),
    )(idx, gate, xa, dya, w_in, w_out)


def weight_kernel(b, h, g, da, dw_in, dw_out):
    for p in range(PAIR):
        at = slice(p * SLOTS, (p + 1) * SLOTS)
        dw_in[p] = dot(b[at, :], da[at, :], ((0,), (0,))).astype(jnp.bfloat16)
        dw_out[p] = dot(h[at, :], g[at, :], ((0,), (0,))).astype(jnp.bfloat16)


def weight_grads(b, h, g, da, n_e):
    d_model, d_ff = b.shape[1], h.shape[1]
    rows = PAIR * SLOTS
    return pl.pallas_call(
        weight_kernel,
        grid=(n_e // PAIR,),
        out_shape=[jax.ShapeDtypeStruct((n_e, d_model, d_ff), jnp.bfloat16), jax.ShapeDtypeStruct((n_e, d_ff, d_model), jnp.bfloat16)],
        in_specs=[pl.BlockSpec((rows, d_model), lambda i: (i, 0)), pl.BlockSpec((rows, d_ff), lambda i: (i, 0)),
                  pl.BlockSpec((rows, d_model), lambda i: (i, 0)), pl.BlockSpec((rows, d_ff), lambda i: (i, 0))],
        out_specs=[pl.BlockSpec((PAIR, d_model, d_ff), lambda i: (i, 0, 0)), pl.BlockSpec((PAIR, d_ff, d_model), lambda i: (i, 0, 0))],
        compiler_params=pltpu.CompilerParams(vmem_limit_bytes=48 * 1024 * 1024),
        cost_estimate=pl.CostEstimate(flops=4 * n_e * SLOTS * d_model * d_ff, bytes_accessed=4 * n_e * d_model * d_ff, transcendentals=0),
    )(b, h, g, da)


def solution(mesh):
    tok_spec = P(('data', 'expert'), None)
    weight_spec = P('expert', None, None)
    grad_spec = P(('data', 'expert'), None, None)
    to_sib = [(i, i ^ 1) for i in range(4)]
    to_cross = [(i, i ^ 2) for i in range(4)]

    def device_pass(x_in, expert_idx, gate_weight, grad_y, w_in, w_out):
        n_tokens, d_model = x_in.shape
        me = lax.axis_index('expert')
        core, chip = lax.rem(me, 2), me // 2
        xa, dya, ida, ga = gather_group(x_in, grad_y, expert_idx.T, gate_weight.T)
        yp, dxp, dgp, b, h, g, da = experts(ida, ga, xa.reshape(512, d_model), dya.reshape(512, d_model), w_in, w_out)

        def reduce_back(part):
            part = part.reshape((2, 2) + part.shape[1:])
            mine = lax.dynamic_index_in_dim(part, core, 1, keepdims=False)
            theirs = lax.dynamic_index_in_dim(part, 1 - core, 1, keepdims=False)
            mine = mine + lax.ppermute(theirs, 'expert', to_sib)
            far = lax.ppermute(lax.dynamic_index_in_dim(mine, 1 - chip, 0, keepdims=False), 'expert', to_cross)
            return lax.dynamic_index_in_dim(mine, chip, 0, keepdims=False) + far

        y_sum, dx_sum, dg_sum = reduce_back(yp), reduce_back(dxp), reduce_back(dgp)
        grad_w_in, grad_w_out = weight_grads(b, h, g, da, w_in.shape[0])
        y_out = (x_in.astype(jnp.float32) + y_sum).astype(jnp.bfloat16)
        grad_x = (grad_y.astype(jnp.float32) + dx_sum).astype(jnp.bfloat16)
        return y_out, grad_x, dg_sum.T, grad_w_in, grad_w_out

    return jax.shard_map(device_pass, mesh=mesh,
                         in_specs=(tok_spec, tok_spec, tok_spec, tok_spec, weight_spec, weight_spec),
                         out_specs=(tok_spec, tok_spec, tok_spec, grad_spec, grad_spec), check_vma=False)
```

time: 370 us -> 138 us (0.37)
  local copies, waits for them, and re-layouts: 125 us -> 4.33 us
  Pallas kernels: 0 us -> 120 us
  waiting for transfers between devices: 107 us -> 2.17 us
  matrix products: 82.3 us -> 0 us
  other arithmetic: 24.4 us -> 6.31 us
  starting transfers between devices: 19.8 us -> 4.32 us
  blocking collectives: 9.81 us -> 0 us
    pallas_call x0 -> x3, Pallas kernels: none -> 120 us  [the longest x1 78.3 us: experts(): pl.pallas_call(expert_kernel, grid=(2 * half,), out_shape=outs, in_specs=...]
    gather x15 -> x0, local copies, waits for them, and re-layouts: 111 us -> none  [the longest x8 76.7 us: gather_rows(): return jnp.take(table, positions, axis=0, mode='fill', fill_value=0)]
    all_to_all x4 -> x0, waiting for transfers between devices: 107 us -> none  [exchange(): return lax.all_to_all(rows, 'expert', 0, 0, tiled=True)]
    dot_general x7 -> x0, matrix products: 82.3 us -> none  [the longest x1 14.9 us: device_pass(): jnp.einsum('lcf,lfd->lcd', act_bf, w_out, preferred_element_type=jnp.floa...]
    all_to_all x4 -> x0, starting transfers between devices: 19.8 us -> none  [exchange(): return lax.all_to_all(rows, 'expert', 0, 0, tiled=True)]
    select_n x9 -> x0, other arithmetic: 17 us -> none  [the longest x5 16.8 us: gather_rows(): return jnp.take(table, positions, axis=0, mode='fill', fill_value=0)]
    all_gather x1 -> x0, blocking collectives: 9.81 us -> none  [device_pass(): counts_all = lax.all_gather(counts, 'expert')]
    scatter x2 -> x0, local copies, waits for them, and re-layouts: 9.57 us -> none  [the longest x1 5.25 us: exchange_maps(): jnp.full((groups * pair_cap,), local_experts * capacity, jnp.int32)]
  transfers between devices with their start and end apart: 4 -> 6, of which waited for: 4 -> 1; matrix products, arithmetic and copies ran while one was open for 23% -> 5% of each run, Pallas kernels for 0% -> 16%
where the time goes in v1:
time: 138 us
  Pallas kernels  120 us (87%)
  other arithmetic  6.31 us (5%)
  local copies, waits for them, and re-layouts  4.33 us (3%)
  starting transfers between devices  4.32 us (3%)
  waiting for transfers between devices  2.17 us (2%)
    pallas_call x1, Pallas kernels, experts(): pl.pallas_call(expert_kernel, grid=(2 * half,), out_shape=outs, in_specs=...  78.3 us
    pallas_call x1, Pallas kernels, weight_grads(): pl.pallas_call(weight_kernel, grid=(n_e // PAIR,), out_shape=[jax.ShapeDt...  21.7 us
    pallas_call x1, Pallas kernels, gather_group(): pl.pallas_call(gather_kernel, out_shape=[jax.ShapeDtypeStruct((4, rows, w...  20 us
    ppermute x3, starting transfers between devices, reduce_back(): lax.ppermute(lax.dynamic_index_in_dim(mine, 1 - chip, 0, keepdims=False),...  3.42 us
    add x3, other arithmetic, reduce_back(): mine = mine + lax.ppermute(theirs, 'expert', to_sib)  3.08 us
  transfers between devices with their start and end apart: 6, of which 1 were waited for; matrix products, arithmetic and copies ran while one was open for 5% of the time, Pallas kernels for 16%

profile of v1, /device:TPU:0, one launch (start us, length us, event | category | flops | bytes accessed | tf_op | source)
XLA Modules:
  0.0 137.8 jit_solution(10363658325086233312)
XLA Ops:
  0.6 20.0 %shard_map.101 = (bf16[4,128,1024]{2,1,0:T(8,128)(2,1)}, bf16[4,128,1024]{2,1,0:T(8,128)(2,1)}, s32[4,8,128]{2,1,0:T(8,128)}, f32[4,8,128]{2,1,0:T(8,128)}) custom-call(bf16[128,1024]{1,0:T(8,128)(2,1)} %x_ref.1, bf16[128,1024]{1,0:T(8,128)(2,1)} %dy_ref.1, s32[8,128]{1,0:T(8,128)} %bitcast.51, f32[8,128]{1,0:T(8,128)} %bitcast.52), custom_call_target="tpu_custom_call" | custom-call | tf_op jit(solution)/shard_map/pallas_call | solution.py:65
  20.7 78.3 %shard_map.102 = (f32[4,128,1024]{2,1,0:T(8,128)}, f32[4,128,1024]{2,1,0:T(8,128)}, f32[4,8,128]{2,1,0:T(8,128)}, bf16[1536,1024]{1,0:T(8,128)(2,1)}, bf16[1536,...) custom-call(s32[4,8,128]{2,1,0:T(8,128)} %get-tuple-element.18.idx, ...), custom_call_target="tpu_custom_call" | custom-call | flops 4831838208 | bytes 50331648 | tf_op jit(solution)/shard_map/pallas_call | solution.py:232
  98.9 0.0 copy-start.8
  99.0 0.0 copy-start.5
  99.0 1.5 %dynamic-slice_bitcast_fusion.1 = f32[2,128,1024]{2,1,0:T(8,128)S(1)} fusion(f32[2,2,128,1024]{3,2,1,0:T(8,128)} %bitcast.45, s32[]{:T(128)S(6)} %select_n.30), kind=kLoop, calls=%fused_computation.3 | loop fusion | bytes 2097156 | tf_op jit(solution)/shard_map/jit(dynamic_index_in_dim)/squeeze | solution.py:289
  100.4 0.4 collective-permute-start
  100.8 0.0 copy-done.3
  100.9 1.1 dynamic-slice_bitcast_fusion
  102.0 0.4 collective-permute-start.2
  102.4 0.0 copy-done.8
  102.4 0.1 collective-permute-start.4
  102.5 2.2 %collective-permute-done.4 = f32[2,8,128]{2,1,0:T(8,128)S(1)} collective-permute-done((f32[2,8,128]{2,1,0:T(8,128)S(1)}, f32[2,8,128]{2,1,0:T(8,128)S(1)}, u32[]{:S(2)}, u32[]{:S(2)}) %collective-permute-start.4) | collective-permute-done | bytes 8224 | tf_op jit(solution)/shard_map/ppermute | solution.py:290
  104.7 1.6 %collective-permute-start.5 = (f32[8,128]{1,0:T(8,128)S(1)}, f32[8,128]{1,0:T(8,128)S(1)}, u32[]{:S(2)}, u32[]{:S(2)}) collective-permute-start(f32[8,128]{1,0:T(8,128)S(1)} %dynamic-slice_bitcast_fusion.5), channel_id=1, source_target_pairs={{0,2},{1,3},{2,0},{3,1},{4,6},{5,7},{6,4},{7,5}} | collective-permute-start | bytes 12296 | tf_op jit(solution)/shard_map/ppermute | solution.py:291
  106.3 0.0 collective-permute-done
  106.3 0.0 copy-done.5
  106.3 1.5 %bitcast_add_fusion.1 = f32[2,128,1024]{2,1,0:T(8,128)S(1)} fusion(f32[2,128,1024]{2,1,0:T(8,128)} %collective-permute-done, f32[2,2,128,1024]{3,2,1,0:T(8,128)S(1)} %bitcast.46, s32[]{:T(128)S(6)} %select_n.29), kind=kLoop, calls=%fused_computation.1 | loop fusion | flops 262144 | bytes 3145732 | tf_op jit(solution)/shard_map/add | solution.py:290
  107.8 0.0 copy-start.1
  107.8 0.8 dynamic-slice_bitcast_fusion.3
  108.6 0.5 collective-permute-start.1
  109.1 0.0 collective-permute-done.2
  109.1 1.6 %bitcast_add_fusion = f32[2,128,1024]{2,1,0:T(8,128)S(1)} fusion(f32[2,128,1024]{2,1,0:T(8,128)} %collective-permute-done.2, f32[2,2,128,1024]{3,2,1,0:T(8,128)S(1)} %bitcast.44, s32[]{:T(128)S(6)} %select_n.29), kind=kLoop, calls=%fused_computation | loop fusion | flops 262144 | bytes 3145732 | tf_op jit(solution)/shard_map/add | solution.py:290
  110.8 0.8 dynamic-slice_bitcast_fusion.2
  111.6 1.3 collective-permute-start.3
  112.9 0.0 copy-done.1
  112.9 0.0 copy-start.7
  112.9 21.7 %shard_map.103 = (bf16[32,1024,384]{2,1,0:T(8,128)(2,1)}, bf16[32,384,1024]{2,1,0:T(8,128)(2,1)}) custom-call(bf16[1536,1024]{1,0:T(8,128)(2,1)S(1)} %copy-done, bf16[1536,384]{1,0:T(8,128)(2,1)S(1)} %copy-done.1, bf16[1536,1024]{1,0:T(8,128)(2,1)} %get-tuple-element.27.g, bf16[1536,384]{1,0:T(8,128)(2,1)S(1)} %copy-done.2), custom_call_target="tpu_custom_call" | custom-call | flops 2415919104 | bytes 50331648 | tf_op jit(solution)/shard_map/pallas_call | solution.py:260
  134.6 0.0 collective-permute-done.5
  134.6 0.6 fusion.4
  135.2 0.0 collective-permute-done.1
  135.2 0.8 fusion.3
  136.0 0.0 collective-permute-done.3
  136.0 1.8 %fusion.1 = bf16[128,1024]{1,0:T(8,128)(2,1)} fusion(f32[128,1024]{1,0:T(8,128)} %collective-permute-done.3, f32[2,128,1024]{2,1,0:T(8,128)S(1)} %bitcast_add_fusion, s32[]{:T(128)S(6)} %select_n.32, bf16[128,1024]{1,0:T(8,128)(2,1)S(1)} %copy-done.7), kind=kLoop, calls=%fused_computation.6 | loop fusion | flops 524288 | bytes 1572868 | tf_op jit(solution)/shard_map/convert_element_type | solution.py:297
  (13 shorter events, 0.0 us)
Async XLA Ops:
  98.9 1.9 %copy-start.3 = (f32[4,128,1024]{2,1,0:T(8,128)S(1)}, f32[4,128,1024]{2,1,0:T(8,128)}, u32[]{:S(2)}) copy-start(f32[4,128,1024]{2,1,0:T(8,128)} %get-tuple-element.23) | copy-start | bytes 6291460
  98.9 3.4 %copy-start.8 = (f32[4,8,128]{2,1,0:T(8,128)S(1)}, f32[4,8,128]{2,1,0:T(8,128)}, u32[]{:S(2)}) copy-start(f32[4,8,128]{2,1,0:T(8,128)} %get-tuple-element.24) | copy-start | bytes 49156
  99.0 7.4 %copy-start.5 = (f32[4,128,1024]{2,1,0:T(8,128)S(1)}, f32[4,128,1024]{2,1,0:T(8,128)}, u32[]{:S(2)}) copy-start(f32[4,128,1024]{2,1,0:T(8,128)} %get-tuple-element.22) | copy-start | bytes 6291460
  100.4 5.9 %collective-permute-start = (f32[2,128,1024]{2,1,0:T(8,128)S(1)}, f32[2,128,1024]{2,1,0:T(8,128)}, u32[]{:S(2)}, u32[]{:S(2)}) collective-permute-start(f32[2,128,1024]{2,1,0:T(8,128)S(1)} %dynamic-slice_bitcast_fusion.1), channel_id=1, source_target_pairs={{0,1},{1,0},{2,3},{3,2},{4,5},{5,4},{6,7},{7,6}} | collective-permute-start | bytes 3145736 | tf_op jit(solution)/shard_map/ppermute | solution.py:290
  102.0 7.1 %collective-permute-start.2 = (f32[2,128,1024]{2,1,0:T(8,128)}, f32[2,128,1024]{2,1,0:T(8,128)}, u32[]{:S(2)}, u32[]{:S(2)}) collective-permute-start(f32[2,128,1024]{2,1,0:T(8,128)} %dynamic-slice_bitcast_fusion), channel_id=1, source_target_pairs={{0,1},{1,0},{2,3},{3,2},{4,5},{5,4},{6,7},{7,6}} | collective-permute-start | bytes 3145736 | tf_op jit(solution)/shard_map/ppermute | solution.py:290
  102.4 2.3 %collective-permute-start.4 = (f32[2,8,128]{2,1,0:T(8,128)S(1)}, f32[2,8,128]{2,1,0:T(8,128)S(1)}, u32[]{:S(2)}, u32[]{:S(2)}) collective-permute-start(f32[2,8,128]{2,1,0:T(8,128)S(1)} %dynamic-slice_bitcast_fusion.4), channel_id=1, source_target_pairs={{0,1},{1,0},{2,3},{3,2},{4,5},{5,4},{6,7},{7,6}} | collective-permute-start | bytes 24584 | tf_op jit(solution)/shard_map/ppermute | solution.py:290
  104.7 4.5 %copy-start.4 = (f32[4,128,1024]{2,1,0:T(8,128)S(1)}, f32[4,128,1024]{2,1,0:T(8,128)}, u32[]{:S(2)}) copy-start(f32[4,128,1024]{2,1,0:T(8,128)} %get-tuple-element.23) | copy-start | bytes 6291460
  104.7 29.9 %collective-permute-start.5 = (f32[8,128]{1,0:T(8,128)S(1)}, f32[8,128]{1,0:T(8,128)S(1)}, u32[]{:S(2)}, u32[]{:S(2)}) collective-permute-start(f32[8,128]{1,0:T(8,128)S(1)} %dynamic-slice_bitcast_fusion.5), channel_id=1, source_target_pairs={{0,2},{1,3},{2,0},{3,1},{4,6},{5,7},{6,4},{7,5}} | collective-permute-start | bytes 12296 | tf_op jit(solution)/shard_map/ppermute | solution.py:291
  106.3 6.5 %copy-start.2 = (bf16[1536,384]{1,0:T(8,128)(2,1)S(1)}, bf16[1536,384]{1,0:T(8,128)(2,1)}, u32[]{:S(2)}) copy-start(bf16[1536,384]{1,0:T(8,128)(2,1)} %get-tuple-element.28.da) | copy-start | bytes 3538948
  107.8 5.1 %copy-start.1 = (bf16[1536,384]{1,0:T(8,128)(2,1)S(1)}, bf16[1536,384]{1,0:T(8,128)(2,1)}, u32[]{:S(2)}) copy-start(bf16[1536,384]{1,0:T(8,128)(2,1)} %get-tuple-element.26.h) | copy-start | bytes 3538948
  108.6 4.2 %copy-start = (bf16[1536,1024]{1,0:T(8,128)(2,1)S(1)}, bf16[1536,1024]{1,0:T(8,128)(2,1)}, u32[]{:S(2)}) copy-start(bf16[1536,1024]{1,0:T(8,128)(2,1)} %get-tuple-element.25.b) | copy-start | bytes 9437188
  108.6 26.5 %collective-permute-start.1 = (f32[128,1024]{1,0:T(8,128)}, f32[128,1024]{1,0:T(8,128)S(1)}, u32[]{:S(2)}, u32[]{:S(2)}) collective-permute-start(f32[128,1024]{1,0:T(8,128)} %dynamic-slice_bitcast_fusion.3), channel_id=1, source_target_pairs={{0,2},{1,3},{2,0},{3,1},{4,6},{5,7},{6,4},{7,5}} | collective-permute-start | bytes 1572872 | tf_op jit(solution)/shard_map/ppermute | solution.py:291
  111.6 24.4 %collective-permute-start.3 = (f32[128,1024]{1,0:T(8,128)}, f32[128,1024]{1,0:T(8,128)}, u32[]{:S(2)}, u32[]{:S(2)}) collective-permute-start(f32[128,1024]{1,0:T(8,128)} %dynamic-slice_bitcast_fusion.2), channel_id=1, source_target_pairs={{0,2},{1,3},{2,0},{3,1},{4,6},{5,7},{6,4},{7,5}} | collective-permute-start | bytes 1572872 | tf_op jit(solution)/shard_map/ppermute | solution.py:291
  112.9 22.3 %copy-start.6 = (bf16[128,1024]{1,0:T(8,128)(2,1)S(1)}, bf16[128,1024]{1,0:T(8,128)(2,1)}, u32[]{:S(2)}) copy-start(bf16[128,1024]{1,0:T(8,128)(2,1)} %x_ref.1) | copy-start | bytes 786436
  112.9 23.1 %copy-start.7 = (bf16[128,1024]{1,0:T(8,128)(2,1)S(1)}, bf16[128,1024]{1,0:T(8,128)(2,1)}, u32[]{:S(2)}) copy-start(bf16[128,1024]{1,0:T(8,128)(2,1)} %dy_ref.1) | copy-start | bytes 786436

commit v2 on v0

v2 whole, which is shorter than its diff:
```python
import functools

import jax
import jax.numpy as jnp
from jax import lax
from jax.experimental import pallas as pl
from jax.experimental.pallas import tpu as pltpu
from jax.sharding import PartitionSpec as P

MESH = pl.DeviceIdType.MESH
CAP = 40
SLOTS = 48
PAIR = 2
AHEAD = 4
PICK = 384
C0 = 0.7978845608028654
C1 = 0.044715


def dot(a, b, dims=((1,), (0,))):
    return lax.dot_general(a, b, (dims, ((), ())), preferred_element_type=jnp.float32)


def tables(ids_all, first, rj, r0s, r1s):
    eid = lax.broadcasted_iota(jnp.int32, (32, 128), 0) + first
    earlier = (lax.broadcasted_iota(jnp.int32, (128, 128), 0) < lax.broadcasted_iota(jnp.int32, (128, 128), 1)).astype(jnp.bfloat16)
    offset = jnp.zeros((32, 1), jnp.float32)
    for d in range(4):
        ids = ids_all[d]
        hits = [(ids[j:j + 1, :] == eid).astype(jnp.float32) for j in range(8)]
        count = sum(hits[1:], hits[0])
        rank = dot(count.astype(jnp.bfloat16), earlier) + offset
        r0s[d] = rank
        for j in range(8):
            rj[j, d] = jnp.where((hits[j] > 0.0) & (rank < CAP), rank, -1.0)
            rank = rank + hits[j]
        r1s[d] = jnp.minimum(rank, CAP)
        offset = offset + jnp.sum(count, axis=1, keepdims=True)


def slot_rows(e):
    return pl.ds(pl.multiple_of(e * SLOTS, SLOTS), SLOTS)


def expert_kernel(x, dy, idx, gate, w_in, w_out, y_out, dg_out, dx_own, dx_far, b_out, h_out, g_out, da_out,
                  xa, dya, ida, ga, rj, r0s, r1s, pm, pt, gs, b_s, g_s, h_s, da_s, o_s, slope, sp, zs, dg_tab, dgp, dgr,
                  wi, wo, yp, yr, yfar, ygot, dxp, dxr,
                  wi_sem, wo_sem, out_sem, small_s, small_r, sib_s, sib_r, cross_s, cross_r, fwd_s, fwd_r,
                  yd_s, yd_r, yx_s, yx_r, dd_s, dd_r, dg_s, dg_r):
    me = lax.axis_index("expert")
    sib, cross = me + 1 - 2 * lax.rem(me, 2), lax.rem(me + 2, 4)
    diag = lax.rem(sib + 2, 4)
    n_pairs = w_in.shape[0] // PAIR
    slots = 32 * SLOTS
    bf, f32 = jnp.bfloat16, jnp.float32

    def fetch_in(q, slot):
        return pltpu.make_async_copy(w_in.at[pl.ds(PAIR * q, PAIR)], wi.at[slot], wi_sem.at[slot])

    def fetch_out(q, slot):
        return pltpu.make_async_copy(w_out.at[pl.ds(PAIR * q, PAIR)], wo.at[slot], wo_sem.at[slot])

    def remote(src, dst, s, r, peer):
        return pltpu.make_async_remote_copy(src_ref=src, dst_ref=dst, send_sem=s, recv_sem=r,
                                            device_id={"expert": peer}, device_id_type=MESH)

    for q in range(AHEAD):
        fetch_in(q, q).start()
        fetch_out(q, q).start()

    barrier = pltpu.get_barrier_semaphore()
    for peer in (sib, cross, diag):
        pl.semaphore_signal(barrier, inc=1, device_id={"expert": peer}, device_id_type=MESH)
    pl.semaphore_wait(barrier, 3)

    small, over, near, far = [], [], [], []
    for k, peer in enumerate((cross, diag, sib)):
        small.append(remote(idx, ida.at[me], small_s.at[2 * k], small_r.at[2 * k], peer))
        small.append(remote(gate, ga.at[me], small_s.at[2 * k + 1], small_r.at[2 * k + 1], peer))
    for a, (src, dst) in enumerate(((x, xa), (dy, dya))):
        for c in range(2):
            rows = pl.ds(64 * c, 64)
            n = 2 * a + c
            over.append(remote(src.at[rows], dst.at[me, rows], cross_s.at[n], cross_r.at[n], cross))
            far.append(remote(dst.at[cross, rows], dst.at[cross, rows], fwd_s.at[n], fwd_r.at[n], sib))
        near.append(remote(src, dst.at[me], sib_s.at[a], sib_r.at[a], sib))
    for copy in small + over[:2] + near[:1] + over[2:] + near[1:]:
        copy.start()
    xa[me] = x[...]
    dya[me] = dy[...]
    ida[me] = idx[...]
    ga[me] = gate[...]
    zs[...] = jnp.zeros_like(zs)

    def forward(n):
        over[n].wait_recv()
        far[n].start()

    for copy in small:
        copy.wait_recv()
    tables(ida, me * 32, rj, r0s, r1s)
    slot_id = lax.broadcasted_iota(jnp.int32, (SLOTS, 128), 0).astype(f32)

    def one(e, _):
        total = jnp.zeros((SLOTS, 128), f32)
        for d in range(4):
            lanes = slice(128 * d, 128 * (d + 1))
            inside = (slot_id >= r0s[d, pl.ds(e, 1), :]) & (slot_id < r1s[d, pl.ds(e, 1), :])
            pm[slot_rows(e), lanes] = jnp.where(inside, 1.0, 0.0).astype(bf)
            for j in range(8):
                total = jnp.where(slot_id == rj[j, d, pl.ds(e, 1), :], ga[d, j:j + 1, :], total)
        gs[slot_rows(e), :] = jnp.sum(total, axis=1, keepdims=True)
        return 0

    lax.fori_loop(0, 32, one, 0)
    forward(0)

    def turn(c, _):
        at = pl.ds(pl.multiple_of(c * 128, 128), 128)
        pt[:, at] = pm[at, :].astype(f32).T.astype(bf)
        return 0

    lax.fori_loop(0, slots // 128, turn, 0)
    forward(1)
    near[0].wait_recv()
    far[0].wait_recv()
    far[1].wait_recv()

    def pick_x(c, _):
        at = pl.ds(pl.multiple_of(c * PICK, PICK), PICK)
        b_s[at, :] = dot(pm[at, :], xa[...].reshape(512, xa.shape[2])).astype(bf)
        return 0

    lax.fori_loop(0, slots // PICK, pick_x, 0)
    pltpu.make_async_copy(b_s, b_out, out_sem.at[0]).start()

    def fwd_step(i, _):
        slot = lax.rem(i, AHEAD)
        fetch_in(i, slot).wait()
        fetch_out(i, slot).wait()
        for p in range(PAIR):
            at = slot_rows(i * PAIR + p)
            a = dot(b_s[at, :], wi[slot, p])
            th = jnp.tanh(C0 * (a + C1 * (a * a * a)))
            cdf = 0.5 * (1.0 + th)
            slope[at, :] = cdf + 0.5 * a * (1.0 - th * th) * (C0 * (1.0 + 3.0 * C1 * (a * a)))
            h = (a * cdf).astype(bf)
            h_s[at, :] = h
            o = dot(h, wo[slot, p]).astype(bf)
            o_s[at, :] = o
            s = o.astype(f32) * gs[at, :]
            s1 = s.astype(bf)
            s = s - s1.astype(f32)
            s2 = s.astype(bf)
            s = s - s2.astype(f32)
            sp[0, at, :] = s1
            sp[1, at, :] = s2
            sp[2, at, :] = s.astype(bf)

        @pl.when(i < n_pairs - AHEAD)
        def _():
            fetch_in(i + AHEAD, slot).start()
            fetch_out(i + AHEAD, slot).start()

        @pl.when(i >= n_pairs - AHEAD)
        def _():
            fetch_in(2 * n_pairs - 1 - AHEAD - i, slot).start()
            fetch_out(2 * n_pairs - 1 - AHEAD - i, slot).start()

        for n, when in ((2, 1), (3, 4)):
            @pl.when(i == when)
            def _(n=n):
                forward(n)
        return 0

    lax.fori_loop(0, n_pairs, fwd_step, 0)
    pltpu.make_async_copy(h_s, h_out, out_sem.at[1]).start()

    def to_sib(part, got, s, r, n, k):
        return remote(part.at[n, sib if k == 0 else diag], got.at[n, k], s.at[n, k], r.at[n, k], sib)

    def y_part(n, _):
        lanes = pl.ds(pl.multiple_of(n * 256, 256), 256)
        out = dot(pt[...], sp[0, :, lanes]) + dot(pt[...], sp[1, :, lanes]) + dot(pt[...], sp[2, :, lanes])
        for d in range(4):
            yp[n, d] = out[128 * d:128 * (d + 1)]

        @pl.when(n > 0)
        def _():
            for k in range(2):
                to_sib(yp, yr, yd_s, yd_r, n - 1, k).start()
        return 0

    lax.fori_loop(0, 4, y_part, 0)
    near[1].wait_recv()
    far[2].wait_recv()
    far[3].wait_recv()
    for k in range(2):
        to_sib(yp, yr, yd_s, yd_r, 3, k).start()

    def pick_dy(c, _):
        at = pl.ds(pl.multiple_of(c * PICK, PICK), PICK)
        rows = dot(pm[at, :], dya[...].reshape(512, dya.shape[2]))
        g_s[at, :] = (rows * gs[at, :]).astype(bf)
        prod = rows * o_s[at, :].astype(f32)
        part = sum((prod[:, 128 * k:128 * (k + 1)] for k in range(1, 8)), prod[:, :128])
        for k in range(PICK // SLOTS):
            dg_tab[pl.ds(c * (PICK // SLOTS) + k, 1), :SLOTS] = jnp.sum(part[SLOTS * k:SLOTS * (k + 1)].T, axis=0, keepdims=True)
        return 0

    lax.fori_loop(0, slots // PICK, pick_dy, 0)
    pltpu.make_async_copy(g_s, g_out, out_sem.at[2]).start()
    for n in range(4):
        for k in range(2):
            to_sib(yp, yr, yd_s, yd_r, n, k).wait()
        yfar[n] = yp[n, cross] + yr[n, 1]
    for d in range(4):
        for j in range(8):
            at = rj[j, d].astype(jnp.int32)
            got = jnp.take_along_axis(dg_tab[...], jnp.maximum(at, 0), axis=1)
            dgp[d, j:j + 1, :] = jnp.sum(jnp.where(at >= 0, got, 0.0), axis=0, keepdims=True)
    y_cross = remote(yfar, ygot, yx_s, yx_r, cross)
    y_cross.start()
    dg_back = [remote(dgp.at[peer], dgr.at[k], dg_s.at[k], dg_r.at[k], peer) for k, peer in enumerate((cross, diag, sib))]

    def zero(n, like):
        return jnp.zeros((n, like.shape[1]), bf)

    def back_h(q, i):
        slot = lax.rem(i, AHEAD)
        fetch_out(q, slot).wait()
        g0, g1 = g_s[slot_rows(q * PAIR), :], g_s[slot_rows(q * PAIR + 1), :]
        both = dot(wo[slot, 0], jnp.concatenate([g0, zero(80, g0)], axis=0), ((1,), (1,)))
        both = both + dot(wo[slot, 1], jnp.concatenate([zero(64, g1), g1, zero(16, g1)], axis=0), ((1,), (1,)))
        dh = both.astype(bf).T.astype(f32)
        for p in range(PAIR):
            at = slot_rows(q * PAIR + p)
            da = (dh[64 * p:64 * p + SLOTS] * slope[at, :]).astype(bf)
            da_s[at, :] = da
            zs[lax.rem(i, 2), 64 * p:64 * p + SLOTS, 384 * p:384 * (p + 1)] = da

    def back_x(q, i):
        slot = lax.rem(i, AHEAD)
        fetch_in(q, slot).wait()
        wide = jnp.concatenate([wi[slot, 0], wi[slot, 1]], axis=1)
        both = dot(wide, zs[lax.rem(i, 2)], ((1,), (1,))).astype(bf).T
        for p in range(PAIR):
            sp[0, slot_rows(q * PAIR + p), :] = both[64 * p:64 * p + SLOTS]

    last = n_pairs - 1
    back_h(last, 0)
    fetch_out(last - AHEAD, 0).start()
    for copy in dg_back:
        copy.start()

    def bwd_step(i, _):
        back_x(last + 1 - i, i - 1)
        back_h(last - i, i)

        @pl.when(i < n_pairs - AHEAD)
        def _():
            fetch_out(last - AHEAD - i, lax.rem(i, AHEAD)).start()

        @pl.when(i < n_pairs - AHEAD + 1)
        def _():
            fetch_in(last + 1 - AHEAD - i, lax.rem(i - 1, AHEAD)).start()
        return 0

    lax.fori_loop(1, n_pairs, bwd_step, 0)
    pltpu.make_async_copy(da_s, da_out, out_sem.at[3]).start()
    back_x(0, last)

    def dx_part(n, _):
        lanes = pl.ds(pl.multiple_of(n * 256, 256), 256)
        out = dot(pt[...], sp[0, :, lanes])
        for d in range(4):
            dxp[n, d] = out[128 * d:128 * (d + 1)]

        @pl.when(n > 0)
        def _():
            for k in range(2):
                to_sib(dxp, dxr, dd_s, dd_r, n - 1, k).start()
        return 0

    lax.fori_loop(0, 4, dx_part, 0)
    y_cross.wait()
    for k in range(2):
        to_sib(dxp, dxr, dd_s, dd_r, 3, k).start()
    for n in range(4):
        lanes = slice(256 * n, 256 * (n + 1))
        y_out[:, lanes] = (x[:, lanes].astype(f32) + (yp[n, me] + yr[n, 0] + ygot[n])).astype(bf)
    for copy in dg_back:
        copy.wait()
    dg_out[...] = dgp[me] + (dgr[0] + (dgr[1] + dgr[2]))
    for n in range(4):
        lanes = slice(256 * n, 256 * (n + 1))
        for k in range(2):
            to_sib(dxp, dxr, dd_s, dd_r, n, k).wait()
        dx_own[:, lanes] = dxp[n, me] + dxr[n, 0]
        dx_far[:, lanes] = dxp[n, cross] + dxr[n, 1]
    for copy in small + over + near + far:
        copy.wait_send()
    for k, (src, dst) in enumerate(((b_s, b_out), (h_s, h_out), (g_s, g_out), (da_s, da_out))):
        pltpu.make_async_copy(src, dst, out_sem.at[k]).wait()


def experts(x, dy, idx_t, gate_t, w_in, w_out):
    n_e, d_model, d_ff = w_in.shape
    slots = n_e * SLOTS
    bf, f32 = jnp.bfloat16, jnp.float32
    vmem, hbm = pl.BlockSpec(memory_space=pltpu.VMEM), pl.BlockSpec(memory_space=pl.ANY)
    shape, buf, dma = jax.ShapeDtypeStruct, pltpu.VMEM, pltpu.SemaphoreType.DMA
    return pl.pallas_call(
        expert_kernel,
        out_shape=[shape((128, d_model), bf), shape((8, 128), f32), shape((128, d_model), f32), shape((128, d_model), f32),
                   shape((slots, d_model), bf), shape((slots, d_ff), bf), shape((slots, d_model), bf), shape((slots, d_ff), bf)],
        in_specs=[vmem] * 4 + [hbm] * 2,
        out_specs=[vmem] * 4 + [hbm] * 4,
        scratch_shapes=[
            buf((4, 128, d_model), bf), buf((4, 128, d_model), bf), buf((4, 8, 128), jnp.int32), buf((4, 8, 128), f32),
            buf((8, 4, n_e, 128), f32), buf((4, n_e, 128), f32), buf((4, n_e, 128), f32),
            buf((slots, 512), bf), buf((512, slots), bf), buf((slots, 1), f32),
            buf((slots, d_model), bf), buf((slots, d_model), bf), buf((slots, d_ff), bf), buf((slots, d_ff), bf),
            buf((slots, d_model), bf), buf((slots, d_ff), f32), buf((3, slots, d_model), bf), buf((2, 128, PAIR * d_ff), bf),
            buf((n_e, 128), f32), buf((4, 8, 128), f32), buf((3, 8, 128), f32),
            buf((AHEAD, PAIR, d_model, d_ff), bf), buf((AHEAD, PAIR, d_ff, d_model), bf),
            buf((4, 4, 128, 256), f32), buf((4, 2, 128, 256), f32), buf((4, 128, 256), f32), buf((4, 128, 256), f32),
            buf((4, 4, 128, 256), f32), buf((4, 2, 128, 256), f32),
            dma((AHEAD,)), dma((AHEAD,)), dma((4,)), dma((6,)), dma((6,)), dma((2,)), dma((2,)), dma((4,)), dma((4,)),
            dma((4,)), dma((4,)), dma((4, 2)), dma((4, 2)), dma(()), dma(()), dma((4, 2)), dma((4, 2)), dma((3,)), dma((3,))],
        compiler_params=pltpu.CompilerParams(collective_id=0, has_side_effects=True, vmem_limit_bytes=63 * 1024 * 1024),
        cost_estimate=pl.CostEstimate(flops=8 * slots * d_model * d_ff, bytes_accessed=8 * n_e * d_model * d_ff, transcendentals=0),
    )(x, dy, idx_t, gate_t, w_in, w_out)


def weight_kernel(b, h, g, da, dw_in, dw_out):
    for p in range(PAIR):
        at = slice(p * SLOTS, (p + 1) * SLOTS)
        dw_in[p] = dot(b[at, :], da[at, :], ((0,), (0,))).astype(jnp.bfloat16)
        dw_out[p] = dot(h[at, :], g[at, :], ((0,), (0,))).astype(jnp.bfloat16)


def weight_grads(b, h, g, da, n_e):
    d_model, d_ff = b.shape[1], h.shape[1]
    rows = PAIR * SLOTS
    return pl.pallas_call(
        weight_kernel,
        grid=(n_e // PAIR,),
        out_shape=[jax.ShapeDtypeStruct((n_e, d_model, d_ff), jnp.bfloat16), jax.ShapeDtypeStruct((n_e, d_ff, d_model), jnp.bfloat16)],
        in_specs=[pl.BlockSpec((rows, d_model), lambda i: (i, 0)), pl.BlockSpec((rows, d_ff), lambda i: (i, 0)),
                  pl.BlockSpec((rows, d_model), lambda i: (i, 0)), pl.BlockSpec((rows, d_ff), lambda i: (i, 0))],
        out_specs=[pl.BlockSpec((PAIR, d_model, d_ff), lambda i: (i, 0, 0)), pl.BlockSpec((PAIR, d_ff, d_model), lambda i: (i, 0, 0))],
        compiler_params=pltpu.CompilerParams(vmem_limit_bytes=48 * 1024 * 1024),
        cost_estimate=pl.CostEstimate(flops=4 * n_e * SLOTS * d_model * d_ff, bytes_accessed=4 * n_e * d_model * d_ff, transcendentals=0),
    )(b, h, g, da)


def solution(mesh):
    tok_spec = P(('data', 'expert'), None)
    weight_spec = P('expert', None, None)
    grad_spec = P(('data', 'expert'), None, None)
    to_cross = [(i, i ^ 2) for i in range(4)]

    def device_pass(x_in, expert_idx, gate_weight, grad_y, w_in, w_out):
        y_out, dg, dx_own, dx_far, b, h, g, da = experts(x_in, grad_y, expert_idx.T, gate_weight.T, w_in, w_out)
        dx_got = lax.ppermute(dx_far, 'expert', to_cross)
        grad_w_in, grad_w_out = weight_grads(b, h, g, da, w_in.shape[0])
        grad_x = (grad_y.astype(jnp.float32) + (dx_own + dx_got)).astype(jnp.bfloat16)
        return y_out, grad_x, dg.T, grad_w_in, grad_w_out

    return jax.shard_map(device_pass, mesh=mesh,
                         in_specs=(tok_spec, tok_spec, tok_spec, tok_spec, weight_spec, weight_spec),
                         out_specs=(tok_spec, tok_spec, tok_spec, grad_spec, grad_spec), check_vma=False)
```

time: 370 us -> 110 us (0.30)
  local copies, waits for them, and re-layouts: 125 us -> 7.37 us
  waiting for transfers between devices: 107 us -> 0.01 us
  Pallas kernels: 0 us -> 97.5 us
  matrix products: 82.3 us -> 0 us
  other arithmetic: 24.4 us -> 1.84 us
  starting transfers between devices: 19.8 us -> 2.04 us
  blocking collectives: 9.81 us -> 0 us
    gather x15 -> x0, local copies, waits for them, and re-layouts: 111 us -> none  [the longest x8 76.7 us: gather_rows(): return jnp.take(table, positions, axis=0, mode='fill', fill_value=0)]
    all_to_all x4 -> x0, waiting for transfers between devices: 107 us -> none  [exchange(): return lax.all_to_all(rows, 'expert', 0, 0, tiled=True)]
    pallas_call x0 -> x2, Pallas kernels: none -> 97.5 us  [the longest x1 75.9 us: experts(): pl.pallas_call(expert_kernel, out_shape=[shape((128, d_model), bf), shape...]
    dot_general x7 -> x0, matrix products: 82.3 us -> none  [the longest x1 14.9 us: device_pass(): jnp.einsum('lcf,lfd->lcd', act_bf, w_out, preferred_element_type=jnp.floa...]
    all_to_all x4 -> x0, starting transfers between devices: 19.8 us -> none  [exchange(): return lax.all_to_all(rows, 'expert', 0, 0, tiled=True)]
    select_n x9 -> x0, other arithmetic: 17 us -> none  [the longest x5 16.8 us: gather_rows(): return jnp.take(table, positions, axis=0, mode='fill', fill_value=0)]
    all_gather x1 -> x0, blocking collectives: 9.81 us -> none  [device_pass(): counts_all = lax.all_gather(counts, 'expert')]
    scatter x2 -> x0, local copies, waits for them, and re-layouts: 9.57 us -> none  [the longest x1 5.25 us: exchange_maps(): jnp.full((groups * pair_cap,), local_experts * capacity, jnp.int32)]
  transfers between devices with their start and end apart: 4 -> 1, of which waited for: 4 -> 0; matrix products, arithmetic and copies ran while one was open for 23% -> 0% of each run, Pallas kernels for 0% -> 20%
where the time goes in v2:
time: 110 us; the launch traced here: 109 us
  Pallas kernels  97.5 us (89%)
  local copies, waits for them, and re-layouts  7.37 us (7%)
  starting transfers between devices  2.04 us (2%)
  other arithmetic  1.84 us (2%)
    pallas_call x1, Pallas kernels, experts(): pl.pallas_call(expert_kernel, out_shape=[shape((128, d_model), bf), shape...  75.9 us
    pallas_call x1, Pallas kernels, weight_grads(): pl.pallas_call(weight_kernel, grid=(n_e // PAIR,), out_shape=[jax.ShapeDt...  21.6 us
    unnamed x10, local copies, waits for them, and re-layouts  7.37 us
  transfers between devices with their start and end apart: 1, of which 0 were waited for; matrix products, arithmetic and copies ran while one was open for 0% of the time, Pallas kernels for 20%

profile of v2, /device:TPU:0, one launch (start us, length us, event | category | flops | bytes accessed | tf_op | source)
XLA Modules:
  0.0 109.4 jit_solution(8501236385435622322)
XLA Ops:
  0.6 0.0 copy-start.3
  0.6 75.9 %shard_map.101 = (bf16[128,1024]{1,0:T(8,128)(2,1)}, f32[8,128]{1,0:T(8,128)}, f32[128,1024]{1,0:T(8,128)}, f32[128,1024]{1,0:T(8,128)}, bf16[1536,1024]{1,0:T(8...) custom-call(bf16[128,1024]{1,0:T(8,128)(2,1)} %x.1, ...), custom_call_target="tpu_custom_call" | custom-call | flops 4831838208 | bytes 100663296 | tf_op jit(solution)/shard_map/pallas_call | solution.py:313
  76.5 2.0 %collective-permute-start = (f32[128,1024]{1,0:T(8,128)}, f32[128,1024]{1,0:T(8,128)S(1)}, u32[]{:S(2)}, u32[]{:S(2)}) collective-permute-start(f32[128,1024]{1,0:T(8,128)} %get-tuple-element.17), channel_id=1, source_target_pairs={{0,2},{1,3},{2,0},{3,1},{4,6},{5,7},{6,4},{7,5}} | collective-permute-start | bytes 1572872 | tf_op jit(solution)/shard_map/ppermute | solution.py:366
  78.5 0.0 copy-start
  78.5 1.9 %copy-done = bf16[1536,1024]{1,0:T(8,128)(2,1)S(1)} copy-done((bf16[1536,1024]{1,0:T(8,128)(2,1)S(1)}, bf16[1536,1024]{1,0:T(8,128)(2,1)}, u32[]{:S(2)}) %copy-start) | copy-done | bytes 3145752
  80.4 0.0 copy-start.1
  80.4 1.3 %copy-done.1 = bf16[1536,384]{1,0:T(8,128)(2,1)S(1)} copy-done((bf16[1536,384]{1,0:T(8,128)(2,1)S(1)}, bf16[1536,384]{1,0:T(8,128)(2,1)}, u32[]{:S(2)}) %copy-start.1) | copy-done | bytes 1179672
  81.7 0.0 copy-start.2
  81.7 1.3 %copy-done.2 = bf16[1536,384]{1,0:T(8,128)(2,1)S(1)} copy-done((bf16[1536,384]{1,0:T(8,128)(2,1)S(1)}, bf16[1536,384]{1,0:T(8,128)(2,1)}, u32[]{:S(2)}) %copy-start.2) | copy-done | bytes 1179672
  83.0 21.6 %shard_map.102 = (bf16[32,1024,384]{2,1,0:T(8,128)(2,1)}, bf16[32,384,1024]{2,1,0:T(8,128)(2,1)}) custom-call(bf16[1536,1024]{1,0:T(8,128)(2,1)S(1)} %copy-done, bf16[1536,384]{1,0:T(8,128)(2,1)S(1)} %copy-done.1, bf16[1536,1024]{1,0:T(8,128)(2,1)} %get-tuple-element.21.g, bf16[1536,384]{1,0:T(8,128)(2,1)S(1)} %copy-done.2), custom_call_target="tpu_custom_call" | custom-call | flops 2415919104 | bytes 50331648 | tf_op jit(solution)/shard_map/pallas_call | solution.py:346
  104.6 0.0 collective-permute-done
  104.6 0.0 copy-done.3
  104.6 1.8 %add_convert_fusion = bf16[128,1024]{1,0:T(8,128)(2,1)} fusion(f32[128,1024]{1,0:T(8,128)} %get-tuple-element.16, f32[128,1024]{1,0:T(8,128)S(1)} %collective-permute-done, bf16[128,1024]{1,0:T(8,128)(2,1)S(1)} %copy-done.3), kind=kLoop, calls=%fused_computation | loop fusion | flops 524288 | bytes 1572864 | tf_op jit(solution)/shard_map/convert_element_type | solution.py:368
  106.4 1.7 %copy.13 = bf16[128,1024]{1,0:T(8,128)(2,1)} copy(bf16[128,1024]{1,0:T(8,128)(2,1)} %get-tuple-element.30) | data formatting | bytes 524288
  108.1 1.3 %copy.14 = f32[128,8]{0,1:T(8,128)} copy(f32[128,8]{0,1:T(8,128)} %bitcast.3) | data formatting | bytes 8192
Async XLA Ops:
  0.6 104.0 %copy-start.3 = (bf16[128,1024]{1,0:T(8,128)(2,1)S(1)}, bf16[128,1024]{1,0:T(8,128)(2,1)}, u32[]{:S(2)}) copy-start(bf16[128,1024]{1,0:T(8,128)(2,1)} %dy.1) | copy-start | bytes 786436
  76.5 28.1 %collective-permute-start = (f32[128,1024]{1,0:T(8,128)}, f32[128,1024]{1,0:T(8,128)S(1)}, u32[]{:S(2)}, u32[]{:S(2)}) collective-permute-start(f32[128,1024]{1,0:T(8,128)} %get-tuple-element.17), channel_id=1, source_target_pairs={{0,2},{1,3},{2,0},{3,1},{4,6},{5,7},{6,4},{7,5}} | collective-permute-start | bytes 1572872 | tf_op jit(solution)/shard_map/ppermute | solution.py:366
  78.5 1.9 %copy-start = (bf16[1536,1024]{1,0:T(8,128)(2,1)S(1)}, bf16[1536,1024]{1,0:T(8,128)(2,1)}, u32[]{:S(2)}) copy-start(bf16[1536,1024]{1,0:T(8,128)(2,1)} %get-tuple-element.19.b) | copy-start | bytes 9437188
  80.4 1.3 %copy-start.1 = (bf16[1536,384]{1,0:T(8,128)(2,1)S(1)}, bf16[1536,384]{1,0:T(8,128)(2,1)}, u32[]{:S(2)}) copy-start(bf16[1536,384]{1,0:T(8,128)(2,1)} %get-tuple-element.20.h) | copy-start | bytes 3538948
  81.7 1.3 %copy-start.2 = (bf16[1536,384]{1,0:T(8,128)(2,1)S(1)}, bf16[1536,384]{1,0:T(8,128)(2,1)}, u32[]{:S(2)}) copy-start(bf16[1536,384]{1,0:T(8,128)(2,1)} %get-tuple-element.22.da) | copy-start | bytes 3538948

commit v3 on v2

--- a/solution.py
+++ b/solution.py
@@ -228,7 +228,6 @@
 
     def back_h(q, i):
         slot = lax.rem(i, AHEAD)
-        fetch_out(q, slot).wait()
         g0, g1 = g_s[slot_rows(q * PAIR), :], g_s[slot_rows(q * PAIR + 1), :]
         both = dot(wo[slot, 0], jnp.concatenate([g0, zero(80, g0)], axis=0), ((1,), (1,)))
         both = both + dot(wo[slot, 1], jnp.concatenate([zero(64, g1), g1, zero(16, g1)], axis=0), ((1,), (1,)))
@@ -241,19 +240,21 @@
 
     def back_x(q, i):
         slot = lax.rem(i, AHEAD)
-        fetch_in(q, slot).wait()
         wide = jnp.concatenate([wi[slot, 0], wi[slot, 1]], axis=1)
         both = dot(wide, zs[lax.rem(i, 2)], ((1,), (1,))).astype(bf).T
         for p in range(PAIR):
             sp[0, slot_rows(q * PAIR + p), :] = both[64 * p:64 * p + SLOTS]
 
     last = n_pairs - 1
+    fetch_out(last, 0).wait()
     back_h(last, 0)
     fetch_out(last - AHEAD, 0).start()
     for copy in dg_back:
         copy.start()
 
     def bwd_step(i, _):
+        fetch_in(last + 1 - i, lax.rem(i - 1, AHEAD)).wait()
+        fetch_out(last - i, lax.rem(i, AHEAD)).wait()
         back_x(last + 1 - i, i - 1)
         back_h(last - i, i)
 
@@ -268,6 +269,7 @@
 
     lax.fori_loop(1, n_pairs, bwd_step, 0)
     pltpu.make_async_copy(da_s, da_out, out_sem.at[3]).start()
+    fetch_in(0, lax.rem(last, AHEAD)).wait()
     back_x(0, last)
 
     def dx_part(n, _):
@@ -333,26 +335,33 @@
     )(x, dy, idx_t, gate_t, w_in, w_out)
 
 
-def weight_kernel(b, h, g, da, dw_in, dw_out):
+def weight_kernel(b, h, g, da, y, dg, dw_in, dw_out, y_out, dg_out):
     for p in range(PAIR):
         at = slice(p * SLOTS, (p + 1) * SLOTS)
         dw_in[p] = dot(b[at, :], da[at, :], ((0,), (0,))).astype(jnp.bfloat16)
         dw_out[p] = dot(h[at, :], g[at, :], ((0,), (0,))).astype(jnp.bfloat16)
 
-
-def weight_grads(b, h, g, da, n_e):
+    @pl.when(pl.program_id(0) == 0)
+    def _():
+        y_out[...] = y[...]
+        dg_out[...] = dg[...]
+
+
+def weight_grads(b, h, g, da, y, dg, n_e):
     d_model, d_ff = b.shape[1], h.shape[1]
     rows = PAIR * SLOTS
+    whole = [pl.BlockSpec(y.shape, lambda i: (0, 0)), pl.BlockSpec(dg.shape, lambda i: (0, 0))]
     return pl.pallas_call(
         weight_kernel,
         grid=(n_e // PAIR,),
-        out_shape=[jax.ShapeDtypeStruct((n_e, d_model, d_ff), jnp.bfloat16), jax.ShapeDtypeStruct((n_e, d_ff, d_model), jnp.bfloat16)],
+        out_shape=[jax.ShapeDtypeStruct((n_e, d_model, d_ff), jnp.bfloat16), jax.ShapeDtypeStruct((n_e, d_ff, d_model), jnp.bfloat16),
+                   jax.ShapeDtypeStruct(y.shape, y.dtype), jax.ShapeDtypeStruct(dg.shape, dg.dtype)],
         in_specs=[pl.BlockSpec((rows, d_model), lambda i: (i, 0)), pl.BlockSpec((rows, d_ff), lambda i: (i, 0)),
-                  pl.BlockSpec((rows, d_model), lambda i: (i, 0)), pl.BlockSpec((rows, d_ff), lambda i: (i, 0))],
-        out_specs=[pl.BlockSpec((PAIR, d_model, d_ff), lambda i: (i, 0, 0)), pl.BlockSpec((PAIR, d_ff, d_model), lambda i: (i, 0, 0))],
-        compiler_params=pltpu.CompilerParams(vmem_limit_bytes=48 * 1024 * 1024),
+                  pl.BlockSpec((rows, d_model), lambda i: (i, 0)), pl.BlockSpec((rows, d_ff), lambda i: (i, 0))] + whole,
+        out_specs=[pl.BlockSpec((PAIR, d_model, d_ff), lambda i: (i, 0, 0)), pl.BlockSpec((PAIR, d_ff, d_model), lambda i: (i, 0, 0))] + whole,
+        compiler_params=pltpu.CompilerParams(vmem_limit_bytes=62 * 1024 * 1024),
         cost_estimate=pl.CostEstimate(flops=4 * n_e * SLOTS * d_model * d_ff, bytes_accessed=4 * n_e * d_model * d_ff, transcendentals=0),
-    )(b, h, g, da)
+    )(b, h, g, da, y, dg)
 
 
 def solution(mesh):
@@ -362,9 +371,9 @@
     to_cross = [(i, i ^ 2) for i in range(4)]
 
     def device_pass(x_in, expert_idx, gate_weight, grad_y, w_in, w_out):
-        y_out, dg, dx_own, dx_far, b, h, g, da = experts(x_in, grad_y, expert_idx.T, gate_weight.T, w_in, w_out)
+        y_mid, dg, dx_own, dx_far, b, h, g, da = experts(x_in, grad_y, expert_idx.T, gate_weight.T, w_in, w_out)
         dx_got = lax.ppermute(dx_far, 'expert', to_cross)
-        grad_w_in, grad_w_out = weight_grads(b, h, g, da, w_in.shape[0])
+        grad_w_in, grad_w_out, y_out, dg = weight_grads(b, h, g, da, y_mid, dg, w_in.shape[0])
         grad_x = (grad_y.astype(jnp.float32) + (dx_own + dx_got)).astype(jnp.bfloat16)
         return y_out, grad_x, dg.T, grad_w_in, grad_w_out
 

time: 110 us -> 92.5 us (0.84)
  Pallas kernels: 97.5 us -> 87.3 us
  local copies, waits for them, and re-layouts: 7.37 us -> 0.01 us
    pallas_call x1, Pallas kernels: 75.9 us -> 61.8 us  [experts(): pl.pallas_call(expert_kernel, out_shape=[shape((128, d_model), bf), shape...]
    unnamed x10 -> x2, local copies, waits for them, and re-layouts: 7.37 us -> 0.01 us
    pallas_call x1, Pallas kernels: 21.6 us -> 25.5 us  [weight_grads(): pl.pallas_call(weight_kernel, grid=(n_e // PAIR,), out_shape=[jax.ShapeDt...]
  transfers between devices with their start and end apart: 1 -> 1, of which waited for: 0 -> 0; matrix products, arithmetic and copies ran while one was open for 0% -> 0% of each run, Pallas kernels for 20% -> 28%
where the time goes in v3:
time: 92.5 us; the launch traced here: 91.9 us
  Pallas kernels  87.3 us (94%)
  starting transfers between devices  2.04 us (2%)
  other arithmetic  1.84 us (2%)
    pallas_call x1, Pallas kernels, experts(): pl.pallas_call(expert_kernel, out_shape=[shape((128, d_model), bf), shape...  61.8 us
    pallas_call x1, Pallas kernels, weight_grads(): pl.pallas_call(weight_kernel, grid=(n_e // PAIR,), out_shape=[jax.ShapeDt...  25.5 us
    ppermute x1, starting transfers between devices, device_pass(): dx_got = lax.ppermute(dx_far, 'expert', to_cross)  2.04 us
  transfers between devices with their start and end apart: 1, of which 0 were waited for; matrix products, arithmetic and copies ran while one was open for 0% of the time, Pallas kernels for 28%

profile of v3, /device:TPU:0, one launch (start us, length us, event | category | flops | bytes accessed | tf_op | source)
XLA Modules:
  0.0 91.9 jit_solution(16709684376940064155)
XLA Ops:
  0.6 0.0 copy-start
  0.6 61.8 %shard_map.101 = (bf16[128,1024]{1,0:T(8,128)(2,1)}, f32[8,128]{1,0:T(8,128)}, f32[128,1024]{1,0:T(8,128)}, f32[128,1024]{1,0:T(8,128)}, bf16[1536,1024]{1,0:T(8...) custom-call(bf16[128,1024]{1,0:T(8,128)(2,1)} %x.1, ...), custom_call_target="tpu_custom_call" | custom-call | flops 4831838208 | bytes 100663296 | tf_op jit(solution)/shard_map/pallas_call | solution.py:315
  62.4 2.0 %collective-permute-start = (f32[128,1024]{1,0:T(8,128)}, f32[128,1024]{1,0:T(8,128)S(1)}, u32[]{:S(2)}, u32[]{:S(2)}) collective-permute-start(f32[128,1024]{1,0:T(8,128)} %get-tuple-element.25), channel_id=1, source_target_pairs={{0,2},{1,3},{2,0},{3,1},{4,6},{5,7},{6,4},{7,5}} | collective-permute-start | bytes 1572872 | tf_op jit(solution)/shard_map/ppermute | solution.py:375
  64.5 25.5 %shard_map.102 = (bf16[32,1024,384]{2,1,0:T(8,128)(2,1)}, bf16[32,384,1024]{2,1,0:T(8,128)(2,1)}, bf16[128,1024]{1,0:T(8,128)(2,1)}, f32[8,128]{1,0:T(8,128)}) custom-call(bf16[1536,1024]{1,0:T(8,128)(2,1)} %get-tuple-element.17.b, bf16[1536,384]{1,0:T(8,128)(2,1)} %get-tuple-element.18.h, bf16[1536,1024]{1,0:T(8,128)(2,1)} %get-tuple-element.19.g, ...), custom_call_target="tpu_custom_call" | custom-call | flops 2415919104 | bytes 50331648 | tf_op jit(solution)/shard_map/pallas_call | solution.py:354
  90.0 0.0 collective-permute-done
  90.0 0.0 copy-done
  90.0 1.8 %add_convert_fusion = bf16[128,1024]{1,0:T(8,128)(2,1)} fusion(f32[128,1024]{1,0:T(8,128)} %get-tuple-element.24, f32[128,1024]{1,0:T(8,128)S(1)} %collective-permute-done, bf16[128,1024]{1,0:T(8,128)(2,1)S(1)} %copy-done), kind=kLoop, calls=%fused_computation | loop fusion | flops 524288 | bytes 1572864 | tf_op jit(solution)/shard_map/convert_element_type | solution.py:377
Async XLA Ops:
  0.6 89.4 %copy-start = (bf16[128,1024]{1,0:T(8,128)(2,1)S(1)}, bf16[128,1024]{1,0:T(8,128)(2,1)}, u32[]{:S(2)}) copy-start(bf16[128,1024]{1,0:T(8,128)(2,1)} %dy.1) | copy-start | bytes 786436
  62.4 27.6 %collective-permute-start = (f32[128,1024]{1,0:T(8,128)}, f32[128,1024]{1,0:T(8,128)S(1)}, u32[]{:S(2)}, u32[]{:S(2)}) collective-permute-start(f32[128,1024]{1,0:T(8,128)} %get-tuple-element.25), channel_id=1, source_target_pairs={{0,2},{1,3},{2,0},{3,1},{4,6},{5,7},{6,4},{7,5}} | collective-permute-start | bytes 1572872 | tf_op jit(solution)/shard_map/ppermute | solution.py:375

commit v4 on v3

--- a/solution.py
+++ b/solution.py
@@ -42,10 +42,10 @@
     return pl.ds(pl.multiple_of(e * SLOTS, SLOTS), SLOTS)
 
 
-def expert_kernel(x, dy, idx, gate, w_in, w_out, y_out, dg_out, dx_own, dx_far, b_out, h_out, g_out, da_out,
-                  xa, dya, ida, ga, rj, r0s, r1s, pm, pt, gs, b_s, g_s, h_s, da_s, o_s, slope, sp, zs, dg_tab, dgp, dgr,
+def expert_kernel(x, dy, idx, gate, w_in, w_out, y_out, dg_out, dx_own, dx_far, b_s, h_s, g_s, da_s,
+                  xa, dya, ida, ga, rj, r0s, r1s, pm, pt, gs, o_s, slope, sp, zs, dg_tab, dgp, dgr,
                   wi, wo, yp, yr, yfar, ygot, dxp, dxr,
-                  wi_sem, wo_sem, out_sem, small_s, small_r, sib_s, sib_r, cross_s, cross_r, fwd_s, fwd_r,
+                  wi_sem, wo_sem, small_s, small_r, sib_s, sib_r, cross_s, cross_r, fwd_s, fwd_r,
                   yd_s, yd_r, yx_s, yx_r, dd_s, dd_r, dg_s, dg_r):
     me = lax.axis_index("expert")
     sib, cross = me + 1 - 2 * lax.rem(me, 2), lax.rem(me + 2, 4)
@@ -132,7 +132,6 @@
         return 0
 
     lax.fori_loop(0, slots // PICK, pick_x, 0)
-    pltpu.make_async_copy(b_s, b_out, out_sem.at[0]).start()
 
     def fwd_step(i, _):
         slot = lax.rem(i, AHEAD)
@@ -174,7 +173,6 @@
         return 0
 
     lax.fori_loop(0, n_pairs, fwd_step, 0)
-    pltpu.make_async_copy(h_s, h_out, out_sem.at[1]).start()
 
     def to_sib(part, got, s, r, n, k):
         return remote(part.at[n, sib if k == 0 else diag], got.at[n, k], s.at[n, k], r.at[n, k], sib)
@@ -209,7 +207,6 @@
         return 0
 
     lax.fori_loop(0, slots // PICK, pick_dy, 0)
-    pltpu.make_async_copy(g_s, g_out, out_sem.at[2]).start()
     for n in range(4):
         for k in range(2):
             to_sib(yp, yr, yd_s, yd_r, n, k).wait()
@@ -268,7 +265,6 @@
         return 0
 
     lax.fori_loop(1, n_pairs, bwd_step, 0)
-    pltpu.make_async_copy(da_s, da_out, out_sem.at[3]).start()
     fetch_in(0, lax.rem(last, AHEAD)).wait()
     back_x(0, last)
 
@@ -302,8 +298,6 @@
         dx_far[:, lanes] = dxp[n, cross] + dxr[n, 1]
     for copy in small + over + near + far:
         copy.wait_send()
-    for k, (src, dst) in enumerate(((b_s, b_out), (h_s, h_out), (g_s, g_out), (da_s, da_out))):
-        pltpu.make_async_copy(src, dst, out_sem.at[k]).wait()
 
 
 def experts(x, dy, idx_t, gate_t, w_in, w_out):
@@ -311,33 +305,32 @@
     slots = n_e * SLOTS
     bf, f32 = jnp.bfloat16, jnp.float32
     vmem, hbm = pl.BlockSpec(memory_space=pltpu.VMEM), pl.BlockSpec(memory_space=pl.ANY)
-    shape, buf, dma = jax.ShapeDtypeStruct, pltpu.VMEM, pltpu.SemaphoreType.DMA
+    buf, dma = pltpu.VMEM, pltpu.SemaphoreType.DMA
     return pl.pallas_call(
         expert_kernel,
-        out_shape=[shape((128, d_model), bf), shape((8, 128), f32), shape((128, d_model), f32), shape((128, d_model), f32),
-                   shape((slots, d_model), bf), shape((slots, d_ff), bf), shape((slots, d_model), bf), shape((slots, d_ff), bf)],
+        out_shape=[buf((128, d_model), bf), buf((8, 128), f32), buf((128, d_model), f32), buf((128, d_model), f32),
+                   buf((slots, d_model), bf), buf((slots, d_ff), bf), buf((slots, d_model), bf), buf((slots, d_ff), bf)],
         in_specs=[vmem] * 4 + [hbm] * 2,
-        out_specs=[vmem] * 4 + [hbm] * 4,
+        out_specs=[vmem] * 8,
         scratch_shapes=[
             buf((4, 128, d_model), bf), buf((4, 128, d_model), bf), buf((4, 8, 128), jnp.int32), buf((4, 8, 128), f32),
             buf((8, 4, n_e, 128), f32), buf((4, n_e, 128), f32), buf((4, n_e, 128), f32),
             buf((slots, 512), bf), buf((512, slots), bf), buf((slots, 1), f32),
-            buf((slots, d_model), bf), buf((slots, d_model), bf), buf((slots, d_ff), bf), buf((slots, d_ff), bf),
             buf((slots, d_model), bf), buf((slots, d_ff), f32), buf((3, slots, d_model), bf), buf((2, 128, PAIR * d_ff), bf),
             buf((n_e, 128), f32), buf((4, 8, 128), f32), buf((3, 8, 128), f32),
             buf((AHEAD, PAIR, d_model, d_ff), bf), buf((AHEAD, PAIR, d_ff, d_model), bf),
             buf((4, 4, 128, 256), f32), buf((4, 2, 128, 256), f32), buf((4, 128, 256), f32), buf((4, 128, 256), f32),
             buf((4, 4, 128, 256), f32), buf((4, 2, 128, 256), f32),
-            dma((AHEAD,)), dma((AHEAD,)), dma((4,)), dma((6,)), dma((6,)), dma((2,)), dma((2,)), dma((4,)), dma((4,)),
+            dma((AHEAD,)), dma((AHEAD,)), dma((6,)), dma((6,)), dma((2,)), dma((2,)), dma((4,)), dma((4,)),
             dma((4,)), dma((4,)), dma((4, 2)), dma((4, 2)), dma(()), dma(()), dma((4, 2)), dma((4, 2)), dma((3,)), dma((3,))],
-        compiler_params=pltpu.CompilerParams(collective_id=0, has_side_effects=True, vmem_limit_bytes=63 * 1024 * 1024),
+        compiler_params=pltpu.CompilerParams(collective_id=0, has_side_effects=True, vmem_limit_bytes=53 * 1024 * 1024),
         cost_estimate=pl.CostEstimate(flops=8 * slots * d_model * d_ff, bytes_accessed=8 * n_e * d_model * d_ff, transcendentals=0),
     )(x, dy, idx_t, gate_t, w_in, w_out)
 
 
 def weight_kernel(b, h, g, da, y, dg, dw_in, dw_out, y_out, dg_out):
     for p in range(PAIR):
-        at = slice(p * SLOTS, (p + 1) * SLOTS)
+        at = slot_rows(pl.program_id(0) * PAIR + p)
         dw_in[p] = dot(b[at, :], da[at, :], ((0,), (0,))).astype(jnp.bfloat16)
         dw_out[p] = dot(h[at, :], g[at, :], ((0,), (0,))).astype(jnp.bfloat16)
 
@@ -349,17 +342,15 @@
 
 def weight_grads(b, h, g, da, y, dg, n_e):
     d_model, d_ff = b.shape[1], h.shape[1]
-    rows = PAIR * SLOTS
     whole = [pl.BlockSpec(y.shape, lambda i: (0, 0)), pl.BlockSpec(dg.shape, lambda i: (0, 0))]
     return pl.pallas_call(
         weight_kernel,
         grid=(n_e // PAIR,),
         out_shape=[jax.ShapeDtypeStruct((n_e, d_model, d_ff), jnp.bfloat16), jax.ShapeDtypeStruct((n_e, d_ff, d_model), jnp.bfloat16),
                    jax.ShapeDtypeStruct(y.shape, y.dtype), jax.ShapeDtypeStruct(dg.shape, dg.dtype)],
-        in_specs=[pl.BlockSpec((rows, d_model), lambda i: (i, 0)), pl.BlockSpec((rows, d_ff), lambda i: (i, 0)),
-                  pl.BlockSpec((rows, d_model), lambda i: (i, 0)), pl.BlockSpec((rows, d_ff), lambda i: (i, 0))] + whole,
+        in_specs=[pl.BlockSpec(memory_space=pltpu.VMEM)] * 6,
         out_specs=[pl.BlockSpec((PAIR, d_model, d_ff), lambda i: (i, 0, 0)), pl.BlockSpec((PAIR, d_ff, d_model), lambda i: (i, 0, 0))] + whole,
-        compiler_params=pltpu.CompilerParams(vmem_limit_bytes=62 * 1024 * 1024),
+        compiler_params=pltpu.CompilerParams(vmem_limit_bytes=40 * 1024 * 1024),
         cost_estimate=pl.CostEstimate(flops=4 * n_e * SLOTS * d_model * d_ff, bytes_accessed=4 * n_e * d_model * d_ff, transcendentals=0),
     )(b, h, g, da, y, dg)
 

time: 92.5 us -> 86.6 us (0.936)
  Pallas kernels: 87.3 us -> 83 us
  other arithmetic: 1.84 us -> 0.81 us
    pallas_call x1, Pallas kernels: 25.5 us -> 22.3 us  [weight_grads(): pl.pallas_call(weight_kernel, grid=(n_e // PAIR,), out_shape=[jax.ShapeDt...]
    pallas_call x1, Pallas kernels: 61.8 us -> 60.7 us  [experts(): pl.pallas_call(expert_kernel, out_shape=[buf((128, d_model), bf), buf((8,...]
    convert_element_type x1, other arithmetic: 1.84 us -> 0.81 us  [device_pass(): (grad_y.astype(jnp.float32) + (dx_own + dx_got)).astype(jnp.bfloat16)]
  transfers between devices with their start and end apart: 1 -> 1, of which waited for: 0 -> 0; matrix products, arithmetic and copies ran while one was open for 0% -> 0% of each run, Pallas kernels for 28% -> 26%
where the time goes in v4:
time: 86.6 us; the launch traced here: 86.5 us
  Pallas kernels  83 us (96%)
  starting transfers between devices  2.04 us (2%)
    pallas_call x1, Pallas kernels, experts(): pl.pallas_call(expert_kernel, out_shape=[buf((128, d_model), bf), buf((8,...  60.7 us
    pallas_call x1, Pallas kernels, weight_grads(): pl.pallas_call(weight_kernel, grid=(n_e // PAIR,), out_shape=[jax.ShapeDt...  22.3 us
    ppermute x1, starting transfers between devices, device_pass(): dx_got = lax.ppermute(dx_far, 'expert', to_cross)  2.04 us
  transfers between devices with their start and end apart: 1, of which 0 were waited for; matrix products, arithmetic and copies ran while one was open for 0% of the time, Pallas kernels for 26%

profile of v4, /device:TPU:0, one launch (start us, length us, event | category | flops | bytes accessed | tf_op | source)
XLA Modules:
  0.0 86.5 jit_solution(18015673562795801487)
XLA Ops:
  0.6 0.0 copy-start
  0.6 60.7 %shard_map.101 = (bf16[128,1024]{1,0:T(8,128)(2,1)S(1)}, f32[8,128]{1,0:T(8,128)S(1)}, f32[128,1024]{1,0:T(8,128)S(1)}, f32[128,1024]{1,0:T(8,128)S(1)}, bf16[15...) custom-call(bf16[128,1024]{1,0:T(8,128)(2,1)} %x.1, ...), custom_call_target="tpu_custom_call" | custom-call | flops 4831838208 | bytes 100663296 | tf_op jit(solution)/shard_map/pallas_call | solution.py:309
  61.3 2.0 %collective-permute-start = (f32[128,1024]{1,0:T(8,128)S(1)}, f32[128,1024]{1,0:T(8,128)S(1)}, u32[]{:S(2)}, u32[]{:S(2)}) collective-permute-start(f32[128,1024]{1,0:T(8,128)S(1)} %get-tuple-element.25), channel_id=1, source_target_pairs={{0,2},{1,3},{2,0},{3,1},{4,6},{5,7},{6,4},{7,5}} | collective-permute-start | bytes 1572872 | tf_op jit(solution)/shard_map/ppermute | solution.py:366
  63.4 22.3 %shard_map.102 = (bf16[32,1024,384]{2,1,0:T(8,128)(2,1)}, bf16[32,384,1024]{2,1,0:T(8,128)(2,1)}, bf16[128,1024]{1,0:T(8,128)(2,1)}, f32[8,128]{1,0:T(8,128)}) custom-call(bf16[1536,1024]{1,0:T(8,128)(2,1)S(1)} %get-tuple-element.17.b, bf16[1536,384]{1,0:T(8,128)(2,1)S(1)} %get-tuple-element.18.h, bf16[1536,1024]{1,0:T(8,128)(2,1)S(1)} %get-tuple-element.19.g, ...), custom_call_target="tpu_custom_call" | custom-call | flops 2415919104 | bytes 50331648 | tf_op jit(solution)/shard_map/pallas_call | solution.py:346
  85.7 0.0 collective-permute-done
  85.7 0.0 copy-done
  85.7 0.8 add_convert_fusion
Async XLA Ops:
  0.6 85.1 %copy-start = (bf16[128,1024]{1,0:T(8,128)(2,1)S(1)}, bf16[128,1024]{1,0:T(8,128)(2,1)}, u32[]{:S(2)}) copy-start(bf16[128,1024]{1,0:T(8,128)(2,1)} %dy.1) | copy-start | bytes 786436
  61.3 24.3 %collective-permute-start = (f32[128,1024]{1,0:T(8,128)S(1)}, f32[128,1024]{1,0:T(8,128)S(1)}, u32[]{:S(2)}, u32[]{:S(2)}) collective-permute-start(f32[128,1024]{1,0:T(8,128)S(1)} %get-tuple-element.25), channel_id=1, source_target_pairs={{0,2},{1,3},{2,0},{3,1},{4,6},{5,7},{6,4},{7,5}} | collective-permute-start | bytes 1572872 | tf_op jit(solution)/shard_map/ppermute | solution.py:366

commit v5 on v4

--- a/solution.py
+++ b/solution.py
@@ -11,6 +11,7 @@
 CAP = 40
 SLOTS = 48
 PAIR = 2
+RING = 4
 AHEAD = 4
 PICK = 384
 C0 = 0.7978845608028654
@@ -42,10 +43,10 @@
     return pl.ds(pl.multiple_of(e * SLOTS, SLOTS), SLOTS)
 
 
-def expert_kernel(x, dy, idx, gate, w_in, w_out, y_out, dg_out, dx_own, dx_far, b_s, h_s, g_s, da_s,
-                  xa, dya, ida, ga, rj, r0s, r1s, pm, pt, gs, o_s, slope, sp, zs, dg_tab, dgp, dgr,
+def expert_kernel(x_hbm, dy_hbm, idx_hbm, gate_hbm, w_in, w_out, y_out, dg_out, dx_own, dx_far, b_s, h_s, g_s, da_s,
+                  x, dy, idx, gate, xa, dya, ida, ga, rj, r0s, r1s, pm, pt, gs, o_s, slope, sp, zs, dg_tab, dgp, dgr,
                   wi, wo, yp, yr, yfar, ygot, dxp, dxr,
-                  wi_sem, wo_sem, small_s, small_r, sib_s, sib_r, cross_s, cross_r, fwd_s, fwd_r,
+                  arg_sem, wi_sem, wo_sem, small_s, small_r, sib_s, sib_r, cross_s, cross_r, fwd_s, fwd_r,
                   yd_s, yd_r, yx_s, yx_r, dd_s, dd_r, dg_s, dg_r):
     me = lax.axis_index("expert")
     sib, cross = me + 1 - 2 * lax.rem(me, 2), lax.rem(me + 2, 4)
@@ -64,13 +65,19 @@
         return pltpu.make_async_remote_copy(src_ref=src, dst_ref=dst, send_sem=s, recv_sem=r,
                                             device_id={"expert": peer}, device_id_type=MESH)
 
+    barrier = pltpu.get_barrier_semaphore()
+    for peer in (sib, cross, diag):
+        pl.semaphore_signal(barrier, inc=1, device_id={"expert": peer}, device_id_type=MESH)
+    args = [pltpu.make_async_copy(src, dst, arg_sem.at[k])
+            for k, (src, dst) in enumerate(((idx_hbm, idx), (gate_hbm, gate), (x_hbm, x), (dy_hbm, dy)))]
+    for copy in args:
+        copy.start()
     for q in range(AHEAD):
         fetch_in(q, q).start()
         fetch_out(q, q).start()
-
-    barrier = pltpu.get_barrier_semaphore()
-    for peer in (sib, cross, diag):
-        pl.semaphore_signal(barrier, inc=1, device_id={"expert": peer}, device_id_type=MESH)
+    zs[...] = jnp.zeros_like(zs)
+    for copy in args:
+        copy.wait()
     pl.semaphore_wait(barrier, 3)
 
     small, over, near, far = [], [], [], []
@@ -90,7 +97,6 @@
     dya[me] = dy[...]
     ida[me] = idx[...]
     ga[me] = gate[...]
-    zs[...] = jnp.zeros_like(zs)
 
     def forward(n):
         over[n].wait_recv()
@@ -310,9 +316,10 @@
         expert_kernel,
         out_shape=[buf((128, d_model), bf), buf((8, 128), f32), buf((128, d_model), f32), buf((128, d_model), f32),
                    buf((slots, d_model), bf), buf((slots, d_ff), bf), buf((slots, d_model), bf), buf((slots, d_ff), bf)],
-        in_specs=[vmem] * 4 + [hbm] * 2,
+        in_specs=[hbm] * 6,
         out_specs=[vmem] * 8,
         scratch_shapes=[
+            buf((128, d_model), bf), buf((128, d_model), bf), buf((8, 128), jnp.int32), buf((8, 128), f32),
             buf((4, 128, d_model), bf), buf((4, 128, d_model), bf), buf((4, 8, 128), jnp.int32), buf((4, 8, 128), f32),
             buf((8, 4, n_e, 128), f32), buf((4, n_e, 128), f32), buf((4, n_e, 128), f32),
             buf((slots, 512), bf), buf((512, slots), bf), buf((slots, 1), f32),
@@ -321,35 +328,58 @@
             buf((AHEAD, PAIR, d_model, d_ff), bf), buf((AHEAD, PAIR, d_ff, d_model), bf),
             buf((4, 4, 128, 256), f32), buf((4, 2, 128, 256), f32), buf((4, 128, 256), f32), buf((4, 128, 256), f32),
             buf((4, 4, 128, 256), f32), buf((4, 2, 128, 256), f32),
-            dma((AHEAD,)), dma((AHEAD,)), dma((6,)), dma((6,)), dma((2,)), dma((2,)), dma((4,)), dma((4,)),
+            dma((4,)), dma((AHEAD,)), dma((AHEAD,)), dma((6,)), dma((6,)), dma((2,)), dma((2,)), dma((4,)), dma((4,)),
             dma((4,)), dma((4,)), dma((4, 2)), dma((4, 2)), dma(()), dma(()), dma((4, 2)), dma((4, 2)), dma((3,)), dma((3,))],
         compiler_params=pltpu.CompilerParams(collective_id=0, has_side_effects=True, vmem_limit_bytes=53 * 1024 * 1024),
         cost_estimate=pl.CostEstimate(flops=8 * slots * d_model * d_ff, bytes_accessed=8 * n_e * d_model * d_ff, transcendentals=0),
     )(x, dy, idx_t, gate_t, w_in, w_out)
 
 
-def weight_kernel(b, h, g, da, y, dg, dw_in, dw_out, y_out, dg_out):
-    for p in range(PAIR):
-        at = slot_rows(pl.program_id(0) * PAIR + p)
-        dw_in[p] = dot(b[at, :], da[at, :], ((0,), (0,))).astype(jnp.bfloat16)
-        dw_out[p] = dot(h[at, :], g[at, :], ((0,), (0,))).astype(jnp.bfloat16)
-
-    @pl.when(pl.program_id(0) == 0)
-    def _():
-        y_out[...] = y[...]
-        dg_out[...] = dg[...]
+def weight_kernel(b, h, g, da, y, dg, dw_in, dw_out, y_out, dg_out, ring_in, ring_out, sem_in, sem_out, sem):
+    n_steps = dw_in.shape[0] // PAIR
+    passed = [pltpu.make_async_copy(y, y_out, sem.at[0]), pltpu.make_async_copy(dg, dg_out, sem.at[1])]
+    for copy in passed:
+        copy.start()
+
+    def copies(i):
+        slot = lax.rem(i, RING)
+        return [pltpu.make_async_copy(ring.at[slot, p], out.at[i * PAIR + p], sems.at[slot, p])
+                for p in range(PAIR) for ring, out, sems in ((ring_in, dw_in, sem_in), (ring_out, dw_out, sem_out))]
+
+    def step(i, _):
+        slot = lax.rem(i, RING)
+
+        @pl.when(i >= RING)
+        def _():
+            for copy in copies(i - RING):
+                copy.wait()
+
+        for p in range(PAIR):
+            at = slot_rows(i * PAIR + p)
+            ring_in[slot, p] = dot(b[at, :], da[at, :], ((0,), (0,))).astype(jnp.bfloat16)
+            ring_out[slot, p] = dot(h[at, :], g[at, :], ((0,), (0,))).astype(jnp.bfloat16)
+        for copy in copies(i):
+            copy.start()
+        return 0
+
+    lax.fori_loop(0, n_steps, step, 0)
+    for i in range(n_steps - RING, n_steps):
+        for copy in copies(i):
+            copy.wait()
+    for copy in passed:
+        copy.wait()
 
 
 def weight_grads(b, h, g, da, y, dg, n_e):
     d_model, d_ff = b.shape[1], h.shape[1]
-    whole = [pl.BlockSpec(y.shape, lambda i: (0, 0)), pl.BlockSpec(dg.shape, lambda i: (0, 0))]
+    bf, shape, dma = jnp.bfloat16, jax.ShapeDtypeStruct, pltpu.SemaphoreType.DMA
     return pl.pallas_call(
         weight_kernel,
-        grid=(n_e // PAIR,),
-        out_shape=[jax.ShapeDtypeStruct((n_e, d_model, d_ff), jnp.bfloat16), jax.ShapeDtypeStruct((n_e, d_ff, d_model), jnp.bfloat16),
-                   jax.ShapeDtypeStruct(y.shape, y.dtype), jax.ShapeDtypeStruct(dg.shape, dg.dtype)],
+        out_shape=[shape((n_e, d_model, d_ff), bf), shape((n_e, d_ff, d_model), bf), shape(y.shape, y.dtype), shape(dg.shape, dg.dtype)],
         in_specs=[pl.BlockSpec(memory_space=pltpu.VMEM)] * 6,
-        out_specs=[pl.BlockSpec((PAIR, d_model, d_ff), lambda i: (i, 0, 0)), pl.BlockSpec((PAIR, d_ff, d_model), lambda i: (i, 0, 0))] + whole,
+        out_specs=[pl.BlockSpec(memory_space=pl.ANY)] * 4,
+        scratch_shapes=[pltpu.VMEM((RING, PAIR, d_model, d_ff), bf), pltpu.VMEM((RING, PAIR, d_ff, d_model), bf),
+                        dma((RING, PAIR)), dma((RING, PAIR)), dma((2,))],
         compiler_params=pltpu.CompilerParams(vmem_limit_bytes=40 * 1024 * 1024),
         cost_estimate=pl.CostEstimate(flops=4 * n_e * SLOTS * d_model * d_ff, bytes_accessed=4 * n_e * d_model * d_ff, transcendentals=0),
     )(b, h, g, da, y, dg)

time: 86.6 us -> 84.1 us (0.971)
  starting transfers between devices: 2.04 us -> 0.03 us
    pallas_call x1, Pallas kernels: 22.3 us -> 18.1 us  [weight_grads(): pl.pallas_call(weight_kernel, out_shape=[shape((n_e, d_model, d_ff), bf),...]
    pallas_call x1, Pallas kernels: 60.7 us -> 64.3 us  [experts(): pl.pallas_call(expert_kernel, out_shape=[buf((128, d_model), bf), buf((8,...]
    ppermute x1, starting transfers between devices: 2.04 us -> 0.03 us  [device_pass(): dx_got = lax.ppermute(dx_far, 'expert', to_cross)]
  transfers between devices with their start and end apart: 1 -> 1, of which waited for: 0 -> 0; matrix products, arithmetic and copies ran while one was open for 0% -> 0% of each run, Pallas kernels for 26% -> 22%
where the time goes in v5:
time: 84.1 us; the launch traced here: 84 us
  Pallas kernels  82.4 us (98%)
    pallas_call x1, Pallas kernels, experts(): pl.pallas_call(expert_kernel, out_shape=[buf((128, d_model), bf), buf((8,...  64.3 us
    pallas_call x1, Pallas kernels, weight_grads(): pl.pallas_call(weight_kernel, out_shape=[shape((n_e, d_model, d_ff), bf),...  18.1 us
  transfers between devices with their start and end apart: 1, of which 0 were waited for; matrix products, arithmetic and copies ran while one was open for 0% of the time, Pallas kernels for 22%

profile of v5, /device:TPU:0, one launch (start us, length us, event | category | flops | bytes accessed | tf_op | source)
XLA Modules:
  0.0 84.0 jit_solution(5462113818563089424)
XLA Ops:
  0.6 0.0 copy-start
  0.6 64.3 %shard_map.101 = (bf16[128,1024]{1,0:T(8,128)(2,1)S(1)}, f32[8,128]{1,0:T(8,128)S(1)}, f32[128,1024]{1,0:T(8,128)S(1)}, f32[128,1024]{1,0:T(8,128)S(1)}, bf16[15...) custom-call(bf16[128,1024]{1,0:T(8,128)(2,1)} %x_hbm.1, ...), custom_call_target="tpu_custom_call" | custom-call | flops 4831838208 | bytes 100663296 | tf_op jit(solution)/shard_map/pallas_call | solution.py:315
  64.9 0.0 collective-permute-start
  65.0 18.1 %shard_map.102 = (bf16[32,1024,384]{2,1,0:T(8,128)(2,1)}, bf16[32,384,1024]{2,1,0:T(8,128)(2,1)}, bf16[128,1024]{1,0:T(8,128)(2,1)}, f32[8,128]{1,0:T(8,128)}) custom-call(bf16[1536,1024]{1,0:T(8,128)(2,1)S(1)} %get-tuple-element.17.b, bf16[1536,384]{1,0:T(8,128)(2,1)S(1)} %get-tuple-element.18.h, bf16[1536,1024]{1,0:T(8,128)(2,1)S(1)} %get-tuple-element.19.g, ...), custom_call_target="tpu_custom_call" | custom-call | flops 2415919104 | bytes 50331648 | tf_op jit(solution)/shard_map/pallas_call | solution.py:376
  83.1 0.0 collective-permute-done
  83.1 0.0 copy-done
  83.1 0.8 add_convert_fusion
Async XLA Ops:
  0.6 82.5 %copy-start = (bf16[128,1024]{1,0:T(8,128)(2,1)S(1)}, bf16[128,1024]{1,0:T(8,128)(2,1)}, u32[]{:S(2)}) copy-start(bf16[128,1024]{1,0:T(8,128)(2,1)} %dy_hbm.1) | copy-start | bytes 786436
  64.9 18.2 %collective-permute-start = (f32[128,1024]{1,0:T(8,128)S(1)}, f32[128,1024]{1,0:T(8,128)S(1)}, u32[]{:S(2)}, u32[]{:S(2)}) collective-permute-start(f32[128,1024]{1,0:T(8,128)S(1)} %get-tuple-element.25), channel_id=1, source_target_pairs={{0,2},{1,3},{2,0},{3,1},{4,6},{5,7},{6,4},{7,5}} | collective-permute-start | bytes 1572872 | tf_op jit(solution)/shard_map/ppermute | solution.py:396

commit v6 on v5

--- a/solution.py
+++ b/solution.py
@@ -9,11 +9,10 @@
 
 MESH = pl.DeviceIdType.MESH
 CAP = 40
-SLOTS = 48
 PAIR = 2
 RING = 4
 AHEAD = 4
-PICK = 384
+PICK = 640
 C0 = 0.7978845608028654
 C1 = 0.044715
 
@@ -39,12 +38,12 @@
         offset = offset + jnp.sum(count, axis=1, keepdims=True)
 
 
-def slot_rows(e):
-    return pl.ds(pl.multiple_of(e * SLOTS, SLOTS), SLOTS)
+def pair_rows(q):
+    return pl.ds(pl.multiple_of(q * PAIR * CAP, 16), PAIR * CAP)
 
 
 def expert_kernel(x_hbm, dy_hbm, idx_hbm, gate_hbm, w_in, w_out, y_out, dg_out, dx_own, dx_far, b_s, h_s, g_s, da_s,
-                  x, dy, idx, gate, xa, dya, ida, ga, rj, r0s, r1s, pm, pt, gs, o_s, slope, sp, zs, dg_tab, dgp, dgr,
+                  x, dy, idx, gate, xa, dya, ida, ga, rj, r0s, r1s, pm, pt, gs, o_s, slope, sp, dg_tab, dgp, dgr,
                   wi, wo, yp, yr, yfar, ygot, dxp, dxr,
                   arg_sem, wi_sem, wo_sem, small_s, small_r, sib_s, sib_r, cross_s, cross_r, fwd_s, fwd_r,
                   yd_s, yd_r, yx_s, yx_r, dd_s, dd_r, dg_s, dg_r):
@@ -52,8 +51,9 @@
     sib, cross = me + 1 - 2 * lax.rem(me, 2), lax.rem(me + 2, 4)
     diag = lax.rem(sib + 2, 4)
     n_pairs = w_in.shape[0] // PAIR
-    slots = 32 * SLOTS
+    slots = 32 * CAP
     bf, f32 = jnp.bfloat16, jnp.float32
+    d_ff = w_in.shape[2]
 
     def fetch_in(q, slot):
         return pltpu.make_async_copy(w_in.at[pl.ds(PAIR * q, PAIR)], wi.at[slot], wi_sem.at[slot])
@@ -75,7 +75,6 @@
     for q in range(AHEAD):
         fetch_in(q, q).start()
         fetch_out(q, q).start()
-    zs[...] = jnp.zeros_like(zs)
     for copy in args:
         copy.wait()
     pl.semaphore_wait(barrier, 3)
@@ -105,28 +104,22 @@
     for copy in small:
         copy.wait_recv()
     tables(ida, me * 32, rj, r0s, r1s)
-    slot_id = lax.broadcasted_iota(jnp.int32, (SLOTS, 128), 0).astype(f32)
-
-    def one(e, _):
-        total = jnp.zeros((SLOTS, 128), f32)
+    slot_id = lax.broadcasted_iota(jnp.int32, (CAP, 128), 0).astype(f32)
+
+    def one(q, _):
+        inside, total = [], [jnp.zeros((CAP, 128), f32) for _ in range(PAIR)]
         for d in range(4):
-            lanes = slice(128 * d, 128 * (d + 1))
-            inside = (slot_id >= r0s[d, pl.ds(e, 1), :]) & (slot_id < r1s[d, pl.ds(e, 1), :])
-            pm[slot_rows(e), lanes] = jnp.where(inside, 1.0, 0.0).astype(bf)
-            for j in range(8):
-                total = jnp.where(slot_id == rj[j, d, pl.ds(e, 1), :], ga[d, j:j + 1, :], total)
-        gs[slot_rows(e), :] = jnp.sum(total, axis=1, keepdims=True)
-        return 0
-
-    lax.fori_loop(0, 32, one, 0)
+            for p in range(PAIR):
+                e = pl.ds(q * PAIR + p, 1)
+                inside.append(jnp.where((slot_id >= r0s[d, e, :]) & (slot_id < r1s[d, e, :]), 1.0, 0.0))
+                for j in range(8):
+                    total[p] = jnp.where(slot_id == rj[j, d, e, :], ga[d, j:j + 1, :], total[p])
+            pm[pair_rows(q), 128 * d:128 * (d + 1)] = jnp.concatenate(inside[-PAIR:], axis=0).astype(bf)
+        gs[pair_rows(q), :] = jnp.sum(jnp.concatenate(total, axis=0), axis=1, keepdims=True)
+        return 0
+
+    lax.fori_loop(0, n_pairs, one, 0)
     forward(0)
-
-    def turn(c, _):
-        at = pl.ds(pl.multiple_of(c * 128, 128), 128)
-        pt[:, at] = pm[at, :].astype(f32).T.astype(bf)
-        return 0
-
-    lax.fori_loop(0, slots // 128, turn, 0)
     forward(1)
     near[0].wait_recv()
     far[0].wait_recv()
@@ -139,28 +132,34 @@
 
     lax.fori_loop(0, slots // PICK, pick_x, 0)
 
+    first = lax.broadcasted_iota(jnp.int32, (PAIR * CAP, d_ff), 0) < CAP
+
     def fwd_step(i, _):
         slot = lax.rem(i, AHEAD)
         fetch_in(i, slot).wait()
         fetch_out(i, slot).wait()
-        for p in range(PAIR):
-            at = slot_rows(i * PAIR + p)
-            a = dot(b_s[at, :], wi[slot, p])
-            th = jnp.tanh(C0 * (a + C1 * (a * a * a)))
-            cdf = 0.5 * (1.0 + th)
-            slope[at, :] = cdf + 0.5 * a * (1.0 - th * th) * (C0 * (1.0 + 3.0 * C1 * (a * a)))
-            h = (a * cdf).astype(bf)
-            h_s[at, :] = h
-            o = dot(h, wo[slot, p]).astype(bf)
-            o_s[at, :] = o
-            s = o.astype(f32) * gs[at, :]
-            s1 = s.astype(bf)
-            s = s - s1.astype(f32)
-            s2 = s.astype(bf)
-            s = s - s2.astype(f32)
-            sp[0, at, :] = s1
-            sp[1, at, :] = s2
-            sp[2, at, :] = s.astype(bf)
+        at = pair_rows(i)
+        rows = b_s[at, :]
+        a = jnp.concatenate([dot(rows, wi[slot, 0])[:CAP], dot(rows, wi[slot, 1])[CAP:]], axis=0)
+        th = jnp.tanh(C0 * (a + C1 * (a * a * a)))
+        cdf = 0.5 * (1.0 + th)
+        slope[at, :] = cdf + 0.5 * a * (1.0 - th * th) * (C0 * (1.0 + 3.0 * C1 * (a * a)))
+        h = a * cdf
+        h = jnp.concatenate([jnp.where(first, h, 0.0), jnp.where(first, 0.0, h)], axis=1).astype(bf)
+        h_s[at, :] = h
+        o = dot(h, jnp.concatenate([wo[slot, 0], wo[slot, 1]], axis=0)).astype(bf)
+        o_s[at, :] = o
+        s = o.astype(f32) * gs[at, :]
+        s1 = s.astype(bf)
+        s = s - s1.astype(f32)
+        s2 = s.astype(bf)
+        s = s - s2.astype(f32)
+        sp[0, at, :] = s1
+        sp[1, at, :] = s2
+        sp[2, at, :] = s.astype(bf)
+        turned = i * (slots // 128) // n_pairs
+        tile = pl.ds(pl.multiple_of(turned * 128, 128), 128)
+        pt[:, tile] = pm[tile, :].astype(f32).T.astype(bf)
 
         @pl.when(i < n_pairs - AHEAD)
         def _():
@@ -208,8 +207,8 @@
         g_s[at, :] = (rows * gs[at, :]).astype(bf)
         prod = rows * o_s[at, :].astype(f32)
         part = sum((prod[:, 128 * k:128 * (k + 1)] for k in range(1, 8)), prod[:, :128])
-        for k in range(PICK // SLOTS):
-            dg_tab[pl.ds(c * (PICK // SLOTS) + k, 1), :SLOTS] = jnp.sum(part[SLOTS * k:SLOTS * (k + 1)].T, axis=0, keepdims=True)
+        for k in range(PICK // CAP):
+            dg_tab[pl.ds(c * (PICK // CAP) + k, 1), :CAP] = jnp.sum(part[CAP * k:CAP * (k + 1)].T, axis=0, keepdims=True)
         return 0
 
     lax.fori_loop(0, slots // PICK, pick_dy, 0)
@@ -226,53 +225,69 @@
     y_cross.start()
     dg_back = [remote(dgp.at[peer], dgr.at[k], dg_s.at[k], dg_r.at[k], peer) for k, peer in enumerate((cross, diag, sib))]
 
-    def zero(n, like):
-        return jnp.zeros((n, like.shape[1]), bf)
-
-    def back_h(q, i):
-        slot = lax.rem(i, AHEAD)
-        g0, g1 = g_s[slot_rows(q * PAIR), :], g_s[slot_rows(q * PAIR + 1), :]
-        both = dot(wo[slot, 0], jnp.concatenate([g0, zero(80, g0)], axis=0), ((1,), (1,)))
-        both = both + dot(wo[slot, 1], jnp.concatenate([zero(64, g1), g1, zero(16, g1)], axis=0), ((1,), (1,)))
-        dh = both.astype(bf).T.astype(f32)
-        for p in range(PAIR):
-            at = slot_rows(q * PAIR + p)
-            da = (dh[64 * p:64 * p + SLOTS] * slope[at, :]).astype(bf)
-            da_s[at, :] = da
-            zs[lax.rem(i, 2), 64 * p:64 * p + SLOTS, 384 * p:384 * (p + 1)] = da
-
-    def back_x(q, i):
-        slot = lax.rem(i, AHEAD)
+    mine = lax.broadcasted_iota(jnp.int32, (d_ff, PAIR * CAP), 1) < CAP
+    last = n_pairs - 1
+
+    def back_h(i):
+        slot, at = lax.rem(i, AHEAD), pair_rows(last - i)
+        g = g_s[at, :]
+        dh = jnp.where(mine, dot(wo[slot, 0], g, ((1,), (1,))), dot(wo[slot, 1], g, ((1,), (1,))))
+        da = dh.astype(bf).T.astype(f32) * slope[at, :]
+        da_s[at, :] = jnp.concatenate([jnp.where(first, da, 0.0), jnp.where(first, 0.0, da)], axis=1).astype(bf)
+
+    def back_x(i):
+        slot, at = lax.rem(i, AHEAD), pair_rows(last - i)
         wide = jnp.concatenate([wi[slot, 0], wi[slot, 1]], axis=1)
-        both = dot(wide, zs[lax.rem(i, 2)], ((1,), (1,))).astype(bf).T
-        for p in range(PAIR):
-            sp[0, slot_rows(q * PAIR + p), :] = both[64 * p:64 * p + SLOTS]
-
-    last = n_pairs - 1
-    fetch_out(last, 0).wait()
-    back_h(last, 0)
-    fetch_out(last - AHEAD, 0).start()
+        sp[0, at, :] = dot(wide, da_s[at, :], ((1,), (1,))).astype(bf).T
+
+    def wait_in(i):
+        fetch_in(last - i, lax.rem(i, AHEAD)).wait()
+
+    def wait_out(i):
+        fetch_out(last - i, lax.rem(i, AHEAD)).wait()
+
+    wait_out(0)
+    wait_out(1)
+    back_h(0)
+    back_h(1)
     for copy in dg_back:
         copy.start()
-
-    def bwd_step(i, _):
-        fetch_in(last + 1 - i, lax.rem(i - 1, AHEAD)).wait()
-        fetch_out(last - i, lax.rem(i, AHEAD)).wait()
-        back_x(last + 1 - i, i - 1)
-        back_h(last - i, i)
+    for i in range(2):
+        fetch_out(last - AHEAD - i, i).start()
+
+    def bwd_step(j, _):
+        i = 2 * j
+        for k in range(2):
+            wait_in(i - 2 + k)
+            wait_out(i + k)
+        back_x(i - 2)
+        back_x(i - 1)
+        back_h(i)
+        back_h(i + 1)
 
         @pl.when(i < n_pairs - AHEAD)
         def _():
-            fetch_out(last - AHEAD - i, lax.rem(i, AHEAD)).start()
-
-        @pl.when(i < n_pairs - AHEAD + 1)
-        def _():
-            fetch_in(last + 1 - AHEAD - i, lax.rem(i - 1, AHEAD)).start()
-        return 0
-
-    lax.fori_loop(1, n_pairs, bwd_step, 0)
-    fetch_in(0, lax.rem(last, AHEAD)).wait()
-    back_x(0, last)
+            for k in range(2):
+                fetch_out(last - AHEAD - i - k, lax.rem(i + k, AHEAD)).start()
+
+        @pl.when(i < n_pairs - AHEAD + 2)
+        def _():
+            for k in range(2):
+                fetch_in(last + 2 - AHEAD - i - k, lax.rem(i - 2 + k, AHEAD)).start()
+        return 0
+
+    lax.fori_loop(1, n_pairs // 2, bwd_step, 0)
+    y_cross.wait()
+    for copy in dg_back:
+        copy.wait()
+    for i in range(last - 1, last + 1):
+        wait_in(i)
+    dg_out[...] = dgp[me] + (dgr[0] + (dgr[1] + dgr[2]))
+    for n in range(4):
+        lanes = slice(256 * n, 256 * (n + 1))
+        y_out[:, lanes] = (x[:, lanes].astype(f32) + (yp[n, me] + yr[n, 0] + ygot[n])).astype(bf)
+    back_x(last - 1)
+    back_x(last)
 
     def dx_part(n, _):
         lanes = pl.ds(pl.multiple_of(n * 256, 256), 256)
@@ -287,15 +302,8 @@
         return 0
 
     lax.fori_loop(0, 4, dx_part, 0)
-    y_cross.wait()
     for k in range(2):
         to_sib(dxp, dxr, dd_s, dd_r, 3, k).start()
-    for n in range(4):
-        lanes = slice(256 * n, 256 * (n + 1))
-        y_out[:, lanes] = (x[:, lanes].astype(f32) + (yp[n, me] + yr[n, 0] + ygot[n])).astype(bf)
-    for copy in dg_back:
-        copy.wait()
-    dg_out[...] = dgp[me] + (dgr[0] + (dgr[1] + dgr[2]))
     for n in range(4):
         lanes = slice(256 * n, 256 * (n + 1))
         for k in range(2):
@@ -308,14 +316,14 @@
 
 def experts(x, dy, idx_t, gate_t, w_in, w_out):
     n_e, d_model, d_ff = w_in.shape
-    slots = n_e * SLOTS
+    slots = n_e * CAP
     bf, f32 = jnp.bfloat16, jnp.float32
     vmem, hbm = pl.BlockSpec(memory_space=pltpu.VMEM), pl.BlockSpec(memory_space=pl.ANY)
     buf, dma = pltpu.VMEM, pltpu.SemaphoreType.DMA
     return pl.pallas_call(
         expert_kernel,
         out_shape=[buf((128, d_model), bf), buf((8, 128), f32), buf((128, d_model), f32), buf((128, d_model), f32),
-                   buf((slots, d_model), bf), buf((slots, d_ff), bf), buf((slots, d_model), bf), buf((slots, d_ff), bf)],
+                   buf((slots, d_model), bf), buf((slots, PAIR * d_ff), bf), buf((slots, d_model), bf), buf((slots, PAIR * d_ff), bf)],
         in_specs=[hbm] * 6,
         out_specs=[vmem] * 8,
         scratch_shapes=[
@@ -323,7 +331,7 @@
             buf((4, 128, d_model), bf), buf((4, 128, d_model), bf), buf((4, 8, 128), jnp.int32), buf((4, 8, 128), f32),
             buf((8, 4, n_e, 128), f32), buf((4, n_e, 128), f32), buf((4, n_e, 128), f32),
             buf((slots, 512), bf), buf((512, slots), bf), buf((slots, 1), f32),
-            buf((slots, d_model), bf), buf((slots, d_ff), f32), buf((3, slots, d_model), bf), buf((2, 128, PAIR * d_ff), bf),
+            buf((slots, d_model), bf), buf((slots, d_ff), f32), buf((3, slots, d_model), bf),
             buf((n_e, 128), f32), buf((4, 8, 128), f32), buf((3, 8, 128), f32),
             buf((AHEAD, PAIR, d_model, d_ff), bf), buf((AHEAD, PAIR, d_ff, d_model), bf),
             buf((4, 4, 128, 256), f32), buf((4, 2, 128, 256), f32), buf((4, 128, 256), f32), buf((4, 128, 256), f32),
@@ -336,7 +344,7 @@
 
 
 def weight_kernel(b, h, g, da, y, dg, dw_in, dw_out, y_out, dg_out, ring_in, ring_out, sem_in, sem_out, sem):
-    n_steps = dw_in.shape[0] // PAIR
+    n_steps, d_ff = dw_in.shape[0] // PAIR, dw_in.shape[2]
     passed = [pltpu.make_async_copy(y, y_out, sem.at[0]), pltpu.make_async_copy(dg, dg_out, sem.at[1])]
     for copy in passed:
         copy.start()
@@ -354,10 +362,11 @@
             for copy in copies(i - RING):
                 copy.wait()
 
+        at = pair_rows(i)
         for p in range(PAIR):
-            at = slot_rows(i * PAIR + p)
-            ring_in[slot, p] = dot(b[at, :], da[at, :], ((0,), (0,))).astype(jnp.bfloat16)
-            ring_out[slot, p] = dot(h[at, :], g[at, :], ((0,), (0,))).astype(jnp.bfloat16)
+            own = slice(d_ff * p, d_ff * (p + 1))
+            ring_in[slot, p] = dot(b[at, :], da[at, own], ((0,), (0,))).astype(jnp.bfloat16)
+            ring_out[slot, p] = dot(h[at, own], g[at, :], ((0,), (0,))).astype(jnp.bfloat16)
         for copy in copies(i):
             copy.start()
         return 0
@@ -371,7 +380,7 @@
 
 
 def weight_grads(b, h, g, da, y, dg, n_e):
-    d_model, d_ff = b.shape[1], h.shape[1]
+    d_model, d_ff = b.shape[1], h.shape[1] // PAIR
     bf, shape, dma = jnp.bfloat16, jax.ShapeDtypeStruct, pltpu.SemaphoreType.DMA
     return pl.pallas_call(
         weight_kernel,
@@ -381,7 +390,7 @@
         scratch_shapes=[pltpu.VMEM((RING, PAIR, d_model, d_ff), bf), pltpu.VMEM((RING, PAIR, d_ff, d_model), bf),
                         dma((RING, PAIR)), dma((RING, PAIR)), dma((2,))],
         compiler_params=pltpu.CompilerParams(vmem_limit_bytes=40 * 1024 * 1024),
-        cost_estimate=pl.CostEstimate(flops=4 * n_e * SLOTS * d_model * d_ff, bytes_accessed=4 * n_e * d_model * d_ff, transcendentals=0),
+        cost_estimate=pl.CostEstimate(flops=4 * n_e * CAP * d_model * d_ff, bytes_accessed=4 * n_e * d_model * d_ff, transcendentals=0),
     )(b, h, g, da, y, dg)
 
 

time: 84.1 us -> 82.4 us (0.980)
  Pallas kernels: 82.4 us -> 80.8 us
    pallas_call x1, Pallas kernels: 64.3 us -> 62.7 us  [experts(): pl.pallas_call(expert_kernel, out_shape=[buf((128, d_model), bf), buf((8,...]
where the time goes in v6:
time: 82.4 us; the launch traced here: 82.3 us
  Pallas kernels  80.8 us (98%)
    pallas_call x1, Pallas kernels, experts(): pl.pallas_call(expert_kernel, out_shape=[buf((128, d_model), bf), buf((8,...  62.7 us
    pallas_call x1, Pallas kernels, weight_grads(): pl.pallas_call(weight_kernel, out_shape=[shape((n_e, d_model, d_ff), bf),...  18 us
  transfers between devices with their start and end apart: 1, of which 0 were waited for; matrix products, arithmetic and copies ran while one was open for 0% of the time, Pallas kernels for 22%

profile of v6, /device:TPU:0, one launch (start us, length us, event | category | flops | bytes accessed | tf_op | source)
XLA Modules:
  0.0 82.3 jit_solution(18398510948879732261)
XLA Ops:
  0.6 0.0 copy-start
  0.6 62.7 %shard_map.101 = (bf16[128,1024]{1,0:T(8,128)(2,1)S(1)}, f32[8,128]{1,0:T(8,128)S(1)}, f32[128,1024]{1,0:T(8,128)S(1)}, f32[128,1024]{1,0:T(8,128)S(1)}, bf16[12...) custom-call(bf16[128,1024]{1,0:T(8,128)(2,1)} %x_hbm.1, ...), custom_call_target="tpu_custom_call" | custom-call | flops 4026531840 | bytes 100663296 | tf_op jit(solution)/shard_map/pallas_call | solution.py:323
  63.4 0.0 collective-permute-start
  63.4 18.0 %shard_map.102 = (bf16[32,1024,384]{2,1,0:T(8,128)(2,1)}, bf16[32,384,1024]{2,1,0:T(8,128)(2,1)}, bf16[128,1024]{1,0:T(8,128)(2,1)}, f32[8,128]{1,0:T(8,128)}) custom-call(bf16[1280,1024]{1,0:T(8,128)(2,1)S(1)} %get-tuple-element.17.b, bf16[1280,768]{1,0:T(8,128)(2,1)S(1)} %get-tuple-element.18.h, bf16[1280,1024]{1,0:T(8,128)(2,1)S(1)} %get-tuple-element.19.g, ...), custom_call_target="tpu_custom_call" | custom-call | flops 2013265920 | bytes 50331648 | tf_op jit(solution)/shard_map/pallas_call | solution.py:385
  81.4 0.0 collective-permute-done
  81.5 0.0 copy-done
  81.5 0.8 add_convert_fusion
Async XLA Ops:
  0.6 80.8 %copy-start = (bf16[128,1024]{1,0:T(8,128)(2,1)S(1)}, bf16[128,1024]{1,0:T(8,128)(2,1)}, u32[]{:S(2)}) copy-start(bf16[128,1024]{1,0:T(8,128)(2,1)} %dy_hbm.1) | copy-start | bytes 786436
  63.4 18.1 %collective-permute-start = (f32[128,1024]{1,0:T(8,128)S(1)}, f32[128,1024]{1,0:T(8,128)S(1)}, u32[]{:S(2)}, u32[]{:S(2)}) collective-permute-start(f32[128,1024]{1,0:T(8,128)S(1)} %get-tuple-element.25), channel_id=1, source_target_pairs={{0,2},{1,3},{2,0},{3,1},{4,6},{5,7},{6,4},{7,5}} | collective-permute-start | bytes 1572872 | tf_op jit(solution)/shard_map/ppermute | solution.py:405

commit v7 on v6

--- a/solution.py
+++ b/solution.py
@@ -11,7 +11,7 @@
 CAP = 40
 PAIR = 2
 RING = 4
-AHEAD = 4
+AHEAD = 8
 PICK = 640
 C0 = 0.7978845608028654
 C1 = 0.044715
@@ -55,10 +55,12 @@
     bf, f32 = jnp.bfloat16, jnp.float32
     d_ff = w_in.shape[2]
 
-    def fetch_in(q, slot):
+    def fetch_in(q):
+        slot = lax.rem(q, AHEAD)
         return pltpu.make_async_copy(w_in.at[pl.ds(PAIR * q, PAIR)], wi.at[slot], wi_sem.at[slot])
 
-    def fetch_out(q, slot):
+    def fetch_out(q):
+        slot = lax.rem(q, AHEAD)
         return pltpu.make_async_copy(w_out.at[pl.ds(PAIR * q, PAIR)], wo.at[slot], wo_sem.at[slot])
 
     def remote(src, dst, s, r, peer):
@@ -73,8 +75,8 @@
     for copy in args:
         copy.start()
     for q in range(AHEAD):
-        fetch_in(q, q).start()
-        fetch_out(q, q).start()
+        fetch_in(q).start()
+        fetch_out(q).start()
     for copy in args:
         copy.wait()
     pl.semaphore_wait(barrier, 3)
@@ -136,8 +138,8 @@
 
     def fwd_step(i, _):
         slot = lax.rem(i, AHEAD)
-        fetch_in(i, slot).wait()
-        fetch_out(i, slot).wait()
+        fetch_in(i).wait()
+        fetch_out(i).wait()
         at = pair_rows(i)
         rows = b_s[at, :]
         a = jnp.concatenate([dot(rows, wi[slot, 0])[:CAP], dot(rows, wi[slot, 1])[CAP:]], axis=0)
@@ -163,13 +165,8 @@
 
         @pl.when(i < n_pairs - AHEAD)
         def _():
-            fetch_in(i + AHEAD, slot).start()
-            fetch_out(i + AHEAD, slot).start()
-
-        @pl.when(i >= n_pairs - AHEAD)
-        def _():
-            fetch_in(2 * n_pairs - 1 - AHEAD - i, slot).start()
-            fetch_out(2 * n_pairs - 1 - AHEAD - i, slot).start()
+            fetch_in(i + AHEAD).start()
+            fetch_out(i + AHEAD).start()
 
         for n, when in ((2, 1), (3, 4)):
             @pl.when(i == when)
@@ -229,37 +226,37 @@
     last = n_pairs - 1
 
     def back_h(i):
-        slot, at = lax.rem(i, AHEAD), pair_rows(last - i)
+        slot, at = lax.rem(last - i, AHEAD), pair_rows(last - i)
         g = g_s[at, :]
         dh = jnp.where(mine, dot(wo[slot, 0], g, ((1,), (1,))), dot(wo[slot, 1], g, ((1,), (1,))))
         da = dh.astype(bf).T.astype(f32) * slope[at, :]
         da_s[at, :] = jnp.concatenate([jnp.where(first, da, 0.0), jnp.where(first, 0.0, da)], axis=1).astype(bf)
 
     def back_x(i):
-        slot, at = lax.rem(i, AHEAD), pair_rows(last - i)
+        slot, at = lax.rem(last - i, AHEAD), pair_rows(last - i)
         wide = jnp.concatenate([wi[slot, 0], wi[slot, 1]], axis=1)
         sp[0, at, :] = dot(wide, da_s[at, :], ((1,), (1,))).astype(bf).T
 
-    def wait_in(i):
-        fetch_in(last - i, lax.rem(i, AHEAD)).wait()
-
-    def wait_out(i):
-        fetch_out(last - i, lax.rem(i, AHEAD)).wait()
-
-    wait_out(0)
-    wait_out(1)
     back_h(0)
     back_h(1)
     for copy in dg_back:
         copy.start()
     for i in range(2):
-        fetch_out(last - AHEAD - i, i).start()
+        fetch_out(last - AHEAD - i).start()
 
     def bwd_step(j, _):
         i = 2 * j
-        for k in range(2):
-            wait_in(i - 2 + k)
-            wait_out(i + k)
+
+        @pl.when(i - 2 >= n_pairs - AHEAD)
+        def _():
+            for k in range(2):
+                fetch_in(last + 2 - i - k).wait()
+
+        @pl.when(i >= n_pairs - AHEAD)
+        def _():
+            for k in range(2):
+                fetch_out(last - i - k).wait()
+
         back_x(i - 2)
         back_x(i - 1)
         back_h(i)
@@ -268,20 +265,20 @@
         @pl.when(i < n_pairs - AHEAD)
         def _():
             for k in range(2):
-                fetch_out(last - AHEAD - i - k, lax.rem(i + k, AHEAD)).start()
+                fetch_out(last - AHEAD - i - k).start()
 
         @pl.when(i < n_pairs - AHEAD + 2)
         def _():
             for k in range(2):
-                fetch_in(last + 2 - AHEAD - i - k, lax.rem(i - 2 + k, AHEAD)).start()
+                fetch_in(last + 2 - AHEAD - i - k).start()
         return 0
 
     lax.fori_loop(1, n_pairs // 2, bwd_step, 0)
     y_cross.wait()
     for copy in dg_back:
         copy.wait()
-    for i in range(last - 1, last + 1):
-        wait_in(i)
+    for i in range(2):
+        fetch_in(i).wait()
     dg_out[...] = dgp[me] + (dgr[0] + (dgr[1] + dgr[2]))
     for n in range(4):
         lanes = slice(256 * n, 256 * (n + 1))

time: 82.4 us -> 80.3 us (0.975)
  Pallas kernels: 80.8 us -> 78.3 us
    pallas_call x1, Pallas kernels: 62.7 us -> 60.3 us  [experts(): pl.pallas_call(expert_kernel, out_shape=[buf((128, d_model), bf), buf((8,...]
where the time goes in v7:
time: 80.3 us; the launch traced here: 80.2 us
  Pallas kernels  78.3 us (98%)
  other arithmetic  0.81 us (1%)
    pallas_call x1, Pallas kernels, experts(): pl.pallas_call(expert_kernel, out_shape=[buf((128, d_model), bf), buf((8,...  60.3 us
    pallas_call x1, Pallas kernels, weight_grads(): pl.pallas_call(weight_kernel, out_shape=[shape((n_e, d_model, d_ff), bf),...  18 us
  transfers between devices with their start and end apart: 1, of which 0 were waited for; matrix products, arithmetic and copies ran while one was open for 0% of the time, Pallas kernels for 22%

profile of v7, /device:TPU:0, one launch (start us, length us, event | category | flops | bytes accessed | tf_op | source)
XLA Modules:
  0.0 80.2 jit_solution(7318691441693991058)
XLA Ops:
  0.6 0.0 copy-start
  0.6 60.3 %shard_map.101 = (bf16[128,1024]{1,0:T(8,128)(2,1)S(1)}, f32[8,128]{1,0:T(8,128)S(1)}, f32[128,1024]{1,0:T(8,128)S(1)}, f32[128,1024]{1,0:T(8,128)S(1)}, bf16[12...) custom-call(bf16[128,1024]{1,0:T(8,128)(2,1)} %x_hbm.1, ...), custom_call_target="tpu_custom_call" | custom-call | flops 4026531840 | bytes 100663296 | tf_op jit(solution)/shard_map/pallas_call | solution.py:320
  61.0 0.4 collective-permute-start
  61.4 18.0 %shard_map.102 = (bf16[32,1024,384]{2,1,0:T(8,128)(2,1)}, bf16[32,384,1024]{2,1,0:T(8,128)(2,1)}, bf16[128,1024]{1,0:T(8,128)(2,1)}, f32[8,128]{1,0:T(8,128)}) custom-call(bf16[1280,1024]{1,0:T(8,128)(2,1)S(1)} %get-tuple-element.17.b, bf16[1280,768]{1,0:T(8,128)(2,1)S(1)} %get-tuple-element.18.h, bf16[1280,1024]{1,0:T(8,128)(2,1)S(1)} %get-tuple-element.19.g, ...), custom_call_target="tpu_custom_call" | custom-call | flops 2013265920 | bytes 50331648 | tf_op jit(solution)/shard_map/pallas_call | solution.py:382
  79.4 0.0 collective-permute-done
  79.4 0.0 copy-done
  79.4 0.8 %add_convert_fusion = bf16[128,1024]{1,0:T(8,128)(2,1)} fusion(f32[128,1024]{1,0:T(8,128)S(1)} %get-tuple-element.24, f32[128,1024]{1,0:T(8,128)S(1)} %collective-permute-done, bf16[128,1024]{1,0:T(8,128)(2,1)S(1)} %copy-done), kind=kLoop, calls=%fused_computation | loop fusion | flops 524288 | bytes 1572864 | tf_op jit(solution)/shard_map/convert_element_type | solution.py:404
Async XLA Ops:
  0.6 78.8 %copy-start = (bf16[128,1024]{1,0:T(8,128)(2,1)S(1)}, bf16[128,1024]{1,0:T(8,128)(2,1)}, u32[]{:S(2)}) copy-start(bf16[128,1024]{1,0:T(8,128)(2,1)} %dy_hbm.1) | copy-start | bytes 786436
  61.0 18.4 %collective-permute-start = (f32[128,1024]{1,0:T(8,128)S(1)}, f32[128,1024]{1,0:T(8,128)S(1)}, u32[]{:S(2)}, u32[]{:S(2)}) collective-permute-start(f32[128,1024]{1,0:T(8,128)S(1)} %get-tuple-element.25), channel_id=1, source_target_pairs={{0,2},{1,3},{2,0},{3,1},{4,6},{5,7},{6,4},{7,5}} | collective-permute-start | bytes 1572872 | tf_op jit(solution)/shard_map/ppermute | solution.py:402

commit v8 on v7

--- a/solution.py
+++ b/solution.py
@@ -49,7 +49,7 @@
                   yd_s, yd_r, yx_s, yx_r, dd_s, dd_r, dg_s, dg_r):
     me = lax.axis_index("expert")
     sib, cross = me + 1 - 2 * lax.rem(me, 2), lax.rem(me + 2, 4)
-    diag = lax.rem(sib + 2, 4)
+    diag, chip = lax.rem(sib + 2, 4), me // 2
     n_pairs = w_in.shape[0] // PAIR
     slots = 32 * CAP
     bf, f32 = jnp.bfloat16, jnp.float32
@@ -74,9 +74,6 @@
             for k, (src, dst) in enumerate(((idx_hbm, idx), (gate_hbm, gate), (x_hbm, x), (dy_hbm, dy)))]
     for copy in args:
         copy.start()
-    for q in range(AHEAD):
-        fetch_in(q).start()
-        fetch_out(q).start()
     for copy in args:
         copy.wait()
     pl.semaphore_wait(barrier, 3)
@@ -94,6 +91,9 @@
         near.append(remote(src, dst.at[me], sib_s.at[a], sib_r.at[a], sib))
     for copy in small + over[:2] + near[:1] + over[2:] + near[1:]:
         copy.start()
+    for q in range(AHEAD):
+        fetch_in(q).start()
+        fetch_out(q).start()
     xa[me] = x[...]
     dya[me] = dy[...]
     ida[me] = idx[...]
@@ -122,17 +122,29 @@
 
     lax.fori_loop(0, n_pairs, one, 0)
     forward(0)
+    near[0].wait_recv()
+
+    def half(devices):
+        return pl.ds(pl.multiple_of(devices * 256, 256), 256)
+
+    def pick_near(c, _):
+        at = pl.ds(pl.multiple_of(c * PICK, PICK), PICK)
+        rows = jnp.concatenate([xa[2 * chip], xa[2 * chip + 1]], axis=0)
+        b_s[at, :] = dot(pm[at, half(chip)], rows).astype(bf)
+        return 0
+
+    lax.fori_loop(0, slots // PICK, pick_near, 0)
     forward(1)
-    near[0].wait_recv()
     far[0].wait_recv()
     far[1].wait_recv()
 
-    def pick_x(c, _):
+    def pick_far(c, _):
         at = pl.ds(pl.multiple_of(c * PICK, PICK), PICK)
-        b_s[at, :] = dot(pm[at, :], xa[...].reshape(512, xa.shape[2])).astype(bf)
-        return 0
-
-    lax.fori_loop(0, slots // PICK, pick_x, 0)
+        rows = jnp.concatenate([xa[2 - 2 * chip], xa[3 - 2 * chip]], axis=0)
+        b_s[at, :] += dot(pm[at, half(1 - chip)], rows).astype(bf)
+        return 0
+
+    lax.fori_loop(0, slots // PICK, pick_far, 0)
 
     first = lax.broadcasted_iota(jnp.int32, (PAIR * CAP, d_ff), 0) < CAP
 

time: 80.3 us -> 73.9 us (0.920)
  Pallas kernels: 78.3 us -> 71.3 us
    pallas_call x1, Pallas kernels: 60.3 us -> 53.3 us  [experts(): pl.pallas_call(expert_kernel, out_shape=[buf((128, d_model), bf), buf((8,...]
  transfers between devices with their start and end apart: 1 -> 1, of which waited for: 0 -> 0; matrix products, arithmetic and copies ran while one was open for 0% -> 0% of each run, Pallas kernels for 22% -> 24%
where the time goes in v8:
time: 73.9 us; the launch traced here: 73.8 us
  Pallas kernels  71.3 us (96%)
  starting transfers between devices  0.95 us (1%)
  other arithmetic  0.81 us (1%)
    pallas_call x1, Pallas kernels, experts(): pl.pallas_call(expert_kernel, out_shape=[buf((128, d_model), bf), buf((8,...  53.3 us
    pallas_call x1, Pallas kernels, weight_grads(): pl.pallas_call(weight_kernel, out_shape=[shape((n_e, d_model, d_ff), bf),...  18 us
  transfers between devices with their start and end apart: 1, of which 0 were waited for; matrix products, arithmetic and copies ran while one was open for 0% of the time, Pallas kernels for 24%

profile of v8, /device:TPU:0, one launch (start us, length us, event | category | flops | bytes accessed | tf_op | source)
XLA Modules:
  0.0 73.8 jit_solution(15342568349762105491)
XLA Ops:
  0.6 0.0 copy-start
  0.6 53.3 %shard_map.101 = (bf16[128,1024]{1,0:T(8,128)(2,1)S(1)}, f32[8,128]{1,0:T(8,128)S(1)}, f32[128,1024]{1,0:T(8,128)S(1)}, f32[128,1024]{1,0:T(8,128)S(1)}, bf16[12...) custom-call(bf16[128,1024]{1,0:T(8,128)(2,1)} %x_hbm.1, ...), custom_call_target="tpu_custom_call" | custom-call | flops 4026531840 | bytes 100663296 | tf_op jit(solution)/shard_map/pallas_call | solution.py:332
  54.0 0.9 %collective-permute-start = (f32[128,1024]{1,0:T(8,128)S(1)}, f32[128,1024]{1,0:T(8,128)S(1)}, u32[]{:S(2)}, u32[]{:S(2)}) collective-permute-start(f32[128,1024]{1,0:T(8,128)S(1)} %get-tuple-element.25), channel_id=1, source_target_pairs={{0,2},{1,3},{2,0},{3,1},{4,6},{5,7},{6,4},{7,5}} | collective-permute-start | bytes 1572872 | tf_op jit(solution)/shard_map/ppermute | solution.py:414
  54.9 18.0 %shard_map.102 = (bf16[32,1024,384]{2,1,0:T(8,128)(2,1)}, bf16[32,384,1024]{2,1,0:T(8,128)(2,1)}, bf16[128,1024]{1,0:T(8,128)(2,1)}, f32[8,128]{1,0:T(8,128)}) custom-call(bf16[1280,1024]{1,0:T(8,128)(2,1)S(1)} %get-tuple-element.17.b, bf16[1280,768]{1,0:T(8,128)(2,1)S(1)} %get-tuple-element.18.h, bf16[1280,1024]{1,0:T(8,128)(2,1)S(1)} %get-tuple-element.19.g, ...), custom_call_target="tpu_custom_call" | custom-call | flops 2013265920 | bytes 50331648 | tf_op jit(solution)/shard_map/pallas_call | solution.py:394
  72.9 0.0 collective-permute-done
  72.9 0.0 copy-done
  72.9 0.8 %add_convert_fusion = bf16[128,1024]{1,0:T(8,128)(2,1)} fusion(f32[128,1024]{1,0:T(8,128)S(1)} %get-tuple-element.24, f32[128,1024]{1,0:T(8,128)S(1)} %collective-permute-done, bf16[128,1024]{1,0:T(8,128)(2,1)S(1)} %copy-done), kind=kLoop, calls=%fused_computation | loop fusion | flops 524288 | bytes 1572864 | tf_op jit(solution)/shard_map/convert_element_type | solution.py:416
Async XLA Ops:
  0.6 72.3 %copy-start = (bf16[128,1024]{1,0:T(8,128)(2,1)S(1)}, bf16[128,1024]{1,0:T(8,128)(2,1)}, u32[]{:S(2)}) copy-start(bf16[128,1024]{1,0:T(8,128)(2,1)} %dy_hbm.1) | copy-start | bytes 786436
  54.0 19.0 %collective-permute-start = (f32[128,1024]{1,0:T(8,128)S(1)}, f32[128,1024]{1,0:T(8,128)S(1)}, u32[]{:S(2)}, u32[]{:S(2)}) collective-permute-start(f32[128,1024]{1,0:T(8,128)S(1)} %get-tuple-element.25), channel_id=1, source_target_pairs={{0,2},{1,3},{2,0},{3,1},{4,6},{5,7},{6,4},{7,5}} | collective-permute-start | bytes 1572872 | tf_op jit(solution)/shard_map/ppermute | solution.py:414

commit v9 on v8

--- a/solution.py
+++ b/solution.py
@@ -12,7 +12,7 @@
 PAIR = 2
 RING = 4
 AHEAD = 8
-PICK = 640
+PICK, PICK_DY = 640, 640
 C0 = 0.7978845608028654
 C1 = 0.044715
 
@@ -44,7 +44,7 @@
 
 def expert_kernel(x_hbm, dy_hbm, idx_hbm, gate_hbm, w_in, w_out, y_out, dg_out, dx_own, dx_far, b_s, h_s, g_s, da_s,
                   x, dy, idx, gate, xa, dya, ida, ga, rj, r0s, r1s, pm, pt, gs, o_s, slope, sp, dg_tab, dgp, dgr,
-                  wi, wo, yp, yr, yfar, ygot, dxp, dxr,
+                  wi, wo, yp, yr, yfar, ygot, dxs, dxm, dxr,
                   arg_sem, wi_sem, wo_sem, small_s, small_r, sib_s, sib_r, cross_s, cross_r, fwd_s, fwd_r,
                   yd_s, yd_r, yx_s, yx_r, dd_s, dd_r, dg_s, dg_r):
     me = lax.axis_index("expert")
@@ -148,20 +148,19 @@
 
     first = lax.broadcasted_iota(jnp.int32, (PAIR * CAP, d_ff), 0) < CAP
 
-    def fwd_step(i, _):
-        slot = lax.rem(i, AHEAD)
-        fetch_in(i).wait()
-        fetch_out(i).wait()
-        at = pair_rows(i)
+    def fwd_h(i):
+        slot, at = lax.rem(i, AHEAD), pair_rows(i)
         rows = b_s[at, :]
         a = jnp.concatenate([dot(rows, wi[slot, 0])[:CAP], dot(rows, wi[slot, 1])[CAP:]], axis=0)
         th = jnp.tanh(C0 * (a + C1 * (a * a * a)))
         cdf = 0.5 * (1.0 + th)
         slope[at, :] = cdf + 0.5 * a * (1.0 - th * th) * (C0 * (1.0 + 3.0 * C1 * (a * a)))
         h = a * cdf
-        h = jnp.concatenate([jnp.where(first, h, 0.0), jnp.where(first, 0.0, h)], axis=1).astype(bf)
-        h_s[at, :] = h
-        o = dot(h, jnp.concatenate([wo[slot, 0], wo[slot, 1]], axis=0)).astype(bf)
+        h_s[at, :] = jnp.concatenate([jnp.where(first, h, 0.0), jnp.where(first, 0.0, h)], axis=1).astype(bf)
+
+    def fwd_o(i):
+        slot, at = lax.rem(i, AHEAD), pair_rows(i)
+        o = dot(h_s[at, :], jnp.concatenate([wo[slot, 0], wo[slot, 1]], axis=0)).astype(bf)
         o_s[at, :] = o
         s = o.astype(f32) * gs[at, :]
         s1 = s.astype(bf)
@@ -171,22 +170,48 @@
         sp[0, at, :] = s1
         sp[1, at, :] = s2
         sp[2, at, :] = s.astype(bf)
-        turned = i * (slots // 128) // n_pairs
-        tile = pl.ds(pl.multiple_of(turned * 128, 128), 128)
-        pt[:, tile] = pm[tile, :].astype(f32).T.astype(bf)
+
+    for i in range(2):
+        fetch_in(i).wait()
+    fwd_h(0)
+    fwd_h(1)
+    for i in range(2):
+        fetch_in(AHEAD + i).start()
+
+    def fwd_step(j, _):
+        i = 2 * j
+        for k in range(2):
+            fetch_in(i + k).wait()
+            fetch_out(i - 2 + k).wait()
+        fwd_o(i - 2)
+        fwd_o(i - 1)
+        fwd_h(i)
+        fwd_h(i + 1)
+        for k in range(2):
+            tile = pl.ds(pl.multiple_of(lax.rem(i - 2 + k, slots // 128) * 128, 128), 128)
+            pt[:, tile] = pm[tile, :].astype(f32).T.astype(bf)
 
         @pl.when(i < n_pairs - AHEAD)
         def _():
-            fetch_in(i + AHEAD).start()
-            fetch_out(i + AHEAD).start()
-
-        for n, when in ((2, 1), (3, 4)):
-            @pl.when(i == when)
+            for k in range(2):
+                fetch_in(i + AHEAD + k).start()
+
+        @pl.when(i < n_pairs - AHEAD + 2)
+        def _():
+            for k in range(2):
+                fetch_out(i - 2 + AHEAD + k).start()
+
+        for n, when in ((2, 2), (3, 4)):
+            @pl.when(j == when)
             def _(n=n):
                 forward(n)
         return 0
 
-    lax.fori_loop(0, n_pairs, fwd_step, 0)
+    lax.fori_loop(1, n_pairs // 2, fwd_step, 0)
+    for i in range(n_pairs - 2, n_pairs):
+        fetch_out(i).wait()
+    fwd_o(n_pairs - 2)
+    fwd_o(n_pairs - 1)
 
     def to_sib(part, got, s, r, n, k):
         return remote(part.at[n, sib if k == 0 else diag], got.at[n, k], s.at[n, k], r.at[n, k], sib)
@@ -211,16 +236,16 @@
         to_sib(yp, yr, yd_s, yd_r, 3, k).start()
 
     def pick_dy(c, _):
-        at = pl.ds(pl.multiple_of(c * PICK, PICK), PICK)
+        at = pl.ds(pl.multiple_of(c * PICK_DY, PICK_DY), PICK_DY)
         rows = dot(pm[at, :], dya[...].reshape(512, dya.shape[2]))
         g_s[at, :] = (rows * gs[at, :]).astype(bf)
         prod = rows * o_s[at, :].astype(f32)
         part = sum((prod[:, 128 * k:128 * (k + 1)] for k in range(1, 8)), prod[:, :128])
-        for k in range(PICK // CAP):
-            dg_tab[pl.ds(c * (PICK // CAP) + k, 1), :CAP] = jnp.sum(part[CAP * k:CAP * (k + 1)].T, axis=0, keepdims=True)
-        return 0
-
-    lax.fori_loop(0, slots // PICK, pick_dy, 0)
+        for k in range(PICK_DY // CAP):
+            dg_tab[pl.ds(c * (PICK_DY // CAP) + k, 1), :CAP] = jnp.sum(part[CAP * k:CAP * (k + 1)].T, axis=0, keepdims=True)
+        return 0
+
+    lax.fori_loop(0, slots // PICK_DY, pick_dy, 0)
     for n in range(4):
         for k in range(2):
             to_sib(yp, yr, yd_s, yd_r, n, k).wait()
@@ -298,27 +323,43 @@
     back_x(last - 1)
     back_x(last)
 
-    def dx_part(n, _):
+    def dx_send(n, k):
+        return remote(dxs.at[n, k], dxr.at[n, k], dd_s.at[n, k], dd_r.at[n, k], sib)
+
+    def dx_rows(n, into, d0, d1):
         lanes = pl.ds(pl.multiple_of(n * 256, 256), 256)
-        out = dot(pt[...], sp[0, :, lanes])
-        for d in range(4):
-            dxp[n, d] = out[128 * d:128 * (d + 1)]
+        chosen = jnp.concatenate([pt[pl.ds(pl.multiple_of(d * 128, 128), 128), :] for d in (d0, d1)], axis=0)
+        out = dot(chosen, sp[0, :, lanes])
+        into[n, 0] = out[:128]
+        into[n, 1] = out[128:]
+
+    def dx_theirs(n, _):
+        dx_rows(n, dxs, sib, diag)
 
         @pl.when(n > 0)
         def _():
             for k in range(2):
-                to_sib(dxp, dxr, dd_s, dd_r, n - 1, k).start()
-        return 0
-
-    lax.fori_loop(0, 4, dx_part, 0)
-    for k in range(2):
-        to_sib(dxp, dxr, dd_s, dd_r, 3, k).start()
+                dx_send(n - 1, k).start()
+        return 0
+
+    def dx_ours(n, _):
+        dx_rows(n, dxm, me, cross)
+
+        @pl.when(n == 0)
+        def _():
+            for k in range(2):
+                dx_send(3, k).start()
+        return 0
+
+    lax.fori_loop(0, 4, dx_theirs, 0)
+    lax.fori_loop(0, 4, dx_ours, 0)
+    for n in range(4):
+        for k in range(2):
+            dx_send(n, k).wait()
     for n in range(4):
         lanes = slice(256 * n, 256 * (n + 1))
-        for k in range(2):
-            to_sib(dxp, dxr, dd_s, dd_r, n, k).wait()
-        dx_own[:, lanes] = dxp[n, me] + dxr[n, 0]
-        dx_far[:, lanes] = dxp[n, cross] + dxr[n, 1]
+        dx_own[:, lanes] = dxm[n, 0] + dxr[n, 0]
+        dx_far[:, lanes] = dxm[n, 1] + dxr[n, 1]
     for copy in small + over + near + far:
         copy.wait_send()
 
@@ -344,7 +385,7 @@
             buf((n_e, 128), f32), buf((4, 8, 128), f32), buf((3, 8, 128), f32),
             buf((AHEAD, PAIR, d_model, d_ff), bf), buf((AHEAD, PAIR, d_ff, d_model), bf),
             buf((4, 4, 128, 256), f32), buf((4, 2, 128, 256), f32), buf((4, 128, 256), f32), buf((4, 128, 256), f32),
-            buf((4, 4, 128, 256), f32), buf((4, 2, 128, 256), f32),
+            buf((4, 2, 128, 256), f32), buf((4, 2, 128, 256), f32), buf((4, 2, 128, 256), f32),
             dma((4,)), dma((AHEAD,)), dma((AHEAD,)), dma((6,)), dma((6,)), dma((2,)), dma((2,)), dma((4,)), dma((4,)),
             dma((4,)), dma((4,)), dma((4, 2)), dma((4, 2)), dma(()), dma(()), dma((4, 2)), dma((4, 2)), dma((3,)), dma((3,))],
         compiler_params=pltpu.CompilerParams(collective_id=0, has_side_effects=True, vmem_limit_bytes=53 * 1024 * 1024),
@@ -358,32 +399,38 @@
     for copy in passed:
         copy.start()
 
-    def copies(i):
+    def copy_in(i, p):
         slot = lax.rem(i, RING)
-        return [pltpu.make_async_copy(ring.at[slot, p], out.at[i * PAIR + p], sems.at[slot, p])
-                for p in range(PAIR) for ring, out, sems in ((ring_in, dw_in, sem_in), (ring_out, dw_out, sem_out))]
-
-    def step(i, _):
+        return pltpu.make_async_copy(ring_in.at[slot, p], dw_in.at[i * PAIR + p], sem_in.at[slot, p])
+
+    def copy_out(i, p):
         slot = lax.rem(i, RING)
-
-        @pl.when(i >= RING)
-        def _():
-            for copy in copies(i - RING):
-                copy.wait()
-
-        at = pair_rows(i)
+        return pltpu.make_async_copy(ring_out.at[slot, p], dw_out.at[i * PAIR + p], sem_out.at[slot, p])
+
+    def step(j, _):
+        @pl.when(2 * j >= RING)
+        def _():
+            for k in range(2):
+                for p in range(PAIR):
+                    copy_in(2 * j + k - RING, p).wait()
+                    copy_out(2 * j + k - RING, p).wait()
+
+        for k in range(2):
+            i = 2 * j + k
+            slot, at = lax.rem(i, RING), pair_rows(i)
+            for p in range(PAIR):
+                own = slice(d_ff * p, d_ff * (p + 1))
+                ring_in[slot, p] = dot(b[at, :], da[at, own], ((0,), (0,))).astype(jnp.bfloat16)
+                copy_in(i, p).start()
+                ring_out[slot, p] = dot(h[at, own], g[at, :], ((0,), (0,))).astype(jnp.bfloat16)
+                copy_out(i, p).start()
+        return 0
+
+    lax.fori_loop(0, n_steps // 2, step, 0)
+    for i in range(n_steps - RING, n_steps):
         for p in range(PAIR):
-            own = slice(d_ff * p, d_ff * (p + 1))
-            ring_in[slot, p] = dot(b[at, :], da[at, own], ((0,), (0,))).astype(jnp.bfloat16)
-            ring_out[slot, p] = dot(h[at, own], g[at, :], ((0,), (0,))).astype(jnp.bfloat16)
-        for copy in copies(i):
-            copy.start()
-        return 0
-
-    lax.fori_loop(0, n_steps, step, 0)
-    for i in range(n_steps - RING, n_steps):
-        for copy in copies(i):
-            copy.wait()
+            copy_in(i, p).wait()
+            copy_out(i, p).wait()
     for copy in passed:
         copy.wait()
 

time: 73.9 us -> 69.9 us (0.946)
  Pallas kernels: 71.3 us -> 67.3 us
    pallas_call x1, Pallas kernels: 53.3 us -> 50.9 us  [experts(): pl.pallas_call(expert_kernel, out_shape=[buf((128, d_model), bf), buf((8,...]
    pallas_call x1, Pallas kernels: 18 us -> 16.5 us  [weight_grads(): pl.pallas_call(weight_kernel, out_shape=[shape((n_e, d_model, d_ff), bf),...]
where the time goes in v9:
time: 69.9 us; the launch traced here: 69.8 us
  Pallas kernels  67.3 us (96%)
  starting transfers between devices  0.95 us (1%)
  other arithmetic  0.81 us (1%)
    pallas_call x1, Pallas kernels, experts(): pl.pallas_call(expert_kernel, out_shape=[buf((128, d_model), bf), buf((8,...  50.9 us
    pallas_call x1, Pallas kernels, weight_grads(): pl.pallas_call(weight_kernel, out_shape=[shape((n_e, d_model, d_ff), bf),...  16.5 us
  transfers between devices with their start and end apart: 1, of which 0 were waited for; matrix products, arithmetic and copies ran while one was open for 0% of the time, Pallas kernels for 24%

profile of v9, /device:TPU:0, one launch (start us, length us, event | category | flops | bytes accessed | tf_op | source)
XLA Modules:
  0.0 69.8 jit_solution(12730402945837284442)
XLA Ops:
  0.6 0.0 copy-start
  0.6 50.9 %shard_map.101 = (bf16[128,1024]{1,0:T(8,128)(2,1)S(1)}, f32[8,128]{1,0:T(8,128)S(1)}, f32[128,1024]{1,0:T(8,128)S(1)}, f32[128,1024]{1,0:T(8,128)S(1)}, bf16[12...) custom-call(bf16[128,1024]{1,0:T(8,128)(2,1)} %x_hbm.1, ...), custom_call_target="tpu_custom_call" | custom-call | flops 4026531840 | bytes 100663296 | tf_op jit(solution)/shard_map/pallas_call | solution.py:373
  51.5 0.9 %collective-permute-start = (f32[128,1024]{1,0:T(8,128)S(1)}, f32[128,1024]{1,0:T(8,128)S(1)}, u32[]{:S(2)}, u32[]{:S(2)}) collective-permute-start(f32[128,1024]{1,0:T(8,128)S(1)} %get-tuple-element.25), channel_id=1, source_target_pairs={{0,2},{1,3},{2,0},{3,1},{4,6},{5,7},{6,4},{7,5}} | collective-permute-start | bytes 1572872 | tf_op jit(solution)/shard_map/ppermute | solution.py:461
  52.5 16.5 %shard_map.102 = (bf16[32,1024,384]{2,1,0:T(8,128)(2,1)}, bf16[32,384,1024]{2,1,0:T(8,128)(2,1)}, bf16[128,1024]{1,0:T(8,128)(2,1)}, f32[8,128]{1,0:T(8,128)}) custom-call(bf16[1280,1024]{1,0:T(8,128)(2,1)S(1)} %get-tuple-element.17.b, bf16[1280,768]{1,0:T(8,128)(2,1)S(1)} %get-tuple-element.18.h, bf16[1280,1024]{1,0:T(8,128)(2,1)S(1)} %get-tuple-element.19.g, ...), custom_call_target="tpu_custom_call" | custom-call | flops 2013265920 | bytes 50331648 | tf_op jit(solution)/shard_map/pallas_call | solution.py:441
  69.0 0.0 collective-permute-done
  69.0 0.0 copy-done
  69.0 0.8 %add_convert_fusion = bf16[128,1024]{1,0:T(8,128)(2,1)} fusion(f32[128,1024]{1,0:T(8,128)S(1)} %get-tuple-element.24, f32[128,1024]{1,0:T(8,128)S(1)} %collective-permute-done, bf16[128,1024]{1,0:T(8,128)(2,1)S(1)} %copy-done), kind=kLoop, calls=%fused_computation | loop fusion | flops 524288 | bytes 1572864 | tf_op jit(solution)/shard_map/convert_element_type | solution.py:463
Async XLA Ops:
  0.6 68.3 %copy-start = (bf16[128,1024]{1,0:T(8,128)(2,1)S(1)}, bf16[128,1024]{1,0:T(8,128)(2,1)}, u32[]{:S(2)}) copy-start(bf16[128,1024]{1,0:T(8,128)(2,1)} %dy_hbm.1) | copy-start | bytes 786436
  51.5 17.4 %collective-permute-start = (f32[128,1024]{1,0:T(8,128)S(1)}, f32[128,1024]{1,0:T(8,128)S(1)}, u32[]{:S(2)}, u32[]{:S(2)}) collective-permute-start(f32[128,1024]{1,0:T(8,128)S(1)} %get-tuple-element.25), channel_id=1, source_target_pairs={{0,2},{1,3},{2,0},{3,1},{4,6},{5,7},{6,4},{7,5}} | collective-permute-start | bytes 1572872 | tf_op jit(solution)/shard_map/ppermute | solution.py:461

commit v10 on v9

--- a/solution.py
+++ b/solution.py
@@ -117,7 +117,7 @@
                 for j in range(8):
                     total[p] = jnp.where(slot_id == rj[j, d, e, :], ga[d, j:j + 1, :], total[p])
             pm[pair_rows(q), 128 * d:128 * (d + 1)] = jnp.concatenate(inside[-PAIR:], axis=0).astype(bf)
-        gs[pair_rows(q), :] = jnp.sum(jnp.concatenate(total, axis=0), axis=1, keepdims=True)
+        gs[pair_rows(q), :] = jnp.broadcast_to(jnp.sum(jnp.concatenate(total, axis=0), axis=1, keepdims=True), (PAIR * CAP, 128))
         return 0
 
     lax.fori_loop(0, n_pairs, one, 0)
@@ -162,7 +162,7 @@
         slot, at = lax.rem(i, AHEAD), pair_rows(i)
         o = dot(h_s[at, :], jnp.concatenate([wo[slot, 0], wo[slot, 1]], axis=0)).astype(bf)
         o_s[at, :] = o
-        s = o.astype(f32) * gs[at, :]
+        s = o.astype(f32) * jnp.concatenate([gs[at, :]] * 8, axis=1)
         s1 = s.astype(bf)
         s = s - s1.astype(f32)
         s2 = s.astype(bf)
@@ -216,31 +216,37 @@
     def to_sib(part, got, s, r, n, k):
         return remote(part.at[n, sib if k == 0 else diag], got.at[n, k], s.at[n, k], r.at[n, k], sib)
 
-    def y_part(n, _):
-        lanes = pl.ds(pl.multiple_of(n * 256, 256), 256)
-        out = dot(pt[...], sp[0, :, lanes]) + dot(pt[...], sp[1, :, lanes]) + dot(pt[...], sp[2, :, lanes])
-        for d in range(4):
-            yp[n, d] = out[128 * d:128 * (d + 1)]
-
-        @pl.when(n > 0)
-        def _():
-            for k in range(2):
-                to_sib(yp, yr, yd_s, yd_r, n - 1, k).start()
-        return 0
-
-    lax.fori_loop(0, 4, y_part, 0)
+    def y_part(c, _):
+        for n in (2 * c, 2 * c + 1):
+            lanes = pl.ds(pl.multiple_of(n * 256, 256), 256)
+            out = dot(pt[...], sp[0, :, lanes]) + dot(pt[...], sp[1, :, lanes]) + dot(pt[...], sp[2, :, lanes])
+            for d in range(4):
+                yp[n, d] = out[128 * d:128 * (d + 1)]
+
+        @pl.when(c > 0)
+        def _():
+            for n in range(2):
+                for k in range(2):
+                    to_sib(yp, yr, yd_s, yd_r, n, k).start()
+        return 0
+
+    lax.fori_loop(0, 2, y_part, 0)
     near[1].wait_recv()
     far[2].wait_recv()
     far[3].wait_recv()
-    for k in range(2):
-        to_sib(yp, yr, yd_s, yd_r, 3, k).start()
+    for n in range(2, 4):
+        for k in range(2):
+            to_sib(yp, yr, yd_s, yd_r, n, k).start()
 
     def pick_dy(c, _):
         at = pl.ds(pl.multiple_of(c * PICK_DY, PICK_DY), PICK_DY)
-        rows = dot(pm[at, :], dya[...].reshape(512, dya.shape[2]))
-        g_s[at, :] = (rows * gs[at, :]).astype(bf)
-        prod = rows * o_s[at, :].astype(f32)
-        part = sum((prod[:, 128 * k:128 * (k + 1)] for k in range(1, 8)), prod[:, :128])
+        part = jnp.zeros((PICK_DY, 128), f32)
+        for n in range(4):
+            lanes = slice(256 * n, 256 * (n + 1))
+            rows = dot(pm[at, :], dya[:, :, lanes].reshape(512, 256))
+            g_s[at, lanes] = (rows * jnp.concatenate([gs[at, :]] * 2, axis=1)).astype(bf)
+            prod = rows * o_s[at, lanes].astype(f32)
+            part = part + (prod[:, :128] + prod[:, 128:])
         for k in range(PICK_DY // CAP):
             dg_tab[pl.ds(c * (PICK_DY // CAP) + k, 1), :CAP] = jnp.sum(part[CAP * k:CAP * (k + 1)].T, axis=0, keepdims=True)
         return 0
@@ -250,11 +256,6 @@
         for k in range(2):
             to_sib(yp, yr, yd_s, yd_r, n, k).wait()
         yfar[n] = yp[n, cross] + yr[n, 1]
-    for d in range(4):
-        for j in range(8):
-            at = rj[j, d].astype(jnp.int32)
-            got = jnp.take_along_axis(dg_tab[...], jnp.maximum(at, 0), axis=1)
-            dgp[d, j:j + 1, :] = jnp.sum(jnp.where(at >= 0, got, 0.0), axis=0, keepdims=True)
     y_cross = remote(yfar, ygot, yx_s, yx_r, cross)
     y_cross.start()
     dg_back = [remote(dgp.at[peer], dgr.at[k], dg_s.at[k], dg_r.at[k], peer) for k, peer in enumerate((cross, diag, sib))]
@@ -276,8 +277,6 @@
 
     back_h(0)
     back_h(1)
-    for copy in dg_back:
-        copy.start()
     for i in range(2):
         fetch_out(last - AHEAD - i).start()
 
@@ -298,6 +297,12 @@
         back_x(i - 1)
         back_h(i)
         back_h(i + 1)
+        for k in range(5):
+            row = lax.rem(5 * j - 5 + k, 32)
+            d, choice = row // 8, lax.rem(row, 8)
+            at = rj[choice, d].astype(jnp.int32)
+            got = jnp.take_along_axis(dg_tab[...], jnp.maximum(at, 0), axis=1)
+            dgp[d, pl.ds(choice, 1), :] = jnp.sum(jnp.where(at >= 0, got, 0.0), axis=0, keepdims=True)
 
         @pl.when(i < n_pairs - AHEAD)
         def _():
@@ -311,15 +316,11 @@
         return 0
 
     lax.fori_loop(1, n_pairs // 2, bwd_step, 0)
+    for copy in dg_back:
+        copy.start()
     y_cross.wait()
-    for copy in dg_back:
-        copy.wait()
     for i in range(2):
         fetch_in(i).wait()
-    dg_out[...] = dgp[me] + (dgr[0] + (dgr[1] + dgr[2]))
-    for n in range(4):
-        lanes = slice(256 * n, 256 * (n + 1))
-        y_out[:, lanes] = (x[:, lanes].astype(f32) + (yp[n, me] + yr[n, 0] + ygot[n])).astype(bf)
     back_x(last - 1)
     back_x(last)
 
@@ -327,32 +328,27 @@
         return remote(dxs.at[n, k], dxr.at[n, k], dd_s.at[n, k], dd_r.at[n, k], sib)
 
     def dx_rows(n, into, d0, d1):
-        lanes = pl.ds(pl.multiple_of(n * 256, 256), 256)
+        lanes = slice(256 * n, 256 * (n + 1))
         chosen = jnp.concatenate([pt[pl.ds(pl.multiple_of(d * 128, 128), 128), :] for d in (d0, d1)], axis=0)
         out = dot(chosen, sp[0, :, lanes])
         into[n, 0] = out[:128]
         into[n, 1] = out[128:]
 
-    def dx_theirs(n, _):
+    for n in range(4):
         dx_rows(n, dxs, sib, diag)
-
-        @pl.when(n > 0)
-        def _():
-            for k in range(2):
+        lanes = slice(256 * n, 256 * (n + 1))
+        y_out[:, lanes] = (x[:, lanes].astype(f32) + (yp[n, me] + yr[n, 0] + ygot[n])).astype(bf)
+        for k in range(2):
+            if n > 0:
                 dx_send(n - 1, k).start()
-        return 0
-
-    def dx_ours(n, _):
+    for n in range(4):
         dx_rows(n, dxm, me, cross)
-
-        @pl.when(n == 0)
-        def _():
-            for k in range(2):
+        for k in range(2):
+            if n == 0:
                 dx_send(3, k).start()
-        return 0
-
-    lax.fori_loop(0, 4, dx_theirs, 0)
-    lax.fori_loop(0, 4, dx_ours, 0)
+    for copy in dg_back:
+        copy.wait()
+    dg_out[...] = dgp[me] + (dgr[0] + (dgr[1] + dgr[2]))
     for n in range(4):
         for k in range(2):
             dx_send(n, k).wait()
@@ -380,7 +376,7 @@
             buf((128, d_model), bf), buf((128, d_model), bf), buf((8, 128), jnp.int32), buf((8, 128), f32),
             buf((4, 128, d_model), bf), buf((4, 128, d_model), bf), buf((4, 8, 128), jnp.int32), buf((4, 8, 128), f32),
             buf((8, 4, n_e, 128), f32), buf((4, n_e, 128), f32), buf((4, n_e, 128), f32),
-            buf((slots, 512), bf), buf((512, slots), bf), buf((slots, 1), f32),
+            buf((slots, 512), bf), buf((512, slots), bf), buf((slots, 128), f32),
             buf((slots, d_model), bf), buf((slots, d_ff), f32), buf((3, slots, d_model), bf),
             buf((n_e, 128), f32), buf((4, 8, 128), f32), buf((3, 8, 128), f32),
             buf((AHEAD, PAIR, d_model, d_ff), bf), buf((AHEAD, PAIR, d_ff, d_model), bf),

time: 69.9 us -> 69.5 us (level)
  no operation moved by 1% of the time
where the time goes in v10:
time: 69.5 us; the launch traced here: 69.3 us
  Pallas kernels  66.9 us (96%)
  starting transfers between devices  0.98 us (1%)
  other arithmetic  0.81 us (1%)
    pallas_call x1, Pallas kernels, experts(): pl.pallas_call(expert_kernel, out_shape=[buf((128, d_model), bf), buf((8,...  50.4 us
    pallas_call x1, Pallas kernels, weight_grads(): pl.pallas_call(weight_kernel, out_shape=[shape((n_e, d_model, d_ff), bf),...  16.5 us
  transfers between devices with their start and end apart: 1, of which 0 were waited for; matrix products, arithmetic and copies ran while one was open for 0% of the time, Pallas kernels for 24%

profile of v10, /device:TPU:0, one launch (start us, length us, event | category | flops | bytes accessed | tf_op | source)
XLA Modules:
  0.0 69.3 jit_solution(18413748208218663515)
XLA Ops:
  0.6 0.0 copy-start
  0.6 50.4 %shard_map.101 = (bf16[128,1024]{1,0:T(8,128)(2,1)S(1)}, f32[8,128]{1,0:T(8,128)S(1)}, f32[128,1024]{1,0:T(8,128)S(1)}, f32[128,1024]{1,0:T(8,128)S(1)}, bf16[12...) custom-call(bf16[128,1024]{1,0:T(8,128)(2,1)} %x_hbm.1, ...), custom_call_target="tpu_custom_call" | custom-call | flops 4026531840 | bytes 100663296 | tf_op jit(solution)/shard_map/pallas_call | solution.py:369
  51.1 1.0 %collective-permute-start = (f32[128,1024]{1,0:T(8,128)S(1)}, f32[128,1024]{1,0:T(8,128)S(1)}, u32[]{:S(2)}, u32[]{:S(2)}) collective-permute-start(f32[128,1024]{1,0:T(8,128)S(1)} %get-tuple-element.25), channel_id=1, source_target_pairs={{0,2},{1,3},{2,0},{3,1},{4,6},{5,7},{6,4},{7,5}} | collective-permute-start | bytes 1572872 | tf_op jit(solution)/shard_map/ppermute | solution.py:457
  52.0 16.5 %shard_map.102 = (bf16[32,1024,384]{2,1,0:T(8,128)(2,1)}, bf16[32,384,1024]{2,1,0:T(8,128)(2,1)}, bf16[128,1024]{1,0:T(8,128)(2,1)}, f32[8,128]{1,0:T(8,128)}) custom-call(bf16[1280,1024]{1,0:T(8,128)(2,1)S(1)} %get-tuple-element.17.b, bf16[1280,768]{1,0:T(8,128)(2,1)S(1)} %get-tuple-element.18.h, bf16[1280,1024]{1,0:T(8,128)(2,1)S(1)} %get-tuple-element.19.g, ...), custom_call_target="tpu_custom_call" | custom-call | flops 2013265920 | bytes 50331648 | tf_op jit(solution)/shard_map/pallas_call | solution.py:437
  68.5 0.0 collective-permute-done
  68.5 0.0 copy-done
  68.5 0.8 %add_convert_fusion = bf16[128,1024]{1,0:T(8,128)(2,1)} fusion(f32[128,1024]{1,0:T(8,128)S(1)} %get-tuple-element.24, f32[128,1024]{1,0:T(8,128)S(1)} %collective-permute-done, bf16[128,1024]{1,0:T(8,128)(2,1)S(1)} %copy-done), kind=kLoop, calls=%fused_computation | loop fusion | flops 524288 | bytes 1572864 | tf_op jit(solution)/shard_map/convert_element_type | solution.py:459
Async XLA Ops:
  0.6 67.9 %copy-start = (bf16[128,1024]{1,0:T(8,128)(2,1)S(1)}, bf16[128,1024]{1,0:T(8,128)(2,1)}, u32[]{:S(2)}) copy-start(bf16[128,1024]{1,0:T(8,128)(2,1)} %dy_hbm.1) | copy-start | bytes 786436
  51.1 17.5 %collective-permute-start = (f32[128,1024]{1,0:T(8,128)S(1)}, f32[128,1024]{1,0:T(8,128)S(1)}, u32[]{:S(2)}, u32[]{:S(2)}) collective-permute-start(f32[128,1024]{1,0:T(8,128)S(1)} %get-tuple-element.25), channel_id=1, source_target_pairs={{0,2},{1,3},{2,0},{3,1},{4,6},{5,7},{6,4},{7,5}} | collective-permute-start | bytes 1572872 | tf_op jit(solution)/shard_map/ppermute | solution.py:457

commit v11 on v10

--- a/solution.py
+++ b/solution.py
@@ -138,13 +138,10 @@
     far[0].wait_recv()
     far[1].wait_recv()
 
-    def pick_far(c, _):
-        at = pl.ds(pl.multiple_of(c * PICK, PICK), PICK)
+    for c in range(slots // PICK):
+        at = pl.ds(c * PICK, PICK)
         rows = jnp.concatenate([xa[2 - 2 * chip], xa[3 - 2 * chip]], axis=0)
         b_s[at, :] += dot(pm[at, half(1 - chip)], rows).astype(bf)
-        return 0
-
-    lax.fori_loop(0, slots // PICK, pick_far, 0)
 
     first = lax.broadcasted_iota(jnp.int32, (PAIR * CAP, d_ff), 0) < CAP
 
@@ -238,8 +235,8 @@
         for k in range(2):
             to_sib(yp, yr, yd_s, yd_r, n, k).start()
 
-    def pick_dy(c, _):
-        at = pl.ds(pl.multiple_of(c * PICK_DY, PICK_DY), PICK_DY)
+    for c in range(slots // PICK_DY):
+        at = pl.ds(c * PICK_DY, PICK_DY)
         part = jnp.zeros((PICK_DY, 128), f32)
         for n in range(4):
             lanes = slice(256 * n, 256 * (n + 1))
@@ -249,9 +246,7 @@
             part = part + (prod[:, :128] + prod[:, 128:])
         for k in range(PICK_DY // CAP):
             dg_tab[pl.ds(c * (PICK_DY // CAP) + k, 1), :CAP] = jnp.sum(part[CAP * k:CAP * (k + 1)].T, axis=0, keepdims=True)
-        return 0
-
-    lax.fori_loop(0, slots // PICK_DY, pick_dy, 0)
+
     for n in range(4):
         for k in range(2):
             to_sib(yp, yr, yd_s, yd_r, n, k).wait()
@@ -338,14 +333,11 @@
         dx_rows(n, dxs, sib, diag)
         lanes = slice(256 * n, 256 * (n + 1))
         y_out[:, lanes] = (x[:, lanes].astype(f32) + (yp[n, me] + yr[n, 0] + ygot[n])).astype(bf)
-        for k in range(2):
-            if n > 0:
-                dx_send(n - 1, k).start()
+    for n in range(4):
+        for k in range(2):
+            dx_send(n, k).start()
     for n in range(4):
         dx_rows(n, dxm, me, cross)
-        for k in range(2):
-            if n == 0:
-                dx_send(3, k).start()
     for copy in dg_back:
         copy.wait()
     dg_out[...] = dgp[me] + (dgr[0] + (dgr[1] + dgr[2]))

time: 69.5 us -> 69.4 us (level)
  no operation moved by 1% of the time
where the time goes in v11:
time: 69.4 us; the launch traced here: 69.3 us
  Pallas kernels  66.8 us (96%)
  starting transfers between devices  0.97 us (1%)
  other arithmetic  0.81 us (1%)
    pallas_call x1, Pallas kernels, experts(): pl.pallas_call(expert_kernel, out_shape=[buf((128, d_model), bf), buf((8,...  50.4 us
    pallas_call x1, Pallas kernels, weight_grads(): pl.pallas_call(weight_kernel, out_shape=[shape((n_e, d_model, d_ff), bf),...  16.5 us
  transfers between devices with their start and end apart: 1, of which 0 were waited for; matrix products, arithmetic and copies ran while one was open for 0% of the time, Pallas kernels for 24%

profile of v11, /device:TPU:0, one launch (start us, length us, event | category | flops | bytes accessed | tf_op | source)
XLA Modules:
  0.0 69.3 jit_solution(15160044191020418954)
XLA Ops:
  0.6 0.0 copy-start
  0.6 50.4 %shard_map.101 = (bf16[128,1024]{1,0:T(8,128)(2,1)S(1)}, f32[8,128]{1,0:T(8,128)S(1)}, f32[128,1024]{1,0:T(8,128)S(1)}, f32[128,1024]{1,0:T(8,128)S(1)}, bf16[12...) custom-call(bf16[128,1024]{1,0:T(8,128)(2,1)} %x_hbm.1, ...), custom_call_target="tpu_custom_call" | custom-call | flops 4026531840 | bytes 100663296 | tf_op jit(solution)/shard_map/pallas_call | solution.py:361
  51.0 1.0 %collective-permute-start = (f32[128,1024]{1,0:T(8,128)S(1)}, f32[128,1024]{1,0:T(8,128)S(1)}, u32[]{:S(2)}, u32[]{:S(2)}) collective-permute-start(f32[128,1024]{1,0:T(8,128)S(1)} %get-tuple-element.25), channel_id=1, source_target_pairs={{0,2},{1,3},{2,0},{3,1},{4,6},{5,7},{6,4},{7,5}} | collective-permute-start | bytes 1572872 | tf_op jit(solution)/shard_map/ppermute | solution.py:449
  52.0 16.5 %shard_map.102 = (bf16[32,1024,384]{2,1,0:T(8,128)(2,1)}, bf16[32,384,1024]{2,1,0:T(8,128)(2,1)}, bf16[128,1024]{1,0:T(8,128)(2,1)}, f32[8,128]{1,0:T(8,128)}) custom-call(bf16[1280,1024]{1,0:T(8,128)(2,1)S(1)} %get-tuple-element.17.b, bf16[1280,768]{1,0:T(8,128)(2,1)S(1)} %get-tuple-element.18.h, bf16[1280,1024]{1,0:T(8,128)(2,1)S(1)} %get-tuple-element.19.g, ...), custom_call_target="tpu_custom_call" | custom-call | flops 2013265920 | bytes 50331648 | tf_op jit(solution)/shard_map/pallas_call | solution.py:429
  68.5 0.0 collective-permute-done
  68.5 0.0 copy-done
  68.5 0.8 %add_convert_fusion = bf16[128,1024]{1,0:T(8,128)(2,1)} fusion(f32[128,1024]{1,0:T(8,128)S(1)} %get-tuple-element.24, f32[128,1024]{1,0:T(8,128)S(1)} %collective-permute-done, bf16[128,1024]{1,0:T(8,128)(2,1)S(1)} %copy-done), kind=kLoop, calls=%fused_computation | loop fusion | flops 524288 | bytes 1572864 | tf_op jit(solution)/shard_map/convert_element_type | solution.py:451
Async XLA Ops:
  0.6 67.8 %copy-start = (bf16[128,1024]{1,0:T(8,128)(2,1)S(1)}, bf16[128,1024]{1,0:T(8,128)(2,1)}, u32[]{:S(2)}) copy-start(bf16[128,1024]{1,0:T(8,128)(2,1)} %dy_hbm.1) | copy-start | bytes 786436
  51.0 17.5 %collective-permute-start = (f32[128,1024]{1,0:T(8,128)S(1)}, f32[128,1024]{1,0:T(8,128)S(1)}, u32[]{:S(2)}, u32[]{:S(2)}) collective-permute-start(f32[128,1024]{1,0:T(8,128)S(1)} %get-tuple-element.25), channel_id=1, source_target_pairs={{0,2},{1,3},{2,0},{3,1},{4,6},{5,7},{6,4},{7,5}} | collective-permute-start | bytes 1572872 | tf_op jit(solution)/shard_map/ppermute | solution.py:449

commit v12 on v11

--- a/solution.py
+++ b/solution.py
@@ -329,13 +329,15 @@
         into[n, 0] = out[:128]
         into[n, 1] = out[128:]
 
-    for n in range(4):
-        dx_rows(n, dxs, sib, diag)
-        lanes = slice(256 * n, 256 * (n + 1))
-        y_out[:, lanes] = (x[:, lanes].astype(f32) + (yp[n, me] + yr[n, 0] + ygot[n])).astype(bf)
-    for n in range(4):
-        for k in range(2):
-            dx_send(n, k).start()
+    for two in ((0, 1), (2, 3)):
+        for n in two:
+            dx_rows(n, dxs, sib, diag)
+        for n in two:
+            lanes = slice(256 * n, 256 * (n + 1))
+            y_out[:, lanes] = (x[:, lanes].astype(f32) + (yp[n, me] + yr[n, 0] + ygot[n])).astype(bf)
+        for n in two:
+            for k in range(2):
+                dx_send(n, k).start()
     for n in range(4):
         dx_rows(n, dxm, me, cross)
     for copy in dg_back:

time: 69.4 us -> 69 us (level)
  no operation moved by 1% of the time
where the time goes in v12:
time: 69 us; the launch traced here: 68.9 us
  Pallas kernels  66.4 us (96%)
  starting transfers between devices  0.97 us (1%)
  other arithmetic  0.81 us (1%)
    pallas_call x1, Pallas kernels, experts(): pl.pallas_call(expert_kernel, out_shape=[buf((128, d_model), bf), buf((8,...  49.9 us
    pallas_call x1, Pallas kernels, weight_grads(): pl.pallas_call(weight_kernel, out_shape=[shape((n_e, d_model, d_ff), bf),...  16.5 us
  transfers between devices with their start and end apart: 1, of which 0 were waited for; matrix products, arithmetic and copies ran while one was open for 0% of the time, Pallas kernels for 24%

profile of v12, /device:TPU:0, one launch (start us, length us, event | category | flops | bytes accessed | tf_op | source)
XLA Modules:
  0.0 68.9 jit_solution(8097950603080116595)
XLA Ops:
  0.6 0.0 copy-start
  0.6 49.9 %shard_map.101 = (bf16[128,1024]{1,0:T(8,128)(2,1)S(1)}, f32[8,128]{1,0:T(8,128)S(1)}, f32[128,1024]{1,0:T(8,128)S(1)}, f32[128,1024]{1,0:T(8,128)S(1)}, bf16[12...) custom-call(bf16[128,1024]{1,0:T(8,128)(2,1)} %x_hbm.1, ...), custom_call_target="tpu_custom_call" | custom-call | flops 4026531840 | bytes 100663296 | tf_op jit(solution)/shard_map/pallas_call | solution.py:363
  50.6 1.0 %collective-permute-start = (f32[128,1024]{1,0:T(8,128)S(1)}, f32[128,1024]{1,0:T(8,128)S(1)}, u32[]{:S(2)}, u32[]{:S(2)}) collective-permute-start(f32[128,1024]{1,0:T(8,128)S(1)} %get-tuple-element.25), channel_id=1, source_target_pairs={{0,2},{1,3},{2,0},{3,1},{4,6},{5,7},{6,4},{7,5}} | collective-permute-start | bytes 1572872 | tf_op jit(solution)/shard_map/ppermute | solution.py:451
  51.6 16.5 %shard_map.102 = (bf16[32,1024,384]{2,1,0:T(8,128)(2,1)}, bf16[32,384,1024]{2,1,0:T(8,128)(2,1)}, bf16[128,1024]{1,0:T(8,128)(2,1)}, f32[8,128]{1,0:T(8,128)}) custom-call(bf16[1280,1024]{1,0:T(8,128)(2,1)S(1)} %get-tuple-element.17.b, bf16[1280,768]{1,0:T(8,128)(2,1)S(1)} %get-tuple-element.18.h, bf16[1280,1024]{1,0:T(8,128)(2,1)S(1)} %get-tuple-element.19.g, ...), custom_call_target="tpu_custom_call" | custom-call | flops 2013265920 | bytes 50331648 | tf_op jit(solution)/shard_map/pallas_call | solution.py:431
  68.0 0.0 collective-permute-done
  68.1 0.0 copy-done
  68.1 0.8 %add_convert_fusion = bf16[128,1024]{1,0:T(8,128)(2,1)} fusion(f32[128,1024]{1,0:T(8,128)S(1)} %get-tuple-element.24, f32[128,1024]{1,0:T(8,128)S(1)} %collective-permute-done, bf16[128,1024]{1,0:T(8,128)(2,1)S(1)} %copy-done), kind=kLoop, calls=%fused_computation | loop fusion | flops 524288 | bytes 1572864 | tf_op jit(solution)/shard_map/convert_element_type | solution.py:453
Async XLA Ops:
  0.6 67.4 %copy-start = (bf16[128,1024]{1,0:T(8,128)(2,1)S(1)}, bf16[128,1024]{1,0:T(8,128)(2,1)}, u32[]{:S(2)}) copy-start(bf16[128,1024]{1,0:T(8,128)(2,1)} %dy_hbm.1) | copy-start | bytes 786436
  50.6 17.5 %collective-permute-start = (f32[128,1024]{1,0:T(8,128)S(1)}, f32[128,1024]{1,0:T(8,128)S(1)}, u32[]{:S(2)}, u32[]{:S(2)}) collective-permute-start(f32[128,1024]{1,0:T(8,128)S(1)} %get-tuple-element.25), channel_id=1, source_target_pairs={{0,2},{1,3},{2,0},{3,1},{4,6},{5,7},{6,4},{7,5}} | collective-permute-start | bytes 1572872 | tf_op jit(solution)/shard_map/ppermute | solution.py:451

commit v13 on v12

--- a/solution.py
+++ b/solution.py
@@ -11,7 +11,7 @@
 CAP = 40
 PAIR = 2
 RING = 4
-AHEAD = 8
+AHEAD, AHEAD_IN = 8, 8
 PICK, PICK_DY = 640, 640
 C0 = 0.7978845608028654
 C1 = 0.044715
@@ -44,7 +44,7 @@
 
 def expert_kernel(x_hbm, dy_hbm, idx_hbm, gate_hbm, w_in, w_out, y_out, dg_out, dx_own, dx_far, b_s, h_s, g_s, da_s,
                   x, dy, idx, gate, xa, dya, ida, ga, rj, r0s, r1s, pm, pt, gs, o_s, slope, sp, dg_tab, dgp, dgr,
-                  wi, wo, yp, yr, yfar, ygot, dxs, dxm, dxr,
+                  wi, wo, yp, yr, yfar, ygot, dxs, dxr,
                   arg_sem, wi_sem, wo_sem, small_s, small_r, sib_s, sib_r, cross_s, cross_r, fwd_s, fwd_r,
                   yd_s, yd_r, yx_s, yx_r, dd_s, dd_r, dg_s, dg_r):
     me = lax.axis_index("expert")
@@ -56,7 +56,7 @@
     d_ff = w_in.shape[2]
 
     def fetch_in(q):
-        slot = lax.rem(q, AHEAD)
+        slot = lax.rem(q, AHEAD_IN)
         return pltpu.make_async_copy(w_in.at[pl.ds(PAIR * q, PAIR)], wi.at[slot], wi_sem.at[slot])
 
     def fetch_out(q):
@@ -94,6 +94,8 @@
     for q in range(AHEAD):
         fetch_in(q).start()
         fetch_out(q).start()
+    for q in range(AHEAD, AHEAD_IN):
+        fetch_in(q).start()
     xa[me] = x[...]
     dya[me] = dy[...]
     ida[me] = idx[...]
@@ -146,7 +148,7 @@
     first = lax.broadcasted_iota(jnp.int32, (PAIR * CAP, d_ff), 0) < CAP
 
     def fwd_h(i):
-        slot, at = lax.rem(i, AHEAD), pair_rows(i)
+        slot, at = lax.rem(i, AHEAD_IN), pair_rows(i)
         rows = b_s[at, :]
         a = jnp.concatenate([dot(rows, wi[slot, 0])[:CAP], dot(rows, wi[slot, 1])[CAP:]], axis=0)
         th = jnp.tanh(C0 * (a + C1 * (a * a * a)))
@@ -173,7 +175,7 @@
     fwd_h(0)
     fwd_h(1)
     for i in range(2):
-        fetch_in(AHEAD + i).start()
+        fetch_in(AHEAD_IN + i).start()
 
     def fwd_step(j, _):
         i = 2 * j
@@ -188,10 +190,10 @@
             tile = pl.ds(pl.multiple_of(lax.rem(i - 2 + k, slots // 128) * 128, 128), 128)
             pt[:, tile] = pm[tile, :].astype(f32).T.astype(bf)
 
-        @pl.when(i < n_pairs - AHEAD)
-        def _():
-            for k in range(2):
-                fetch_in(i + AHEAD + k).start()
+        @pl.when(i < n_pairs - AHEAD_IN)
+        def _():
+            for k in range(2):
+                fetch_in(i + AHEAD_IN + k).start()
 
         @pl.when(i < n_pairs - AHEAD + 2)
         def _():
@@ -266,7 +268,7 @@
         da_s[at, :] = jnp.concatenate([jnp.where(first, da, 0.0), jnp.where(first, 0.0, da)], axis=1).astype(bf)
 
     def back_x(i):
-        slot, at = lax.rem(last - i, AHEAD), pair_rows(last - i)
+        slot, at = lax.rem(last - i, AHEAD_IN), pair_rows(last - i)
         wide = jnp.concatenate([wi[slot, 0], wi[slot, 1]], axis=1)
         sp[0, at, :] = dot(wide, da_s[at, :], ((1,), (1,))).astype(bf).T
 
@@ -278,12 +280,12 @@
     def bwd_step(j, _):
         i = 2 * j
 
-        @pl.when(i - 2 >= n_pairs - AHEAD)
+        @pl.when(i - 2 >= AHEAD_IN)
         def _():
             for k in range(2):
                 fetch_in(last + 2 - i - k).wait()
 
-        @pl.when(i >= n_pairs - AHEAD)
+        @pl.when(i >= AHEAD)
         def _():
             for k in range(2):
                 fetch_out(last - i - k).wait()
@@ -304,10 +306,10 @@
             for k in range(2):
                 fetch_out(last - AHEAD - i - k).start()
 
-        @pl.when(i < n_pairs - AHEAD + 2)
-        def _():
-            for k in range(2):
-                fetch_in(last + 2 - AHEAD - i - k).start()
+        @pl.when(i < n_pairs - AHEAD_IN + 2)
+        def _():
+            for k in range(2):
+                fetch_in(last + 2 - AHEAD_IN - i - k).start()
         return 0
 
     lax.fori_loop(1, n_pairs // 2, bwd_step, 0)
@@ -322,16 +324,16 @@
     def dx_send(n, k):
         return remote(dxs.at[n, k], dxr.at[n, k], dd_s.at[n, k], dd_r.at[n, k], sib)
 
-    def dx_rows(n, into, d0, d1):
+    def dx_rows(n, d0, d1):
         lanes = slice(256 * n, 256 * (n + 1))
         chosen = jnp.concatenate([pt[pl.ds(pl.multiple_of(d * 128, 128), 128), :] for d in (d0, d1)], axis=0)
-        out = dot(chosen, sp[0, :, lanes])
-        into[n, 0] = out[:128]
-        into[n, 1] = out[128:]
+        return dot(chosen, sp[0, :, lanes])
 
     for two in ((0, 1), (2, 3)):
         for n in two:
-            dx_rows(n, dxs, sib, diag)
+            out = dx_rows(n, sib, diag)
+            dxs[n, 0] = out[:128]
+            dxs[n, 1] = out[128:]
         for n in two:
             lanes = slice(256 * n, 256 * (n + 1))
             y_out[:, lanes] = (x[:, lanes].astype(f32) + (yp[n, me] + yr[n, 0] + ygot[n])).astype(bf)
@@ -339,7 +341,10 @@
             for k in range(2):
                 dx_send(n, k).start()
     for n in range(4):
-        dx_rows(n, dxm, me, cross)
+        out = dx_rows(n, me, cross)
+        lanes = slice(256 * n, 256 * (n + 1))
+        dx_own[:, lanes] = out[:128]
+        dx_far[:, lanes] = out[128:]
     for copy in dg_back:
         copy.wait()
     dg_out[...] = dgp[me] + (dgr[0] + (dgr[1] + dgr[2]))
@@ -348,8 +353,8 @@
             dx_send(n, k).wait()
     for n in range(4):
         lanes = slice(256 * n, 256 * (n + 1))
-        dx_own[:, lanes] = dxm[n, 0] + dxr[n, 0]
-        dx_far[:, lanes] = dxm[n, 1] + dxr[n, 1]
+        dx_own[:, lanes] += dxr[n, 0]
+        dx_far[:, lanes] += dxr[n, 1]
     for copy in small + over + near + far:
         copy.wait_send()
 
@@ -373,10 +378,10 @@
             buf((slots, 512), bf), buf((512, slots), bf), buf((slots, 128), f32),
             buf((slots, d_model), bf), buf((slots, d_ff), f32), buf((3, slots, d_model), bf),
             buf((n_e, 128), f32), buf((4, 8, 128), f32), buf((3, 8, 128), f32),
-            buf((AHEAD, PAIR, d_model, d_ff), bf), buf((AHEAD, PAIR, d_ff, d_model), bf),
+            buf((AHEAD_IN, PAIR, d_model, d_ff), bf), buf((AHEAD, PAIR, d_ff, d_model), bf),
             buf((4, 4, 128, 256), f32), buf((4, 2, 128, 256), f32), buf((4, 128, 256), f32), buf((4, 128, 256), f32),
-            buf((4, 2, 128, 256), f32), buf((4, 2, 128, 256), f32), buf((4, 2, 128, 256), f32),
-            dma((4,)), dma((AHEAD,)), dma((AHEAD,)), dma((6,)), dma((6,)), dma((2,)), dma((2,)), dma((4,)), dma((4,)),
+            buf((4, 2, 128, 256), f32), buf((4, 2, 128, 256), f32),
+            dma((4,)), dma((AHEAD_IN,)), dma((AHEAD,)), dma((6,)), dma((6,)), dma((2,)), dma((2,)), dma((4,)), dma((4,)),
             dma((4,)), dma((4,)), dma((4, 2)), dma((4, 2)), dma(()), dma(()), dma((4, 2)), dma((4, 2)), dma((3,)), dma((3,))],
         compiler_params=pltpu.CompilerParams(collective_id=0, has_side_effects=True, vmem_limit_bytes=53 * 1024 * 1024),
         cost_estimate=pl.CostEstimate(flops=8 * slots * d_model * d_ff, bytes_accessed=8 * n_e * d_model * d_ff, transcendentals=0),

time: 69 us -> 69 us (level)
  no operation moved by 1% of the time
where the time goes in v13:
time: 69 us; the launch traced here: 68.9 us
  Pallas kernels  66.5 us (96%)
  starting transfers between devices  0.98 us (1%)
  other arithmetic  0.81 us (1%)
    pallas_call x1, Pallas kernels, experts(): pl.pallas_call(expert_kernel, out_shape=[buf((128, d_model), bf), buf((8,...  50 us
    pallas_call x1, Pallas kernels, weight_grads(): pl.pallas_call(weight_kernel, out_shape=[shape((n_e, d_model, d_ff), bf),...  16.5 us
  transfers between devices with their start and end apart: 1, of which 0 were waited for; matrix products, arithmetic and copies ran while one was open for 0% of the time, Pallas kernels for 24%

profile of v13, /device:TPU:0, one launch (start us, length us, event | category | flops | bytes accessed | tf_op | source)
XLA Modules:
  0.0 68.9 jit_solution(5498261411033332261)
XLA Ops:
  0.6 0.0 copy-start
  0.6 50.0 %shard_map.101 = (bf16[128,1024]{1,0:T(8,128)(2,1)S(1)}, f32[8,128]{1,0:T(8,128)S(1)}, f32[128,1024]{1,0:T(8,128)S(1)}, f32[128,1024]{1,0:T(8,128)S(1)}, bf16[12...) custom-call(bf16[128,1024]{1,0:T(8,128)(2,1)} %x_hbm.1, ...), custom_call_target="tpu_custom_call" | custom-call | flops 4026531840 | bytes 100663296 | tf_op jit(solution)/shard_map/pallas_call | solution.py:368
  50.6 1.0 %collective-permute-start = (f32[128,1024]{1,0:T(8,128)S(1)}, f32[128,1024]{1,0:T(8,128)S(1)}, u32[]{:S(2)}, u32[]{:S(2)}) collective-permute-start(f32[128,1024]{1,0:T(8,128)S(1)} %get-tuple-element.25), channel_id=1, source_target_pairs={{0,2},{1,3},{2,0},{3,1},{4,6},{5,7},{6,4},{7,5}} | collective-permute-start | bytes 1572872 | tf_op jit(solution)/shard_map/ppermute | solution.py:456
  51.6 16.5 %shard_map.102 = (bf16[32,1024,384]{2,1,0:T(8,128)(2,1)}, bf16[32,384,1024]{2,1,0:T(8,128)(2,1)}, bf16[128,1024]{1,0:T(8,128)(2,1)}, f32[8,128]{1,0:T(8,128)}) custom-call(bf16[1280,1024]{1,0:T(8,128)(2,1)S(1)} %get-tuple-element.17.b, bf16[1280,768]{1,0:T(8,128)(2,1)S(1)} %get-tuple-element.18.h, bf16[1280,1024]{1,0:T(8,128)(2,1)S(1)} %get-tuple-element.19.g, ...), custom_call_target="tpu_custom_call" | custom-call | flops 2013265920 | bytes 50331648 | tf_op jit(solution)/shard_map/pallas_call | solution.py:436
  68.1 0.0 collective-permute-done
  68.1 0.0 copy-done
  68.1 0.8 %add_convert_fusion = bf16[128,1024]{1,0:T(8,128)(2,1)} fusion(f32[128,1024]{1,0:T(8,128)S(1)} %get-tuple-element.24, f32[128,1024]{1,0:T(8,128)S(1)} %collective-permute-done, bf16[128,1024]{1,0:T(8,128)(2,1)S(1)} %copy-done), kind=kLoop, calls=%fused_computation | loop fusion | flops 524288 | bytes 1572864 | tf_op jit(solution)/shard_map/convert_element_type | solution.py:458
Async XLA Ops:
  0.6 67.5 %copy-start = (bf16[128,1024]{1,0:T(8,128)(2,1)S(1)}, bf16[128,1024]{1,0:T(8,128)(2,1)}, u32[]{:S(2)}) copy-start(bf16[128,1024]{1,0:T(8,128)(2,1)} %dy_hbm.1) | copy-start | bytes 786436
  50.6 17.5 %collective-permute-start = (f32[128,1024]{1,0:T(8,128)S(1)}, f32[128,1024]{1,0:T(8,128)S(1)}, u32[]{:S(2)}, u32[]{:S(2)}) collective-permute-start(f32[128,1024]{1,0:T(8,128)S(1)} %get-tuple-element.25), channel_id=1, source_target_pairs={{0,2},{1,3},{2,0},{3,1},{4,6},{5,7},{6,4},{7,5}} | collective-permute-start | bytes 1572872 | tf_op jit(solution)/shard_map/ppermute | solution.py:456
